TPU v7x, 8 devices: a whole 2x2x1 slice. The times are simulated.
8 devices in a mesh: data: 1 (over z), col: 2 (over y), row: 4 (over x, core).
Axes of the slice: x: 2, y: 2, z: 1, core: 2. Of those that a mesh axis runs over, the one named last changes fastest.
Arguments:
- image: bfloat16 [256, 128, 4], P(('data', 'row'), 'col')
- w_enc1a: bfloat16 [3, 3, 4, 320], replicated
- b_enc1a: float32 [320], replicated
- w_enc1b: bfloat16 [3, 3, 320, 320], replicated
- b_enc1b: float32 [320], replicated
- w_enc2a: bfloat16 [3, 3, 320, 640], replicated
- b_enc2a: float32 [640], replicated
- w_enc2b: bfloat16 [3, 3, 640, 640], replicated
- b_enc2b: float32 [640], replicated
- w_mid_a: bfloat16 [3, 3, 640, 1280], replicated
- b_mid_a: float32 [1280], replicated
- w_mid_b: bfloat16 [3, 3, 1280, 1280], replicated
- b_mid_b: float32 [1280], replicated
- w_up2: bfloat16 [2, 2, 1280, 640], replicated
- w_dec2a: bfloat16 [3, 3, 1280, 640], replicated
- b_dec2a: float32 [640], replicated
- w_dec2b: bfloat16 [3, 3, 640, 640], replicated
- b_dec2b: float32 [640], replicated
- w_up1: bfloat16 [2, 2, 640, 320], replicated
- w_dec1a: bfloat16 [3, 3, 640, 320], replicated
- b_dec1a: float32 [320], replicated
- w_dec1b: bfloat16 [3, 3, 320, 320], replicated
- b_dec1b: float32 [320], replicated
- w_head: bfloat16 [320, 4], replicated
- b_head: float32 [4], replicated
Outputs:
- output: float32 [256, 128, 4], P(('data', 'row'), 'col')
All inputs are finite; a program needn't handle non-finite values.
Results may differ from a plain program's by a relative error of at most 0.0171095.
Values are sent between devices in bfloat16 or wider.
A program may use at most 1 GiB of HBM per device.

v0:
```python
import jax
import jax.numpy as jnp
from jax import lax
from jax.sharding import PartitionSpec as P

CONV_DIMS = ("NHWC", "HWIO", "NHWC")


def solution(mesh):
    row_count = mesh.shape["row"]
    col_count = mesh.shape["col"]
    grid_size = row_count * col_count
    grid_axes = ("col", "row")
    row_next = [(source, source + 1) for source in range(row_count - 1)]
    row_prev = [(source + 1, source) for source in range(row_count - 1)]
    col_next = [(source, source + 1) for source in range(col_count - 1)]
    col_prev = [(source + 1, source) for source in range(col_count - 1)]
    tile_spec = P(("data", "row"), "col", None)

    def with_halo(tile):
        from_above = lax.ppermute(tile[-1:], "row", row_next)
        from_below = lax.ppermute(tile[:1], "row", row_prev)
        tall_tile = jnp.concatenate([from_above, tile, from_below], axis=0)
        from_left = lax.ppermute(tall_tile[:, -1:], "col", col_next)
        from_right = lax.ppermute(tall_tile[:, :1], "col", col_prev)
        return jnp.concatenate([from_left, tall_tile, from_right], axis=1)

    def conv_relu(hidden, weight, bias, padding):
        conv_out = lax.conv_general_dilated(hidden[None], weight, (1, 1), padding, dimension_numbers=CONV_DIMS, preferred_element_type=jnp.float32)[0]
        return jax.nn.relu(conv_out + bias).astype(jnp.bfloat16)

    def double_tile(tile, w_first, b_first, w_second, b_second):
        first = conv_relu(with_halo(tile), w_first, b_first, "VALID")
        return conv_relu(with_halo(first), w_second, b_second, "VALID")

    def max_pool(tile):
        height, width, channels = tile.shape
        return tile.reshape(height // 2, 2, width // 2, 2, channels).max(axis=(1, 3))

    def up_conv(tile, weight):
        height = tile.shape[0]
        width = tile.shape[1]
        summed = jnp.einsum("ijc,abco->iajbo", tile, weight, preferred_element_type=jnp.float32)
        return summed.astype(jnp.bfloat16).reshape(2 * height, 2 * width, weight.shape[3])

    def gather_map(tile):
        height, width, channels = tile.shape
        gathered = lax.all_gather(tile, grid_axes, axis=0)
        gathered = gathered.reshape(col_count, row_count, height, width, channels).transpose(1, 2, 0, 3, 4)
        return gathered.reshape(row_count * height, col_count * width, channels)

    def scatter_map(full_map):
        height = full_map.shape[0] // row_count
        width = full_map.shape[1] // col_count
        channels = full_map.shape[2]
        blocks = full_map.reshape(row_count, height, col_count, width, channels).transpose(2, 0, 1, 3, 4)
        blocks = blocks.reshape(grid_size, height, width, channels)
        return lax.all_to_all(blocks, grid_axes, 0, 3, tiled=True)[0]

    def device_body(image_tile, *params):
        (w_enc1a, b_enc1a, w_enc1b, b_enc1b, w_enc2a, b_enc2a, w_enc2b, b_enc2b,
         w_mid_a, b_mid_a, w_mid_b, b_mid_b, w_up2, w_dec2a, b_dec2a, w_dec2b, b_dec2b,
         w_up1, w_dec1a, b_dec1a, w_dec1b, b_dec1b, w_head, b_head) = params
        shard_id = lax.axis_index("col") * row_count + lax.axis_index("row")
        mid_width = w_mid_a.shape[3] // grid_size
        mid_start = shard_id * mid_width
        skip_one = double_tile(image_tile, w_enc1a, b_enc1a, w_enc1b, b_enc1b)
        skip_two = double_tile(max_pool(skip_one), w_enc2a, b_enc2a, w_enc2b, b_enc2b)
        full_in = gather_map(max_pool(skip_two))
        mid_part = conv_relu(full_in, lax.dynamic_slice_in_dim(w_mid_a, mid_start, mid_width, axis=3), lax.dynamic_slice_in_dim(b_mid_a, mid_start, mid_width), "SAME")
        mid_full = lax.all_gather(mid_part, grid_axes, axis=2, tiled=True)
        mid_part = conv_relu(mid_full, lax.dynamic_slice_in_dim(w_mid_b, mid_start, mid_width, axis=3), lax.dynamic_slice_in_dim(b_mid_b, mid_start, mid_width), "SAME")
        mid_tile = scatter_map(mid_part)
        hidden = double_tile(jnp.concatenate([up_conv(mid_tile, w_up2), skip_two], axis=2), w_dec2a, b_dec2a, w_dec2b, b_dec2b)
        hidden = double_tile(jnp.concatenate([up_conv(hidden, w_up1), skip_one], axis=2), w_dec1a, b_dec1a, w_dec1b, b_dec1b)
        return jnp.einsum("hwc,co->hwo", hidden, w_head, preferred_element_type=jnp.float32) + b_head

    def program(image, *params):
        mapped = jax.shard_map(device_body, mesh=mesh, in_specs=(tile_spec,) + tuple([P()] * len(params)), out_specs=tile_spec, check_vma=False)
        return mapped(image, *params)

    return program
```

profile of v0, /device:TPU:6, one launch (start us, length us, event | category | flops | bytes accessed | tf_op | source)
XLA Modules:
  0.0 546.3 jit_solution(10932541449764763937)
XLA Ops:
  23.8 4.3 broadcast_select_fusion.3
  51.3 17.2 %broadcast_select_fusion.2 = f32[64,8,9,320]{3,1,2,0:T(8,128)S(1)} fusion(pred[8,9]{0,1:T(8,128)(4,1)S(1)} %copy-done.20, bf16[3,3,320,320]{3,2,1,0:T(8,128)(2,1)S(1)} %copy-done, bf16[66,1,7,2,320]{4,2,3,0,1:T(8,128)(2,1)S(1)} %slice.154, bf16[66,1,8,9,320]{4,2,3,0,1:T(8,128)(2,1)S(1)} %copy.166), kind=kOutput, calls=%fused_computation.76 | convolution fusion | flops 8506091520 | bytes 11374152 | tf_op jit(solution)/shard_map/conv_general_dilated | solution.py:29
  76.2 8.3 %squeeze.38 = f32[32,2,32,2,320]{4,1,0,3,2:T(2,128)} reshape(f32[64,1,64,320]{3,0,2,1:T(8,128)} %slice.155) | data formatting | bytes 10485760 | tf_op jit(solution)/shard_map/squeeze | solution.py:29
  84.5 9.0 %fusion.68 = bf16[32,32,320]{2,0,1:T(8,128)(2,1)S(1)} fusion(f32[32,2,32,2,320]{4,1,0,3,2:T(2,128)} %squeeze.38, f32[320]{0:T(512)S(1)} %copy-done.6), kind=kLoop, calls=%fused_computation.81 | loop fusion | flops 4915200 | bytes 5899520 | tf_op jit(solution)/shard_map/reduce_max | solution.py:38
  109.6 6.6 %convolution_select_fusion = f32[32,8,5,640]{3,1,2,0:T(8,128)S(1)} fusion(bf16[3,3,320,640]{3,2,1,0:T(8,128)(2,1)S(1)} %copy-done.16, pred[8,5]{0,1:T(8,128)(4,1)S(1)} %copy-done.22, bf16[34,1,7,2,320]{4,2,3,0,1:T(8,128)(2,1)S(1)} %slice.158, bf16[34,1,8,5,320]{4,2,3,0,1:T(8,128)(2,1)S(1)} %copy.169), kind=kOutput, calls=%fused_computation.127 | convolution fusion | flops 4723066880 | bytes 8138280 | tf_op jit(solution)/shard_map/conv_general_dilated | solution.py:29
  134.8 12.2 %fusion.115 = f32[32,8,5,640]{3,1,2,0:T(8,128)S(1)} fusion(bf16[3,3,640,640]{3,2,1,0:T(8,128)(2,1)S(1)} %bitcast.243, bf16[34,1,7,2,640]{4,2,3,0,1:T(8,128)(2,1)S(1)} %slice.162, bf16[34,1,8,5,640]{4,2,3,0,1:T(8,128)(2,1)S(1)} %copy.172, pred[8,5]{0,1:T(8,128)(4,1)S(1)} %copy-done.22), kind=kOutput, calls=%fused_computation.126 | convolution fusion | flops 9445314560 | bytes 12999720 | tf_op jit(solution)/shard_map/conv_general_dilated | solution.py:29
  149.4 4.4 squeeze.40
  159.7 23.5 %all-gather.6.cloned.1.call-done = bf16[128,16,640]{2,1,0:T(8,128)(2,1)} async-done(((bf16[16,16,640]{2,1,0:T(8,128)(2,1)}), bf16[128,16,640]{2,1,0:T(8,128)(2,1)}) %all-gather.6.cloned.1.call-update) | async-done | bytes 2621456 | tf_op jit(solution)/shard_map/all_gather | solution.py:48
  188.7 12.1 %broadcast_select_fusion.5 = f32[64,8,5,160]{3,1,2,0:T(8,128)S(1)} fusion(pred[8,5]{0,1:T(8,128)(4,1)S(1)} %copy-done.22, bf16[3,3,640,1280]{3,2,1,0:T(8,128)(2,1)} %param.34, s32[]{:T(128)S(6)} %select_n.2, bf16[64,1,7,2,640]{4,2,3,0,1:T(8,128)(2,1)S(1)} %slice.164, bf16[64,1,8,5,640]{4,2,3,0,1:T(8,128)(2,1)S(1)} %copy.178), kind=kOutput, calls=%fused_computation.141 | convolution fusion | flops 4683612160 | bytes 9011244 | tf_op jit(solution)/shard_map/conv_general_dilated | solution.py:29
  206.8 56.8 %all-gather.4.cloned.1.call-done = bf16[64,32,1280]{0,1,2:T(8,128)(2,1)} async-done(((bf16[64,32,160]{0,1,2:T(8,128)(2,1)}), bf16[64,32,1280]{0,1,2:T(8,128)(2,1)}) %all-gather.4.cloned.1.call-update) | async-done | bytes 5242896 | tf_op jit(solution)/shard_map/all_gather | solution.py:71
  263.6 12.7 %copy.182 = bf16[64,32,1280]{2,0,1:T(8,128)(2,1)} copy(bf16[64,32,1280]{0,1,2:T(8,128)(2,1)} %all-gather.4.cloned.1.call-done) | data formatting | bytes 10485760 | tf_op jit(solution)/shard_map/all_gather | solution.py:71
  283.9 19.2 %broadcast_select_fusion.4 = f32[64,8,5,160]{3,1,2,0:T(8,128)S(1)} fusion(pred[8,5]{0,1:T(8,128)(4,1)S(1)} %copy-done.22, bf16[3,3,1280,1280]{3,2,1,0:T(8,128)(2,1)} %param.36, s32[]{:T(128)S(6)} %select_n.2, bf16[64,1,7,2,1280]{4,2,3,0,1:T(8,128)(2,1)S(1)} %slice.166, bf16[64,1,8,5,1280]{4,2,3,0,1:T(8,128)(2,1)S(1)} %copy.184), kind=kOutput, calls=%fused_computation.140 | convolution fusion | flops 9366814720 | bytes 16384044 | tf_op jit(solution)/shard_map/conv_general_dilated | solution.py:29
  306.8 4.3 all-to-all-start
  312.6 11.4 %all-to-all-done = bf16[8,16,16,160]{3,2,1,0:T(8,128)(2,1)} async-done(((bf16[8,16,16,160]{3,2,1,0:T(8,128)(2,1)}), bf16[8,16,16,160]{3,2,1,0:T(8,128)(2,1)}, u32[]{:S(2)}, u32[]{:S(2)}) %all-to-all-start) | async-done | bytes 655392 | tf_op jit(solution)/shard_map/all_to_all | solution.py:58
  326.9 4.7 fusion.129
  351.9 4.6 collective-permute-done.18
  362.7 24.6 %fusion.109 = f32[32,8,5,640]{3,1,2,0:T(8,128)S(1)} fusion(bf16[3,3,1280,640]{3,2,1,0:T(8,128)(2,1)S(1)} %bitcast.241, bf16[34,1,7,2,1280]{4,2,3,0,1:T(8,128)(2,1)S(1)} %slice.168, bf16[34,1,8,5,1280]{4,2,3,0,1:T(8,128)(2,1)S(1)} %copy.193, pred[8,5]{0,1:T(8,128)(4,1)S(1)} %copy-done.22), kind=kOutput, calls=%fused_computation.122 | convolution fusion | flops 18889809920 | bytes 22722600 | tf_op jit(solution)/shard_map/conv_general_dilated | solution.py:29
  405.2 12.4 %fusion.112 = f32[32,8,5,640]{3,1,2,0:T(8,128)S(1)} fusion(bf16[3,3,640,640]{3,2,1,0:T(8,128)(2,1)S(1)} %bitcast.245, bf16[34,1,7,2,640]{4,2,3,0,1:T(8,128)(2,1)S(1)} %slice.172, bf16[34,1,8,5,640]{4,2,3,0,1:T(8,128)(2,1)S(1)} %copy.196, pred[8,5]{0,1:T(8,128)(4,1)S(1)} %copy-done.22), kind=kOutput, calls=%fused_computation.125 | convolution fusion | flops 9445314560 | bytes 12999720 | tf_op jit(solution)/shard_map/conv_general_dilated | solution.py:29
  422.7 4.9 copy.213
  427.6 7.5 %reshape.185 = bf16[64,64,320]{2,0,1:T(8,128)(2,1)} reshape(bf16[32,2,32,2,320]{4,1,0,3,2:T(2,128)(2,1)} %copy.213) | data formatting | bytes 5242880 | tf_op jit(solution)/shard_map/reshape | solution.py:44
  449.4 4.3 collective-permute-done.26
  453.7 7.3 %maximum_bitcast_fusion = bf16[66,1,66,640]{3,0,2,1:T(8,128)(2,1)S(1)} fusion(bf16[66,1,640]{2,0,1:T(8,128)(2,1)S(1)} %collective-permute-done.27, bf16[1,64,640]{2,0,1:T(2,128)(2,1)S(1)} %collective-permute-done.25, bf16[64,64,320]{2,0,1:T(8,128)(2,1)S(1)} %fusion.32, bf16[64,64,320]{2,0,1:T(8,128)(2,1)S(1)} %copy-done.3, ...), kind=kLoop, calls=%fused_computation.41 | loop fusion | flops 33454080 | bytes 11151360 | tf_op jit(solution)/shard_map/broadcast_in_dim | solution.py:29
  463.6 31.5 %broadcast_select_fusion.1 = f32[64,8,9,320]{3,1,2,0:T(8,128)S(1)} fusion(pred[8,9]{0,1:T(8,128)(4,1)S(1)} %copy-done.21, bf16[3,3,640,320]{2,3,1,0:T(8,128)(2,1)S(1)} %copy-done.17, bf16[66,1,7,2,640]{4,2,3,0,1:T(8,128)(2,1)S(1)} %slice.174, bf16[66,1,8,9,640]{4,2,3,0,1:T(8,128)(2,1)S(1)} %copy.202), kind=kOutput, calls=%fused_computation.75 | convolution fusion | flops 17010708480 | bytes 16849992 | tf_op jit(solution)/shard_map/conv_general_dilated | solution.py:29
  518.3 16.9 %broadcast_select_fusion = f32[64,8,9,320]{3,1,2,0:T(8,128)S(1)} fusion(pred[8,9]{0,1:T(8,128)(4,1)S(1)} %copy-done.21, bf16[3,3,320,320]{3,2,1,0:T(8,128)(2,1)S(1)} %copy-done.18, bf16[66,1,7,2,320]{4,2,3,0,1:T(8,128)(2,1)S(1)} %slice.178, bf16[66,1,8,9,320]{4,2,3,0,1:T(8,128)(2,1)S(1)} %copy.205), kind=kOutput, calls=%fused_computation.74 | convolution fusion | flops 8506091520 | bytes 11374152 | tf_op jit(solution)/shard_map/conv_general_dilated | solution.py:29
  (231 shorter events, 210.6 us)
Async XLA Ops:
  6.5 176.6 %all-gather.6.cloned.1.call-start = ((), (), s32[]{:S(2)}) async-start(), calls=%async_computation.2 | async-start | bytes 2949120 | tf_op jit(solution)/shard_map/all_gather | solution.py:48
  7.4 5.6 %collective-permute-start = (bf16[1,64,4]{1,2,0:T(4,128)(2,1)S(1)}, bf16[1,64,4]{1,2,0:T(4,128)(2,1)S(1)}, u32[]{:S(2)}, u32[]{:S(2)}) collective-permute-start(bf16[1,64,4]{1,2,0:T(4,128)(2,1)S(1)} %get-tuple-element.36), channel_id=1, source_target_pairs={{0,1},{1,2},{2,3},{4,5},{5,6},{6,7}} | collective-permute-start | bytes 1544 | tf_op jit(solution)/shard_map/ppermute | solution.py:21
  9.3 4.9 collective-permute-start.1
  16.8 6.2 %collective-permute-start.2 = (bf16[66,1,4]{1,2,0:T(4,128)(2,1)S(1)}, bf16[66,1,4]{1,2,0:T(4,128)(2,1)S(1)}, u32[]{:S(2)}, u32[]{:S(2)}) collective-permute-start(bf16[66,1,4]{1,2,0:T(4,128)(2,1)S(1)} %get-tuple-element.33), channel_id=1, source_target_pairs={{0,4},{1,5},{2,6},{3,7}} | collective-permute-start | bytes 1592 | tf_op jit(solution)/shard_map/ppermute | solution.py:24
  32.9 5.9 %collective-permute-start.4 = (bf16[1,64,320]{2,0,1:T(2,128)(2,1)S(1)}, bf16[1,64,320]{2,0,1:T(2,128)(2,1)S(1)}, u32[]{:S(2)}, u32[]{:S(2)}) collective-permute-start(bf16[1,64,320]{2,0,1:T(2,128)(2,1)S(1)} %get-tuple-element.15), channel_id=1, source_target_pairs={{0,1},{1,2},{2,3},{4,5},{5,6},{6,7}} | collective-permute-start | bytes 122888 | tf_op jit(solution)/shard_map/ppermute | solution.py:21
  40.7 6.0 %collective-permute-start.6 = (bf16[66,1,320]{2,0,1:T(8,128)(2,1)S(1)}, bf16[66,1,320]{2,0,1:T(8,128)(2,1)S(1)}, u32[]{:S(2)}, u32[]{:S(2)}) collective-permute-start(bf16[66,1,320]{2,0,1:T(8,128)(2,1)S(1)} %get-tuple-element.11), channel_id=1, source_target_pairs={{0,4},{1,5},{2,6},{3,7}} | collective-permute-start | bytes 126728 | tf_op jit(solution)/shard_map/ppermute | solution.py:24
  95.5 5.4 collective-permute-start.8
  102.6 6.0 %collective-permute-start.10 = (bf16[34,1,320]{2,0,1:T(8,128)(2,1)S(1)}, bf16[34,1,320]{2,0,1:T(8,128)(2,1)S(1)}, u32[]{:S(2)}, u32[]{:S(2)}) collective-permute-start(bf16[34,1,320]{2,0,1:T(8,128)(2,1)S(1)} %get-tuple-element.29), channel_id=1, source_target_pairs={{0,4},{1,5},{2,6},{3,7}} | collective-permute-start | bytes 65288 | tf_op jit(solution)/shard_map/ppermute | solution.py:24
  117.3 4.6 collective-permute-start.13
  119.5 5.8 %collective-permute-start.12 = (bf16[1,32,640]{2,0,1:T(2,128)(2,1)S(1)}, bf16[1,32,640]{2,0,1:T(2,128)(2,1)S(1)}, u32[]{:S(2)}, u32[]{:S(2)}) collective-permute-start(bf16[1,32,640]{2,0,1:T(2,128)(2,1)S(1)} %get-tuple-element.27), channel_id=1, source_target_pairs={{0,1},{1,2},{2,3},{4,5},{5,6},{6,7}} | collective-permute-start | bytes 122888 | tf_op jit(solution)/shard_map/ppermute | solution.py:21
  127.0 6.3 %collective-permute-start.14 = (bf16[34,1,640]{2,0,1:T(8,128)(2,1)S(1)}, bf16[34,1,640]{2,0,1:T(8,128)(2,1)S(1)}, u32[]{:S(2)}, u32[]{:S(2)}) collective-permute-start(bf16[34,1,640]{2,0,1:T(8,128)(2,1)S(1)} %get-tuple-element.23), channel_id=1, source_target_pairs={{0,4},{1,5},{2,6},{3,7}} | collective-permute-start | bytes 130568 | tf_op jit(solution)/shard_map/ppermute | solution.py:24
  158.9 104.7 %all-gather.4.cloned.1.call-start = ((), (), s32[]{:S(2)}) async-start(), calls=%async_computation.1 | async-start | bytes 11796480 | tf_op jit(solution)/shard_map/all_gather | solution.py:71
  306.8 17.1 %all-to-all-start = ((bf16[8,16,16,160]{3,2,1,0:T(8,128)(2,1)}), bf16[8,16,16,160]{3,2,1,0:T(8,128)(2,1)}, u32[]{:S(2)}, u32[]{:S(2)}) async-start(bf16[8,16,16,160]{3,2,1,0:T(8,128)(2,1)} %bitcast.237), calls=%async_computation | async-start | bytes 2097152 | tf_op jit(solution)/shard_map/all_to_all | solution.py:58
  337.4 5.0 collective-permute-start.17
  339.6 6.7 %collective-permute-start.16 = (bf16[1,32,1280]{2,0,1:T(2,128)(2,1)S(1)}, bf16[1,32,1280]{2,0,1:T(2,128)(2,1)S(1)}, u32[]{:S(2)}, u32[]{:S(2)}) collective-permute-start(bf16[1,32,1280]{2,0,1:T(2,128)(2,1)S(1)} %get-tuple-element.19), channel_id=1, source_target_pairs={{0,1},{1,2},{2,3},{4,5},{5,6},{6,7}} | collective-permute-start | bytes 245768 | tf_op jit(solution)/shard_map/ppermute | solution.py:21
  346.3 5.6 %collective-permute-start.19 = (bf16[34,1,1280]{2,0,1:T(8,128)(2,1)S(1)}, bf16[34,1,1280]{2,0,1:T(8,128)(2,1)S(1)}, u32[]{:S(2)}, u32[]{:S(2)}) collective-permute-start(bf16[34,1,1280]{2,0,1:T(8,128)(2,1)S(1)} %get-tuple-element.18), channel_id=1, source_target_pairs={{4,0},{5,1},{6,2},{7,3}} | collective-permute-start | bytes 261128 | tf_op jit(solution)/shard_map/ppermute | solution.py:25
  349.7 6.8 %collective-permute-start.18 = (bf16[34,1,1280]{2,0,1:T(8,128)(2,1)S(1)}, bf16[34,1,1280]{2,0,1:T(8,128)(2,1)S(1)}, u32[]{:S(2)}, u32[]{:S(2)}) collective-permute-start(bf16[34,1,1280]{2,0,1:T(8,128)(2,1)S(1)} %get-tuple-element.17), channel_id=1, source_target_pairs={{0,4},{1,5},{2,6},{3,7}} | collective-permute-start | bytes 261128 | tf_op jit(solution)/shard_map/ppermute | solution.py:24
  390.3 5.8 %collective-permute-start.20 = (bf16[1,32,640]{2,0,1:T(2,128)(2,1)S(1)}, bf16[1,32,640]{2,0,1:T(2,128)(2,1)S(1)}, u32[]{:S(2)}, u32[]{:S(2)}) collective-permute-start(bf16[1,32,640]{2,0,1:T(2,128)(2,1)S(1)} %get-tuple-element.25), channel_id=1, source_target_pairs={{0,1},{1,2},{2,3},{4,5},{5,6},{6,7}} | collective-permute-start | bytes 122888 | tf_op jit(solution)/shard_map/ppermute | solution.py:21
  397.6 6.0 %collective-permute-start.22 = (bf16[34,1,640]{2,0,1:T(8,128)(2,1)S(1)}, bf16[34,1,640]{2,0,1:T(8,128)(2,1)S(1)}, u32[]{:S(2)}, u32[]{:S(2)}) collective-permute-start(bf16[34,1,640]{2,0,1:T(8,128)(2,1)S(1)} %get-tuple-element.21), channel_id=1, source_target_pairs={{0,4},{1,5},{2,6},{3,7}} | collective-permute-start | bytes 130568 | tf_op jit(solution)/shard_map/ppermute | solution.py:24
  436.9 4.7 collective-permute-start.25
  438.8 6.6 %collective-permute-start.24 = (bf16[1,64,640]{2,0,1:T(2,128)(2,1)S(1)}, bf16[1,64,640]{2,0,1:T(2,128)(2,1)S(1)}, u32[]{:S(2)}, u32[]{:S(2)}) collective-permute-start(bf16[1,64,640]{2,0,1:T(2,128)(2,1)S(1)} %get-tuple-element.7), channel_id=1, source_target_pairs={{0,1},{1,2},{2,3},{4,5},{5,6},{6,7}} | collective-permute-start | bytes 245768 | tf_op jit(solution)/shard_map/ppermute | solution.py:21
  447.3 6.4 %collective-permute-start.26 = (bf16[66,1,640]{2,0,1:T(8,128)(2,1)S(1)}, bf16[66,1,640]{2,0,1:T(8,128)(2,1)S(1)}, u32[]{:S(2)}, u32[]{:S(2)}) collective-permute-start(bf16[66,1,640]{2,0,1:T(8,128)(2,1)S(1)} %get-tuple-element.5), channel_id=1, source_target_pairs={{0,4},{1,5},{2,6},{3,7}} | collective-permute-start | bytes 253448 | tf_op jit(solution)/shard_map/ppermute | solution.py:24
  499.6 5.9 %collective-permute-start.28 = (bf16[1,64,320]{2,0,1:T(2,128)(2,1)S(1)}, bf16[1,64,320]{2,0,1:T(2,128)(2,1)S(1)}, u32[]{:S(2)}, u32[]{:S(2)}) collective-permute-start(bf16[1,64,320]{2,0,1:T(2,128)(2,1)S(1)} %get-tuple-element.13), channel_id=1, source_target_pairs={{0,1},{1,2},{2,3},{4,5},{5,6},{6,7}} | collective-permute-start | bytes 122888 | tf_op jit(solution)/shard_map/ppermute | solution.py:21
  507.1 6.0 %collective-permute-start.30 = (bf16[66,1,320]{2,0,1:T(8,128)(2,1)S(1)}, bf16[66,1,320]{2,0,1:T(8,128)(2,1)S(1)}, u32[]{:S(2)}, u32[]{:S(2)}) collective-permute-start(bf16[66,1,320]{2,0,1:T(8,128)(2,1)S(1)} %get-tuple-element.9), channel_id=1, source_target_pairs={{0,4},{1,5},{2,6},{3,7}} | collective-permute-start | bytes 126728 | tf_op jit(solution)/shard_map/ppermute | solution.py:24
  (44 other events, 317.5 us)
Sparse Core Ops, SparseCore 0:
  159.0 24.1 all-gather.5
  206.2 57.3 all-gather.3
where the time goes:
time: 555 us; the launch traced here: 546 us
  matrix products  167 us (30%)
  waiting for transfers between devices  154 us (28%)
  local copies, waits for them, and re-layouts  100 us (18%)
  starting transfers between devices  68.2 us (12%)
  other arithmetic  41.9 us (8%)
  between operations  14.9 us (3%)
    conv_general_dilated x10, matrix products, conv_relu(): lax.conv_general_dilated(hidden[None], weight, (1, 1), padding, dimension...  157 us
    all_gather x1, waiting for transfers between devices, device_body(): mid_full = lax.all_gather(mid_part, grid_axes, axis=2, tiled=True)  56.8 us
    ppermute x8, waiting for transfers between devices, with_halo(): from_left = lax.ppermute(tall_tile[:, -1:], 'col', col_next)  33.9 us
    conv_general_dilated x34, local copies, waits for them, and re-layouts, conv_relu(): lax.conv_general_dilated(hidden[None], weight, (1, 1), padding, dimension...  27.8 us
    ppermute x8, waiting for transfers between devices, with_halo(): from_above = lax.ppermute(tile[-1:], 'row', row_next)  24.6 us
    all_gather x1, waiting for transfers between devices, gather_map(): gathered = lax.all_gather(tile, grid_axes, axis=0)  23.5 us
    broadcast_in_dim x8, other arithmetic, conv_relu(): hidden[None]  19.5 us
    ppermute x8, starting transfers between devices, with_halo(): from_above = lax.ppermute(tile[-1:], 'row', row_next)  18.5 us
  transfers between devices with their start and end apart: 35, of which 26 were waited for; matrix products, arithmetic and copies ran while one was open for 1% of the time, Pallas kernels for 0%

commit v1 on v0

v1 whole, which is shorter than its diff:
```python
import functools

import jax
import jax.numpy as jnp
from jax import lax
from jax.experimental import pallas as pl
from jax.experimental.pallas import tpu as pltpu
from jax.sharding import PartitionSpec as P

BF16 = jnp.bfloat16
F32 = jnp.float32
MESH = pl.DeviceIdType.MESH
VMEM_LIMIT = 66_900_000
RING_ROWS = 11520


def strip_index():
    col = lax.axis_index("col")
    row = lax.axis_index("row")
    return row + col * (7 - 2 * row)


def strip_device(position):
    col = position // 4
    rest = position % 4
    return (lax.axis_index("data"), col, rest + col * (3 - 2 * rest))


def dot(a, b):
    return jnp.dot(a, b, preferred_element_type=F32)


def shifted(value, width, step):
    if step == 1:
        return value
    rows = value.shape[0]
    column = lax.broadcasted_iota(jnp.int32, value.shape, 0) % width
    if step == 0:
        return jnp.where(column == 0, 0.0, pltpu.roll(value, 1, axis=0))
    return jnp.where(column == width - 1, 0.0, pltpu.roll(value, rows - 1, axis=0))


def put3(dst, row0, lane0, channels, value, width):
    rows, lanes = value.shape
    for step in range(3):
        dst[pl.ds(row0, rows), pl.ds(step * channels + lane0, lanes)] = shifted(value, width, step).astype(BF16)


def put3_320(dst, row0, main, rest, width):
    rows = main.shape[0]
    for step in range(3):
        dst[pl.ds(row0, rows), pl.ds(step * 256, 256)] = shifted(main, width, step).astype(BF16)
    first = shifted(rest, width, 0) + pltpu.roll(rest, 64, axis=1)
    dst[pl.ds(row0, rows), pl.ds(768, 128)] = first.astype(BF16)
    dst[pl.ds(row0, rows), pl.ds(896, 128)] = shifted(rest, width, 2).astype(BF16)


def low_lanes(value):
    return jnp.where(lax.broadcasted_iota(jnp.int32, value.shape, 1) < 64, value, 0.0)


def pack_weights(staged, tap_rows, offset, main_ref, main0, rest_ref, rest0):
    for dj in range(3):
        for start, size, row in ((0, 256, 256 * dj), (256, 64, 768 + 64 * dj)):
            parts = []
            for di in range(3):
                base = (3 * di + dj) * tap_rows + offset + start
                main_ref[pl.ds(main0 + 1024 * di + row, size), :] = staged[pl.ds(base, size), 0:256]
                parts.append(staged[pl.ds(base, size), 256:320])
            parts.append(jnp.zeros((size, 64), BF16))
            rest_ref[pl.ds(rest0 + row, size), :] = jnp.concatenate(parts, axis=1)
    for di in range(3):
        main_ref[pl.ds(main0 + 1024 * di + 960, 64), :] = jnp.zeros((64, 256), BF16)
    rest_ref[pl.ds(rest0 + 960, 64), :] = jnp.zeros((64, 256), BF16)


def rest_sum(y_ref, row0, rows):
    total = y_ref[pl.ds(row0, rows), 0:128] + y_ref[pl.ds(row0 + 256, rows), 128:256]
    return total + pltpu.roll(y_ref[pl.ds(row0 + 128, rows), 0:128], 64, axis=1)


def valid_rows(value, first_row, width):
    row = first_row + lax.broadcasted_iota(jnp.int32, value.shape, 0) // width
    return jnp.where((row >= 0) & (row < 256), value, 0.0)


def pooled(value, width, scratch):
    rows, lanes = value.shape
    tall = jnp.concatenate(
        [jnp.maximum(value[s : s + width], value[s + width : s + 2 * width]) for s in range(0, rows, 2 * width)], axis=0
    )
    halves = []
    for start in range(0, lanes, 128):
        scratch[0 : rows // 2, :] = tall[:, start : start + 128]
        halves.append(
            jnp.maximum(scratch[pl.ds(0, rows // 4, stride=2), :], scratch[pl.ds(1, rows // 4, stride=2), :])
        )
    return jnp.concatenate(halves, axis=1) if len(halves) > 1 else halves[0]


def enc1_kernel(patch, w_a, b_a, w_b, b_b, s1_out, p1_out, x_a, y_rest, w_main, w_rest, pool_buf):
    block = pl.program_id(0)
    strip = strip_index()

    @pl.when(block == 0)
    def _():
        pack_weights(w_b, 320, 0, w_main, 0, w_rest, 0)

        def stem(i, carry):
            row0 = pl.multiple_of(i * 256, 256)
            acc = lax.dot_general(
                patch[:, pl.ds(row0, 256)], w_a[...], (((0,), (0,)), ((), ())), preferred_element_type=F32
            )
            value = valid_rows(jnp.maximum(acc + b_a[...], 0.0), 32 * strip - 3 + 2 * i, 128)
            put3_320(x_a, row0, value[:, 0:256], value[:, 256:384], 128)
            return carry

        lax.fori_loop(0, 19, stem, 0)

        def rest(i, carry):
            row0 = pl.multiple_of(i * 256, 256)
            y_rest[pl.ds(row0, 256), :] = dot(x_a[pl.ds(row0, 256), :], w_rest[...])
            return carry

        lax.fori_loop(0, 19, rest, 0)

    row0 = pl.multiple_of(block * 512, 512)
    acc = dot(x_a[pl.ds(row0, 512), :], w_main[0:1024, :])
    acc = acc + dot(x_a[pl.ds(row0 + 128, 512), :], w_main[1024:2048, :])
    acc = acc + dot(x_a[pl.ds(row0 + 256, 512), :], w_main[2048:3072, :])
    first_row = 32 * strip - 2 + 4 * block
    main = valid_rows(jnp.maximum(acc + b_b[:, 0:256], 0.0), first_row, 128)
    tail = low_lanes(valid_rows(jnp.maximum(rest_sum(y_rest, row0, 512) + b_b[:, 256:384], 0.0), first_row, 128))
    put3_320(s1_out, 0, main, tail, 128)
    put3_320(p1_out, 0, pooled(main, 128, pool_buf), pooled(tail, 128, pool_buf), 64)


def mid_kernel(
    p1, w_2a, w_2b, w_ma, w_mb, w_u2, w_d2a, w_d2b, b_2a, b_2b, b_ma, b_mb, b_d2a, b_d2b, out,
    first_w, ring, x_a, x_s, x_u, m_1, m_2, m_o, d_2, acc_ref, wide, pool_buf,
    sem_2a, sem_2b, sem_ma, sem_mb, sem_u2, sem_d2a, sem_d2b, sem_out, send_sem, recv_sem,
):
    strip = strip_index()
    prev_dev = strip_device((strip + 7) % 8)
    next_dev = strip_device((strip + 1) % 8)

    def exchange(buf, width, lane0, lanes, rows, index):
        lane = pl.ds(lane0, lanes)
        copies = []
        for side, src_row, dst_row, device in ((0, 1, rows + 1, prev_dev), (1, rows, 0, next_dev)):
            copies.append(
                pltpu.make_async_remote_copy(
                    src_ref=buf.at[pl.ds(src_row * width, width), lane],
                    dst_ref=buf.at[pl.ds(dst_row * width, width), lane],
                    send_sem=send_sem.at[index, side],
                    recv_sem=recv_sem.at[index, side],
                    device_id=device,
                    device_id_type=MESH,
                )
            )
        return copies

    def start(copies):
        for copy in copies:
            copy.start()

    def finish(copies):
        for copy in copies:
            copy.wait()

    def halo(buf, width, channels, rows, plain=False):
        for row, inside in ((0, strip > 0), (rows + 1, strip < 7)):
            lanes = pl.ds(0 if plain else channels, channels)
            value = buf[pl.ds(row * width, width), lanes].astype(F32)
            value = jnp.where(inside, value, 0.0)
            if plain:
                buf[pl.ds(row * width, width), lanes] = value.astype(BF16)
            else:
                put3(buf, row * width, 0, channels, value, width)

    copies_2a = []
    for tap in range(9):
        di, dj = tap // 3, tap % 3
        for part, (start_row, size, row) in enumerate(((0, 256, 256 * dj), (256, 64, 768 + 64 * dj))):
            copies_2a.append(
                pltpu.make_async_copy(
                    w_2a.at[pl.ds(320 * tap + start_row, size), :],
                    first_w.at[pl.ds(1024 * di + row, size), :],
                    sem_2a.at[2 * tap + part],
                )
            )

    def tap_copies(src, rows, base, sem):
        return [
            pltpu.make_async_copy(
                src.at[pl.ds(rows * tap, rows), :],
                ring.at[pl.ds(base + rows * (tap // 2), rows), pl.ds(640 * (tap % 2), 640)],
                sem.at[tap],
            )
            for tap in range(src.shape[0] // rows)
        ]

    copies_2b = tap_copies(w_2b, 640, 0, sem_2b)
    copies_ma = [
        pltpu.make_async_copy(w_ma.at[pl.ds(1920 * di, 1920), :], ring.at[pl.ds(3200 + 1920 * t, 1920), :], sem_ma.at[t])
        for t, di in enumerate((1, 0, 2))
    ]

    def mb_row(k):
        return (8960 + 1280 * k) % RING_ROWS

    copies_mb = [
        pltpu.make_async_copy(
            w_mb.at[pl.ds(1280 * (3 * (1, 0, 2)[k // 3] + k % 3), 1280), :], ring.at[pl.ds(mb_row(k), 1280), :], sem_mb.at[k]
        )
        for k in range(9)
    ]
    copies_u2 = tap_copies(w_u2, 1280, 8960, sem_u2)
    copies_d2a = tap_copies(w_d2a, 1280, 0, sem_d2a)
    copies_d2b = tap_copies(w_d2b, 640, 6400, sem_d2b)

    start(copies_2a)
    start(copies_2b)
    start(copies_ma)
    start(copies_mb[0:2])

    barrier = pltpu.get_barrier_semaphore()
    for device in (prev_dev, next_dev):
        pl.semaphore_signal(barrier, inc=1, device_id=device, device_id_type=MESH)
    pl.semaphore_wait(barrier, 2)

    for di in range(3):
        first_w[1024 * di + 960 : 1024 * di + 1024, :] = jnp.zeros((64, 640), BF16)
    finish(copies_2a)

    ex_a = exchange(x_a, 64, 640, 640, 16, 0)
    ex_s = exchange(x_s, 64, 640, 640, 16, 1)
    ex_m1 = exchange(m_1, 32, 640, 640, 8, 2)
    ex_m2 = exchange(m_2, 32, 1280, 1280, 8, 3)
    ex_u = exchange(x_u, 64, 640, 640, 16, 4)
    ex_b = exchange(x_a, 64, 640, 640, 16, 5)
    ex_d = exchange(d_2, 64, 0, 640, 16, 6)
    tiles = ((0, 256), (256, 256), (512, 128))

    def enc2a(i, carry):
        block = i + 1 - 2 * (i % 2)
        row0 = pl.multiple_of(block * 256, 256)

        @pl.when(i == 3)
        def _():
            start(ex_a)

        for lane0, lanes in tiles:
            acc = dot(p1[pl.ds(row0, 256), :], first_w[0:1024, pl.ds(lane0, lanes)])
            for di in (1, 2):
                acc = acc + dot(
                    p1[pl.ds(row0 + 64 * di, 256), :], first_w[1024 * di : 1024 * di + 1024, pl.ds(lane0, lanes)]
                )
            value = jnp.maximum(acc + b_2a[:, pl.ds(lane0, lanes)], 0.0)
            put3(x_a, row0 + 64, lane0, 640, value, 64)
        return carry

    lax.fori_loop(0, 4, enc2a, 0)
    finish(copies_2b)

    def conv640(src, row0, base, lane0, lanes):
        acc = None
        for di in range(3):
            weights = jnp.concatenate(
                [
                    ring[base + 640 * (t // 2) : base + 640 * (t // 2) + 640, pl.ds(640 * (t % 2) + lane0, lanes)]
                    for t in range(3 * di, 3 * di + 3)
                ],
                axis=0,
            )
            part = dot(src[pl.ds(row0 + 64 * di, 256), :], weights)
            acc = part if acc is None else acc + part
        return acc

    def enc2b(i, carry):
        block = i + 1 - 2 * (i % 2)
        row0 = pl.multiple_of(block * 256, 256)

        @pl.when(i == 1)
        def _():
            finish(ex_a)
            halo(x_a, 64, 640, 16)

        @pl.when(i == 3)
        def _():
            start(ex_m1)
            start(ex_s)

        for lane0, lanes in tiles:
            value = jnp.maximum(conv640(x_a, row0, 0, lane0, lanes) + b_2b[:, pl.ds(lane0, lanes)], 0.0)
            put3(x_s, row0 + 64, lane0, 640, value, 64)
            put3(m_1, pl.multiple_of(block * 64 + 32, 32), lane0, 640, pooled(value, 64, pool_buf), 32)
        return carry

    lax.fori_loop(0, 4, enc2b, 0)
    start(copies_mb[2:4])

    acc_ref[...] = jnp.zeros_like(acc_ref)
    finish(copies_ma)

    def mid_a(t, carry):
        di = (t + 1) % 2 + 2 * (t // 2) - t // 2

        @pl.when(t == 1)
        def _():
            finish(ex_m1)
            halo(m_1, 32, 640, 8)

        base = pl.multiple_of(3200 + 1920 * t, 128)
        lhs_row = pl.multiple_of(32 * di, 32)
        for lane0 in range(0, 1280, 256):
            acc_ref[:, pl.ds(lane0, 256)] += dot(
                m_1[pl.ds(lhs_row, 256), :], ring[pl.ds(base, 1920), pl.ds(lane0, 256)]
            )
        return carry

    lax.fori_loop(0, 3, mid_a, 0)
    start(copies_mb[4:9])
    for lane0 in range(0, 1280, 256):
        value = jnp.maximum(acc_ref[:, pl.ds(lane0, 256)] + b_ma[:, pl.ds(lane0, 256)], 0.0)
        put3(m_2, 32, lane0, 1280, value, 32)
    start(ex_m2)
    acc_ref[...] = jnp.zeros_like(acc_ref)

    def mid_b(k, carry):
        t = k // 3
        di = (t + 1) % 2 + 2 * (t // 2) - t // 2

        for j in range(9):
            @pl.when(k == j)
            def _(j=j):
                copies_mb[j].wait()

        @pl.when(k == 3)
        def _():
            start(copies_u2)
            finish(ex_m2)
            halo(m_2, 32, 1280, 8)

        @pl.when(k == 5)
        def _():
            start(copies_d2a[0:4])

        @pl.when(k == 8)
        def _():
            start(copies_d2a[4:9])

        base = pl.multiple_of(mb_row(k), 128)
        lhs_row = pl.multiple_of(32 * di, 32)
        lhs_lane = pl.multiple_of(1280 * (k % 3), 1280)
        for lane0 in range(0, 1280, 256):
            acc_ref[:, pl.ds(lane0, 256)] += dot(
                m_2[pl.ds(lhs_row, 256), pl.ds(lhs_lane, 1280)], ring[pl.ds(base, 1280), pl.ds(lane0, 256)]
            )
        return carry

    lax.fori_loop(0, 9, mid_b, 0)
    for lane0 in range(0, 1280, 256):
        value = jnp.maximum(acc_ref[:, pl.ds(lane0, 256)] + b_mb[:, pl.ds(lane0, 256)], 0.0)
        m_o[:, pl.ds(lane0, 256)] = value.astype(BF16)

    finish(copies_u2)
    for p in range(2):
        for q in range(2):
            for lane0 in range(0, 640, 128):
                wide[lane0 // 128, pl.ds(q, 256, stride=2), :] = dot(
                    m_o[...], ring[8960 + 1280 * p : 10240 + 1280 * p, pl.ds(640 * q + lane0, 128)]
                )

        def place(i, carry):
            src = pl.multiple_of(64 * i, 64)
            dst = pl.multiple_of(64 * (1 + 2 * i + p), 64)
            for lane0 in range(0, 640, 128):
                put3(x_u, dst, lane0, 640, wide[lane0 // 128, pl.ds(src, 64), :], 64)
            return carry

        lax.fori_loop(0, 8, place, 0)
    start(ex_u)
    start(copies_d2b)
    finish(ex_s)
    halo(x_s, 64, 640, 16)
    finish(copies_d2a)

    def dec2a(i, carry):
        block = i + 1 - 2 * (i % 2)
        row0 = pl.multiple_of(block * 256, 256)

        @pl.when(i == 1)
        def _():
            finish(ex_u)
            halo(x_u, 64, 640, 16)

        @pl.when(i == 3)
        def _():
            start(ex_b)

        for lane0, lanes in tiles:
            acc = None
            for tap in range(9):
                rows = pl.ds(row0 + 64 * (tap // 3), 256)
                cols = pl.ds(640 * (tap % 3), 640)
                lhs = jnp.concatenate([x_u[rows, cols], x_s[rows, cols]], axis=1)
                base = 1280 * (tap // 2)
                part = dot(lhs, ring[base : base + 1280, pl.ds(640 * (tap % 2) + lane0, lanes)])
                acc = part if acc is None else acc + part
            value = jnp.maximum(acc + b_d2a[:, pl.ds(lane0, lanes)], 0.0)
            put3(x_a, row0 + 64, lane0, 640, value, 64)
        return carry

    lax.fori_loop(0, 4, dec2a, 0)
    finish(copies_d2b)

    def dec2b(i, carry):
        block = i + 1 - 2 * (i % 2)
        row0 = pl.multiple_of(block * 256, 256)

        @pl.when(i == 1)
        def _():
            finish(ex_b)
            halo(x_a, 64, 640, 16)

        @pl.when(i == 3)
        def _():
            start(ex_d)

        for lane0, lanes in tiles:
            value = jnp.maximum(conv640(x_a, row0, 6400, lane0, lanes) + b_d2b[:, pl.ds(lane0, lanes)], 0.0)
            d_2[pl.ds(row0 + 64, 256), pl.ds(lane0, lanes)] = value.astype(BF16)
        return carry

    lax.fori_loop(0, 4, dec2b, 0)
    finish(ex_d)
    halo(d_2, 64, 640, 16, plain=True)
    result = pltpu.make_async_copy(d_2, out, sem_out)
    result.start()
    result.wait()


def dec1_kernel(
    d_2, s1, w_u1, w_d1a, w_d1b, b_d1a, b_d1b, w_head, b_head, out,
    x_u, x_s, x_d, y_rest, st_u, st_a, st_b, wu_rest, wa_main, wa_rest, wb_main, wb_rest, wide, sem,
):
    strip = strip_index()
    copy_u = pltpu.make_async_copy(w_u1, st_u, sem.at[0])
    copy_a = pltpu.make_async_copy(w_d1a, st_a, sem.at[1])
    copy_s = pltpu.make_async_copy(s1, x_s, sem.at[2])
    copy_b = pltpu.make_async_copy(w_d1b, st_b, sem.at[3])
    for copy in (copy_u, copy_a, copy_s, copy_b):
        copy.start()

    copy_u.wait()
    for start in range(0, 640, 128):
        wu_rest[start : start + 128, :] = jnp.concatenate(
            [st_u[640 * tap + start : 640 * tap + start + 128, 256:320] for tap in range(4)], axis=1
        )

    def up1(i, carry):
        row0 = pl.multiple_of(i * 384, 128)
        lhs = d_2[pl.ds(row0, 384), :]
        rest = dot(lhs, wu_rest[...])
        for p in range(2):
            part = rest[:, 128 * p : 128 * p + 128]
            wide[2, pl.ds(0, 384, stride=2), :] = low_lanes(part)
            wide[2, pl.ds(1, 384, stride=2), :] = low_lanes(pltpu.roll(part, 64, axis=1))
            for q in range(2):
                tap = 2 * p + q
                main = dot(lhs, st_u[640 * tap : 640 * tap + 640, 0:256])
                wide[0, pl.ds(q, 384, stride=2), :] = main[:, 0:128]
                wide[1, pl.ds(q, 384, stride=2), :] = main[:, 128:256]
            for r in range(6):
                main = jnp.concatenate([wide[0, 128 * r : 128 * r + 128, :], wide[1, 128 * r : 128 * r + 128, :]], axis=1)
                put3_320(
                    x_u, pl.multiple_of((12 * i + 2 * r + p) * 128, 128), main, wide[2, 128 * r : 128 * r + 128, :], 128
                )
        return carry

    lax.fori_loop(0, 3, up1, 0)

    copy_a.wait()
    for src in range(2):
        pack_weights(st_a, 640, 320 * src, wa_main, 3072 * src, wa_rest, 1024 * src)
    copy_s.wait()

    def rest_a(i, carry):
        row0 = pl.multiple_of(i * 256, 256)
        rows = pl.ds(row0, 256)
        y_rest[rows, :] = dot(x_u[rows, :], wa_rest[0:1024, :]) + dot(x_s[rows, :], wa_rest[1024:2048, :])
        return carry

    lax.fori_loop(0, 18, rest_a, 0)

    def dec1a(i, carry):
        row0 = pl.multiple_of(i * 256, 256)
        acc = None
        for di in range(3):
            rows = pl.ds(row0 + 128 * di, 256)
            for src, ref in enumerate((x_u, x_s)):
                base = 3072 * src + 1024 * di
                part = dot(ref[rows, :], wa_main[base : base + 1024, :])
                acc = part if acc is None else acc + part
        first_row = 32 * strip - 1 + 2 * i
        main = valid_rows(jnp.maximum(acc + b_d1a[:, 0:256], 0.0), first_row, 128)
        tail = valid_rows(jnp.maximum(rest_sum(y_rest, row0, 256) + b_d1a[:, 256:384], 0.0), first_row, 128)
        put3_320(x_d, row0, main, low_lanes(tail), 128)
        return carry

    lax.fori_loop(0, 17, dec1a, 0)

    copy_b.wait()
    pack_weights(st_b, 320, 0, wb_main, 0, wb_rest, 0)

    def rest_b(i, carry):
        rows = pl.ds(pl.multiple_of(i * 256, 256), 256)
        y_rest[rows, :] = dot(x_d[rows, :], wb_rest[...])
        return carry

    lax.fori_loop(0, 17, rest_b, 0)

    def dec1b(i, carry):
        row0 = pl.multiple_of(i * 512, 512)
        acc = dot(x_d[pl.ds(row0, 512), :], wb_main[0:1024, :])
        acc = acc + dot(x_d[pl.ds(row0 + 128, 512), :], wb_main[1024:2048, :])
        acc = acc + dot(x_d[pl.ds(row0 + 256, 512), :], wb_main[2048:3072, :])
        main = jnp.maximum(acc + b_d1b[:, 0:256], 0.0).astype(BF16)
        tail = low_lanes(jnp.maximum(rest_sum(y_rest, row0, 512) + b_d1b[:, 256:384], 0.0)).astype(BF16)
        hidden = jnp.concatenate([main, tail], axis=1)
        head = lax.dot_general(w_head[...], hidden, (((1,), (1,)), ((), ())), preferred_element_type=F32)
        out[:, pl.ds(row0, 512)] = head[0:8, :] + b_head[...]
        return carry

    lax.fori_loop(0, 8, dec1b, 0)


def solution(mesh):
    tile_spec = P(("data", "row"), "col", None)

    def body(image_tile, *params):
        (w_enc1a, b_enc1a, w_enc1b, b_enc1b, w_enc2a, b_enc2a, w_enc2b, b_enc2b,
         w_mid_a, b_mid_a, w_mid_b, b_mid_b, w_up2, w_dec2a, b_dec2a, w_dec2b, b_dec2b,
         w_up1, w_dec1a, b_dec1a, w_dec1b, b_dec1b, w_head, b_head) = params
        strip = strip_index()
        row = lax.axis_index("row")
        col = lax.axis_index("col")

        planes = lax.all_gather(image_tile.transpose(2, 0, 1), ("col", "row"), axis=0)
        planes = planes.reshape(2, 4, 4, 64, 64).transpose(2, 1, 3, 0, 4).reshape(4, 256, 128)
        planes = jnp.pad(planes, ((0, 0), (4, 4), (1, 1)))
        planes = lax.dynamic_slice_in_dim(planes, 32 * strip, 40, axis=1)
        patch = jnp.stack([planes[:, di : di + 38, dj : dj + 128] for di in range(3) for dj in range(3)])
        patch = jnp.pad(patch.reshape(36, 38 * 128), ((0, 12), (0, 0)))

        def flat(weight):
            return weight.reshape(-1, weight.shape[-1])

        def wide_bias(bias):
            return jnp.pad(bias, (0, 384 - bias.shape[0]))[None]

        vmem = pl.BlockSpec(memory_space=pltpu.VMEM)
        hbm = pl.BlockSpec(memory_space=pl.ANY)
        whole = lambda i: (0, 0)
        s1, p1 = pl.pallas_call(
            enc1_kernel,
            grid=(9,),
            out_shape=(jax.ShapeDtypeStruct((4608, 1024), BF16), jax.ShapeDtypeStruct((1152, 1024), BF16)),
            in_specs=[
                pl.BlockSpec((48, 4864), whole),
                pl.BlockSpec((48, 384), whole),
                pl.BlockSpec((1, 384), whole),
                pl.BlockSpec((2880, 320), whole),
                pl.BlockSpec((1, 384), whole),
            ],
            out_specs=(pl.BlockSpec((512, 1024), lambda i: (i, 0)), pl.BlockSpec((128, 1024), lambda i: (i, 0))),
            scratch_shapes=[
                pltpu.VMEM((4864, 1024), BF16),
                pltpu.VMEM((4864, 256), F32),
                pltpu.VMEM((3072, 256), BF16),
                pltpu.VMEM((1024, 256), BF16),
                pltpu.VMEM((256, 128), F32),
            ],
            compiler_params=pltpu.CompilerParams(vmem_limit_bytes=VMEM_LIMIT, dimension_semantics=("arbitrary",)),
            name="enc1",
        )(
            patch,
            jnp.pad(w_enc1a.reshape(36, 320), ((0, 12), (0, 64))),
            wide_bias(b_enc1a),
            flat(w_enc1b),
            wide_bias(b_enc1b),
        )

        dma = pltpu.SemaphoreType.DMA
        d2 = pl.pallas_call(
            mid_kernel,
            out_shape=jax.ShapeDtypeStruct((1152, 640), BF16),
            in_specs=[vmem] + [hbm] * 7 + [vmem] * 6,
            out_specs=hbm,
            scratch_shapes=[
                pltpu.VMEM((3072, 640), BF16),
                pltpu.VMEM((RING_ROWS, 1280), BF16),
                pltpu.VMEM((1152, 1920), BF16),
                pltpu.VMEM((1152, 1920), BF16),
                pltpu.VMEM((1152, 1920), BF16),
                pltpu.VMEM((320, 1920), BF16),
                pltpu.VMEM((320, 3840), BF16),
                pltpu.VMEM((256, 1280), BF16),
                pltpu.VMEM((1152, 640), BF16),
                pltpu.VMEM((256, 1280), F32),
                pltpu.VMEM((5, 512, 128), F32),
                pltpu.VMEM((128, 128), F32),
                dma((18,)), dma((9,)), dma((3,)), dma((9,)), dma((4,)), dma((9,)), dma((9,)), dma,
                dma((7, 2)), dma((7, 2)),
            ],
            compiler_params=pltpu.CompilerParams(
                vmem_limit_bytes=VMEM_LIMIT, collective_id=0, has_side_effects=True
            ),
            name="mid",
        )(
            p1, flat(w_enc2a), flat(w_enc2b), flat(w_mid_a), flat(w_mid_b), flat(w_up2), flat(w_dec2a), flat(w_dec2b),
            b_enc2a[None], b_enc2b[None], b_mid_a[None], b_mid_b[None], b_dec2a[None], b_dec2b[None],
        )

        y = pl.pallas_call(
            dec1_kernel,
            out_shape=jax.ShapeDtypeStruct((8, 4096), F32),
            in_specs=[vmem] + [hbm] * 4 + [vmem] * 4,
            out_specs=vmem,
            scratch_shapes=[
                pltpu.VMEM((4608, 1024), BF16),
                pltpu.VMEM((4608, 1024), BF16),
                pltpu.VMEM((4352, 1024), BF16),
                pltpu.VMEM((4608, 256), F32),
                pltpu.VMEM((2560, 320), BF16),
                pltpu.VMEM((5760, 320), BF16),
                pltpu.VMEM((2880, 320), BF16),
                pltpu.VMEM((640, 256), BF16),
                pltpu.VMEM((6144, 256), BF16),
                pltpu.VMEM((2048, 256), BF16),
                pltpu.VMEM((3072, 256), BF16),
                pltpu.VMEM((1024, 256), BF16),
                pltpu.VMEM((3, 768, 128), F32),
                dma((4,)),
            ],
            compiler_params=pltpu.CompilerParams(vmem_limit_bytes=VMEM_LIMIT),
            name="dec1",
        )(
            d2, s1, flat(w_up1), flat(w_dec1a), flat(w_dec1b), wide_bias(b_dec1a), wide_bias(b_dec1b),
            jnp.pad(w_head.T, ((0, 12), (0, 64))),
            jnp.pad(b_head, (0, 4))[:, None],
        )

        strips = lax.all_gather(y[0:4].reshape(4, 32, 128), ("col", "row"), axis=0)
        strips = jnp.concatenate([strips[0:4], strips[4:8][::-1]], axis=0)
        pair = lax.dynamic_slice_in_dim(strips, 2 * row, 2, axis=0)
        pair = lax.dynamic_slice_in_dim(pair, 64 * col, 64, axis=3)
        return pair.transpose(0, 2, 3, 1).reshape(64, 64, 4)

    def program(image, *params):
        mapped = jax.shard_map(
            body, mesh=mesh, in_specs=(tile_spec,) + (P(),) * len(params), out_specs=tile_spec, check_vma=False
        )
        return mapped(image, *params)

    return program
```

time: 555 us -> 208 us (0.37)
  the two profiles are of different devices: /device:TPU:6 before, /device:TPU:0 now
where the time goes in v1:
time: 208 us; the launch traced here: 207 us
  Pallas kernels  156 us (75%)
  blocking collectives  27.5 us (13%)
  local copies, waits for them, and re-layouts  23.5 us (11%)
    pallas_call x1, Pallas kernels, body(): pl.pallas_call(mid_kernel, out_shape=jax.ShapeDtypeStruct((1152, 640), BF...  80.5 us
    pallas_call x1, Pallas kernels, body(): pl.pallas_call(dec1_kernel, out_shape=jax.ShapeDtypeStruct((8, 4096), F32...  47.8 us
    pallas_call x1, Pallas kernels, body(): pl.pallas_call(enc1_kernel, grid=(9,), out_shape=(jax.ShapeDtypeStruct((4...  27.7 us
    all_gather x1, blocking collectives, body(): lax.all_gather(image_tile.transpose(2, 0, 1), ('col', 'row'), axis=0)  15.1 us
    unnamed x44, local copies, waits for them, and re-layouts  13.3 us
    all_gather x1, blocking collectives, body(): strips = lax.all_gather(y[0:4].reshape(4, 32, 128), ('col', 'row'), axis=0)  12.3 us

profile of v1, /device:TPU:0, one launch (start us, length us, event | category | flops | bytes accessed | tf_op | source)
XLA Modules:
  0.0 207.4 jit_solution(12765606276810886206)
XLA Ops:
  0.0 0.9 copy.58
  0.9 15.1 %all-gather = bf16[32,64,64]{2,1,0:T(8,128)(2,1)S(1)} all-gather(bf16[4,64,64]{2,1,0:T(8,128)(2,1)S(1)} %bitcast.67), channel_id=2, replica_groups=mesh['data'=1,'col'=2,'row'=4] {'col','row'}, dimensions={0}, use_global_device_ids=true | all-gather | bytes 294912 | tf_op jit(solution)/shard_map/all_gather | solution.py:550
  16.0 0.5 copy.42
  18.2 0.8 pad.34.patch
  19.0 0.6 pad.35.w_a
  20.2 0.6 broadcast_in_dim.34.b_b
  20.8 27.7 %enc1.1 = (bf16[4608,1024]{1,0:T(8,128)(2,1)}, bf16[1152,1024]{1,0:T(8,128)(2,1)}) custom-call(bf16[48,4864]{1,0:T(8,128)(2,1)} %pad.34.patch, bf16[48,384]{1,0:T(8,128)(2,1)} %pad.35.w_a, f32[1,384]{1,0:T(1,128)} %broadcast_in_dim.33.b_a, bf16[2880,320]{1,0:T(8,128)(2,1)} %bitcast.60, f32[1,384]{1,0:T(1,128)} %broadcast_in_dim.34.b_b), custom_call_target="tpu_custom_call" | custom-call | tf_op jit(solution)/shard_map/enc1/pallas_call | solution.py:566
  48.5 0.6 broadcast_in_dim.37.b_ma
  49.1 0.6 broadcast_in_dim.38.b_mb
  49.7 0.6 broadcast_in_dim.35.b_2a
  50.3 0.6 broadcast_in_dim.36.b_2b
  50.9 0.6 broadcast_in_dim.39.b_d2a
  51.5 0.5 broadcast_in_dim.40.b_d2b
  52.0 80.5 %mid.1.d_2 = bf16[1152,640]{1,0:T(8,128)(2,1)} custom-call(bf16[1152,1024]{1,0:T(8,128)(2,1)} %get-tuple-element.7.p1, bf16[2880,640]{1,0:T(8,128)(2,1)} %bitcast.59, bf16[5760,640]{1,0:T(8,128)(2,1)} %bitcast.56, bf16[5760,1280]{1,0:T(8,128)(2,1)} %bitcast.53, bf16[11520,1280]{1,0:T(8,128)(2,1)} %bitcast.51, bf16[5120,640]{1,0:T(8,128)(2,1)} %bitcast.58, ...), custom_call_target="tpu_custom_call" | custom-call | tf_op jit(solution)/shard_map/mid/pallas_call | solution.py:596
  132.6 7.9 %copy.44 = bf16[3,3,640,320]{3,2,1,0:T(8,128)(2,1)} copy(bf16[3,3,640,320]{2,3,1,0:T(8,128)(2,1)} %param.44) | data formatting | bytes 7372800 | tf_op args[19]
  140.5 2.4 %copy.43 = bf16[2,2,640,320]{3,2,1,0:T(8,128)(2,1)} copy(bf16[2,2,640,320]{2,3,1,0:T(8,128)(2,1)S(1)} %copy-done) | data formatting | bytes 3276800 | tf_op args[18]
  142.9 0.6 pad.40.w_head
  143.5 0.7 copy.45.b_head
  144.2 0.6 broadcast_in_dim.41.b_d1a
  144.8 0.6 broadcast_in_dim.42.b_d1b
  145.4 47.8 %dec1.1 = f32[8,4096]{1,0:T(8,128)} custom-call(bf16[1152,640]{1,0:T(8,128)(2,1)} %mid.1.d_2, bf16[4608,1024]{1,0:T(8,128)(2,1)} %get-tuple-element.8.s1, bf16[2560,320]{1,0:T(8,128)(2,1)} %bitcast.55, bf16[5760,320]{1,0:T(8,128)(2,1)} %bitcast.52, bf16[2880,320]{1,0:T(8,128)(2,1)} %bitcast.61, f32[1,384]{1,0:T(1,128)} %broadcast_in_dim.41.b_d1a, ...), custom_call_target="tpu_custom_call" | custom-call | tf_op jit(solution)/shard_map/dec1/pallas_call | solution.py:626
  193.2 0.9 slice_bitcast_fusion
  194.1 12.3 %all_gather.11 = f32[8,4,32,128]{3,2,1,0:T(8,128)S(1)} all-gather(f32[1,4,32,128]{3,2,1,0:T(8,128)S(1)} %copy.57), channel_id=1, replica_groups=mesh['data'=1,'col'=2,'row'=4] {'col','row'}, dimensions={0}, use_global_device_ids=true | all-gather | bytes 589824 | tf_op jit(solution)/shard_map/all_gather | solution.py:655
  206.7 0.7 copy.48
  (52 shorter events, 2.3 us)
Async XLA Ops:
  0.0 19.0 %copy-start.1 = (bf16[3,3,4,320]{3,2,1,0:T(4,128)(2,1)S(1)}, bf16[3,3,4,320]{3,2,1,0:T(4,128)(2,1)}, u32[]{:S(2)}) copy-start(bf16[3,3,4,320]{3,2,1,0:T(4,128)(2,1)} %param.26) | copy-start | bytes 69124
  0.0 19.6 %copy-start.9 = (f32[320]{0:T(512)S(1)}, f32[320]{0:T(512)}, u32[]{:S(2)}) copy-start(f32[320]{0:T(512)} %param.27) | copy-start | bytes 3844
  0.0 20.1 %copy-start.10 = (f32[320]{0:T(512)S(1)}, f32[320]{0:T(512)}, u32[]{:S(2)}) copy-start(f32[320]{0:T(512)} %param.29) | copy-start | bytes 3844
  16.6 31.9 %copy-start.2 = (f32[1280]{0:T(1024)S(1)}, f32[1280]{0:T(1024)}, u32[]{:S(2)}) copy-start(f32[1280]{0:T(1024)} %param.35) | copy-start | bytes 15364
  16.6 32.5 %copy-start.3 = (f32[1280]{0:T(1024)S(1)}, f32[1280]{0:T(1024)}, u32[]{:S(2)}) copy-start(f32[1280]{0:T(1024)} %param.37) | copy-start | bytes 15364
  16.6 33.1 %copy-start.4 = (f32[640]{0:T(1024)S(1)}, f32[640]{0:T(1024)}, u32[]{:S(2)}) copy-start(f32[640]{0:T(1024)} %param.31) | copy-start | bytes 7684
  16.6 33.6 %copy-start.5 = (f32[640]{0:T(1024)S(1)}, f32[640]{0:T(1024)}, u32[]{:S(2)}) copy-start(f32[640]{0:T(1024)} %param.33) | copy-start | bytes 7684
  16.6 34.2 %copy-start.6 = (f32[640]{0:T(1024)S(1)}, f32[640]{0:T(1024)}, u32[]{:S(2)}) copy-start(f32[640]{0:T(1024)} %param.40) | copy-start | bytes 7684
  16.7 34.8 %copy-start.7 = (f32[640]{0:T(1024)S(1)}, f32[640]{0:T(1024)}, u32[]{:S(2)}) copy-start(f32[640]{0:T(1024)} %param.42) | copy-start | bytes 7684
  132.6 7.9 %copy-start = (bf16[2,2,640,320]{2,3,1,0:T(8,128)(2,1)S(1)}, bf16[2,2,640,320]{2,3,1,0:T(8,128)(2,1)}, u32[]{:S(2)}) copy-start(bf16[2,2,640,320]{2,3,1,0:T(8,128)(2,1)} %param.43) | copy-start | bytes 4915204
  132.6 10.4 %copy-start.8 = (bf16[320,4]{0,1:T(4,128)(2,1)S(1)}, bf16[320,4]{0,1:T(4,128)(2,1)}, u32[]{:S(2)}) copy-start(bf16[320,4]{0,1:T(4,128)(2,1)} %param.48) | copy-start | bytes 7684
  132.6 11.0 %copy-start.13 = (f32[4]{0:T(128)S(1)}, f32[4]{0:T(128)}, u32[]{:S(2)}) copy-start(f32[4]{0:T(128)} %param.49) | copy-start | bytes 52
  132.6 11.6 %copy-start.11 = (f32[320]{0:T(512)S(1)}, f32[320]{0:T(512)}, u32[]{:S(2)}) copy-start(f32[320]{0:T(512)} %param.45) | copy-start | bytes 3844
  132.6 12.2 %copy-start.12 = (f32[320]{0:T(512)S(1)}, f32[320]{0:T(512)}, u32[]{:S(2)}) copy-start(f32[320]{0:T(512)} %param.47) | copy-start | bytes 3844

commit v2 on v1

v2 whole, which is shorter than its diff:
```python
import functools

import jax
import jax.numpy as jnp
from jax import lax
from jax.experimental import pallas as pl
from jax.experimental.pallas import tpu as pltpu
from jax.sharding import PartitionSpec as P

IN_CH = 4
FIVE = 5
SIX = 6
LAST_STRIP = 7
STRIPS = 8
TAPS = 9
N12 = 12
N16 = 16
N18 = 18
N28 = 28
N31 = 31
STRIP_ROWS = 32
N36 = 36
N40 = 40
N42 = 42
N60 = 60
REST = 64
N96 = 96
N127 = 127
LANES = 128
TILE = 256
BASE = 320
BASE_PAD = 384
N512 = 512
MIDDLE = 640
REST_AT = 768
N896 = 896
PACK_USED = 960
PACK = 1024
N1152 = 1152
DEEP = 1280
N1536 = 1536
N1792 = 1792
MIDDLE3 = 1920
N2048 = 2048
N2560 = 2560
N2880 = 2880
N3072 = 3072
N3200 = 3200
N3840 = 3840
N4096 = 4096
N4352 = 4352
N4608 = 4608
N5120 = 5120
N6144 = 6144
N6400 = 6400
N8960 = 8960
N10240 = 10240
N11520 = 11520
BF16 = jnp.bfloat16
F32 = jnp.float32
MESH = pl.DeviceIdType.MESH
VMEM_LIMIT = 66_900_000
RING_ROWS = N11520


def strip_index():
    col = lax.axis_index("col")
    row = lax.axis_index("row")
    return row + col * (LAST_STRIP - 2 * row)


def strip_device(position):
    col = position // IN_CH
    rest = position % IN_CH
    return (lax.axis_index("data"), col, rest + col * (3 - 2 * rest))


def dot(a, b):
    return jnp.dot(a, b, preferred_element_type=F32)


def shifted(value, width, step):
    if step == 1:
        return value
    rows = value.shape[0]
    column = lax.broadcasted_iota(jnp.int32, value.shape, 0) % width
    if step == 0:
        return jnp.where(column == 0, 0.0, pltpu.roll(value, 1, axis=0))
    return jnp.where(column == width - 1, 0.0, pltpu.roll(value, rows - 1, axis=0))


def put3(dst, row0, lane0, channels, value, width):
    rows, lanes = value.shape
    for step in range(3):
        dst[pl.ds(row0, rows), pl.ds(step * channels + lane0, lanes)] = shifted(value, width, step).astype(BF16)


def put3_320(dst, row0, main, rest, width):
    rows = main.shape[0]
    for step in range(3):
        dst[pl.ds(row0, rows), pl.ds(step * TILE, TILE)] = shifted(main, width, step).astype(BF16)
    first = shifted(rest, width, 0) + pltpu.roll(rest, REST, axis=1)
    dst[pl.ds(row0, rows), pl.ds(REST_AT, LANES)] = first.astype(BF16)
    dst[pl.ds(row0, rows), pl.ds(N896, LANES)] = shifted(rest, width, 2).astype(BF16)


def low_lanes(value):
    return jnp.where(lax.broadcasted_iota(jnp.int32, value.shape, 1) < REST, value, 0.0)


def pack_weights(staged, main_ref, rest_ref):
    for dj in range(3):
        for start, size, row in ((0, TILE, TILE * dj), (TILE, REST, REST_AT + REST * dj)):
            parts = []
            for di in range(3):
                base = (3 * di + dj) * BASE + start
                main_ref[pl.ds(PACK * di + row, size), :] = staged[pl.ds(base, size), 0:TILE]
                parts.append(staged[pl.ds(base, size), TILE:BASE])
            parts.append(jnp.zeros((size, REST), BF16))
            rest_ref[pl.ds(row, size), :] = jnp.concatenate(parts, axis=1)
    clear_pad(main_ref, 3)
    clear_pad(rest_ref, 1)


def clear_pad(ref, groups):
    for group in range(groups):
        ref[pl.ds(PACK * group + PACK_USED, REST), :] = jnp.zeros((REST, ref.shape[1]), BF16)


def pack_transposed(staged, main_ref, rest_ref):
    for dj in range(3):

        def main_part(di, carry):
            turned = staged[pl.ds(pl.multiple_of(PACK_USED * di + BASE * dj, REST), TILE), :].T
            for src in range(2):
                base = N3072 * src + PACK * di
                main_ref[pl.ds(pl.multiple_of(base + TILE * dj, REST), TILE), :] = turned[BASE * src : BASE * src + TILE]
                main_ref[pl.ds(pl.multiple_of(base + REST_AT + REST * dj, REST), REST), :] = turned[BASE * src + TILE : BASE * src + BASE]
            return carry

        lax.fori_loop(0, 3, main_part, 0)
        parts = [staged[pl.ds(PACK_USED * di + BASE * dj + TILE, REST), :] for di in range(3)] + [jnp.zeros((REST, MIDDLE), BF16)]
        turned = jnp.concatenate(parts, axis=0).T
        for src in range(2):
            rest_ref[pl.ds(PACK * src + TILE * dj, TILE), :] = turned[BASE * src : BASE * src + TILE]
            rest_ref[pl.ds(PACK * src + REST_AT + REST * dj, REST), :] = turned[BASE * src + TILE : BASE * src + BASE]
    clear_pad(main_ref, SIX)
    clear_pad(rest_ref, 2)


def bias_row(ref, start, size):
    return ref[pl.ds(start, size)].reshape(1, size)


def bias_rest(ref):
    return jnp.concatenate([bias_row(ref, TILE, REST), jnp.zeros((1, REST), F32)], axis=1)


def enter_barrier():
    barrier = pltpu.get_barrier_semaphore()
    for position in range(STRIPS):
        pl.semaphore_signal(barrier, inc=1, device_id=strip_device(position), device_id_type=MESH)
    return barrier


class Push:
    def __init__(self, src, dst, send_sem, recv_sem, device, here):
        self.here = here
        self.local = pltpu.make_async_copy(src, dst, recv_sem)
        self.remote = pltpu.make_async_remote_copy(
            src_ref=src, dst_ref=dst, send_sem=send_sem, recv_sem=recv_sem, device_id=device, device_id_type=MESH
        )

    def start(self):
        @pl.when(self.here)
        def _():
            self.local.start()

        @pl.when(jnp.logical_not(self.here))
        def _():
            self.remote.start()

    def wait_send(self):
        @pl.when(jnp.logical_not(self.here))
        def _():
            self.remote.wait_send()

    def wait_recv(self):
        self.remote.wait_recv()


def rest_sum(y_ref, row0, rows):
    total = y_ref[pl.ds(row0, rows), 0:LANES] + y_ref[pl.ds(row0 + TILE, rows), LANES:TILE]
    return total + pltpu.roll(y_ref[pl.ds(row0 + LANES, rows), 0:LANES], REST, axis=1)


def valid_rows(value, first_row, width):
    row = first_row + lax.broadcasted_iota(jnp.int32, value.shape, 0) // width
    return jnp.where((row >= 0) & (row < TILE), value, 0.0)


def pooled(value, width, scratch):
    rows, lanes = value.shape
    tall = jnp.concatenate(
        [jnp.maximum(value[s : s + width], value[s + width : s + 2 * width]) for s in range(0, rows, 2 * width)], axis=0
    )
    halves = []
    for start in range(0, lanes, LANES):
        scratch[0 : rows // 2, :] = tall[:, start : start + LANES]
        halves.append(
            jnp.maximum(scratch[pl.ds(0, rows // IN_CH, stride=2), :], scratch[pl.ds(1, rows // IN_CH, stride=2), :])
        )
    return jnp.concatenate(halves, axis=1) if len(halves) > 1 else halves[0]


def enc1_kernel(
    image, w_a, b_a, w_b, b_b, s1_out, p1_out,
    halves, planes, w_stem, staged, x_a, y_rest, w_main, w_rest, pool_buf, w_sem, send_sem, recv_sem,
):
    step = pl.program_id(0)
    strip = strip_index()

    @pl.when(step == 0)
    def _():
        row = lax.axis_index("row")
        col = lax.axis_index("col")
        copy_w = pltpu.make_async_copy(w_b, staged, w_sem)
        copy_w.start()
        barrier = enter_barrier()

        for di in range(3):
            taps = []
            for dj in range(3):
                tap = jnp.concatenate([w_a[di, dj].astype(F32), jnp.zeros((IN_CH, BASE), F32)], axis=0)
                taps.append(jnp.concatenate([tap, jnp.zeros((STRIPS, REST), F32)], axis=1))
            taps.append(jnp.zeros((STRIPS, BASE_PAD), F32))
            w_stem[STRIP_ROWS * di : STRIP_ROWS * di + STRIP_ROWS, :] = jnp.concatenate(taps, axis=0).astype(BF16)
        planes[N40:N42, :, :] = jnp.zeros((2, STRIP_ROWS, LANES), BF16)

        pl.semaphore_wait(barrier, STRIPS)
        pushes = []
        for index, (target, src_row, dst_row, rows) in enumerate(
            ((2 * row, 0, IN_CH, N36), (2 * row + 1, N28, 0, N36), ((2 * row + 2) % STRIPS, N60, 0, IN_CH), ((2 * row + LAST_STRIP) % STRIPS, 0, N36, IN_CH))
        ):
            pushes.append(
                Push(
                    image.at[pl.ds(src_row, rows)],
                    halves.at[col, pl.ds(dst_row, rows)],
                    send_sem.at[index],
                    recv_sem.at[index // 2, col],
                    strip_device(target),
                    target == strip,
                )
            )
        for push in pushes:
            push.start()
        copy_w.wait()
        pack_weights(staged, w_main, w_rest)
        for push in pushes:
            push.wait_send()
        for kind, rows in ((0, N36), (1, IN_CH)):
            for side in range(2):
                Push(
                    image.at[pl.ds(0, rows)], halves.at[side, pl.ds(0, rows)],
                    send_sem.at[0], recv_sem.at[kind, side], strip_device(strip), strip < 0,
                ).wait_recv()

        def expand(i, carry):
            for j in range(STRIPS):
                r = STRIPS * i + j
                both = jnp.concatenate([halves[0, r].astype(F32), halves[1, r].astype(F32)], axis=1)
                image_row = STRIP_ROWS * strip - IN_CH + r
                both = jnp.where((image_row >= 0) & (image_row < TILE), both, 0.0)
                both = jnp.concatenate([both, jnp.zeros((IN_CH, LANES), F32)], axis=0)
                column = lax.broadcasted_iota(jnp.int32, (STRIPS, LANES), 1)
                before = jnp.where(column == 0, 0.0, pltpu.roll(both, 1, axis=1))
                after = jnp.where(column == N127, 0.0, pltpu.roll(both, N127, axis=1))
                planes[r] = jnp.concatenate([before, both, after, jnp.zeros((STRIPS, LANES), F32)], axis=0).astype(BF16)
            return carry

        lax.fori_loop(0, FIVE, expand, 0)

        def stem(i, carry):
            for j in range(IN_CH):
                r = STRIPS * i + 2 * j
                row0 = pl.multiple_of(r * LANES, TILE)
                patch = jnp.concatenate(
                    [jnp.concatenate([planes[r + k + di] for di in range(3)], axis=0) for k in range(2)], axis=1
                )
                acc = lax.dot_general(patch, w_stem[...], (((0,), (0,)), ((), ())), preferred_element_type=F32)
                main = jnp.maximum(acc[:, 0:TILE] + bias_row(b_a, 0, TILE), 0.0)
                tail = jnp.maximum(acc[:, TILE:BASE_PAD] + bias_rest(b_a), 0.0)
                first_row = STRIP_ROWS * strip - 3 + r
                put3_320(x_a, row0, valid_rows(main, first_row, LANES), valid_rows(tail, first_row, LANES), LANES)
            return carry

        lax.fori_loop(0, FIVE, stem, 0)

    base = pl.multiple_of(step * N1536, N512)

    def rest(j):
        y_rest[TILE * j : TILE * j + TILE, :] = dot(x_a[pl.ds(base + TILE * j, TILE), :], w_rest[...])

    rest(0)
    for j in range(SIX):
        rest(j + 1)
        acc = dot(x_a[pl.ds(base + TILE * j, TILE), :], w_main[0:PACK, :])
        acc = acc + dot(x_a[pl.ds(base + TILE * j + LANES, TILE), :], w_main[PACK:N2048, :])
        acc = acc + dot(x_a[pl.ds(base + TILE * j + TILE, TILE), :], w_main[N2048:N3072, :])
        first_row = STRIP_ROWS * strip - 2 + N12 * step + 2 * j
        main = valid_rows(jnp.maximum(acc + bias_row(b_b, 0, TILE), 0.0), first_row, LANES)
        tail = jnp.maximum(rest_sum(y_rest, TILE * j, TILE) + bias_rest(b_b), 0.0)
        tail = low_lanes(valid_rows(tail, first_row, LANES))
        put3_320(s1_out, TILE * j, main, tail, LANES)
        put3_320(p1_out, REST * j, pooled(main, LANES, pool_buf), pooled(tail, LANES, pool_buf), REST)


def mid_kernel(
    p1, w_2a, w_2b, w_ma, w_mb, w_u2, w_d2a, w_d2b, b_2a, b_2b, b_ma, b_mb, b_d2a, b_d2b, out,
    first_w, ring, x_a, x_s, x_u, m_1, m_2, m_o, d_2, acc_ref, wide, pool_buf,
    sem_2a, sem_2b, sem_ma, sem_mb, sem_u2, sem_d2a, sem_d2b, sem_out, send_sem, recv_sem,
):
    strip = strip_index()
    prev_dev = strip_device((strip + LAST_STRIP) % STRIPS)
    next_dev = strip_device((strip + 1) % STRIPS)

    def exchange(buf, width, lane0, lanes, rows, index):
        lane = pl.ds(lane0, lanes)
        copies = []
        for side, src_row, dst_row, device in ((0, 1, rows + 1, prev_dev), (1, rows, 0, next_dev)):
            copies.append(
                pltpu.make_async_remote_copy(
                    src_ref=buf.at[pl.ds(src_row * width, width), lane],
                    dst_ref=buf.at[pl.ds(dst_row * width, width), lane],
                    send_sem=send_sem.at[index, side],
                    recv_sem=recv_sem.at[index, side],
                    device_id=device,
                    device_id_type=MESH,
                )
            )
        return copies

    def start(copies):
        for copy in copies:
            copy.start()

    def finish(copies):
        for copy in copies:
            copy.wait()

    def halo(buf, width, channels, rows, plain=False):
        for row, inside in ((0, strip > 0), (rows + 1, strip < LAST_STRIP)):
            lanes = pl.ds(0 if plain else channels, channels)
            value = buf[pl.ds(row * width, width), lanes].astype(F32)
            value = jnp.where(inside, value, 0.0)
            if plain:
                buf[pl.ds(row * width, width), lanes] = value.astype(BF16)
            else:
                put3(buf, row * width, 0, channels, value, width)

    copies_2a = []
    for tap in range(TAPS):
        di, dj = tap // 3, tap % 3
        for part, (start_row, size, row) in enumerate(((0, TILE, TILE * dj), (TILE, REST, REST_AT + REST * dj))):
            copies_2a.append(
                pltpu.make_async_copy(
                    w_2a.at[pl.ds(BASE * tap + start_row, size), :],
                    first_w.at[pl.ds(PACK * di + row, size), :],
                    sem_2a.at[2 * tap + part],
                )
            )

    def tap_copies(src, rows, base, sem):
        return [
            pltpu.make_async_copy(
                src.at[pl.ds(rows * tap, rows), :],
                ring.at[pl.ds(base + rows * (tap // 2), rows), pl.ds(MIDDLE * (tap % 2), MIDDLE)],
                sem.at[tap],
            )
            for tap in range(src.shape[0] // rows)
        ]

    copies_2b = tap_copies(w_2b, MIDDLE, 0, sem_2b)
    copies_ma = [
        pltpu.make_async_copy(w_ma.at[pl.ds(MIDDLE3 * di, MIDDLE3), :], ring.at[pl.ds(N3200 + MIDDLE3 * t, MIDDLE3), :], sem_ma.at[t])
        for t, di in enumerate((1, 0, 2))
    ]

    def mb_row(k):
        return (N8960 + DEEP * k) % RING_ROWS

    copies_mb = [
        pltpu.make_async_copy(
            w_mb.at[pl.ds(DEEP * (3 * (1, 0, 2)[k // 3] + k % 3), DEEP), :], ring.at[pl.ds(mb_row(k), DEEP), :], sem_mb.at[k]
        )
        for k in range(TAPS)
    ]
    copies_u2 = tap_copies(w_u2, DEEP, N8960, sem_u2)
    copies_d2a = tap_copies(w_d2a, DEEP, 0, sem_d2a)
    copies_d2b = tap_copies(w_d2b, MIDDLE, N6400, sem_d2b)

    start(copies_2a)
    start(copies_2b)
    start(copies_ma)
    start(copies_mb[0:2])

    barrier = pltpu.get_barrier_semaphore()
    for device in (prev_dev, next_dev):
        pl.semaphore_signal(barrier, inc=1, device_id=device, device_id_type=MESH)
    pl.semaphore_wait(barrier, 2)

    for di in range(3):
        first_w[PACK * di + PACK_USED : PACK * di + PACK, :] = jnp.zeros((REST, MIDDLE), BF16)
    finish(copies_2a)

    ex_a = exchange(x_a, REST, MIDDLE, MIDDLE, N16, 0)
    ex_s = exchange(x_s, REST, MIDDLE, MIDDLE, N16, 1)
    ex_m1 = exchange(m_1, STRIP_ROWS, MIDDLE, MIDDLE, STRIPS, 2)
    ex_m2 = exchange(m_2, STRIP_ROWS, DEEP, DEEP, STRIPS, 3)
    ex_u = exchange(x_u, REST, MIDDLE, MIDDLE, N16, IN_CH)
    ex_b = exchange(x_a, REST, MIDDLE, MIDDLE, N16, FIVE)
    ex_d = exchange(d_2, REST, 0, MIDDLE, N16, SIX)
    tiles = ((0, TILE), (TILE, TILE), (N512, LANES))

    def enc2a(i, carry):
        block = i + 1 - 2 * (i % 2)
        row0 = pl.multiple_of(block * TILE, TILE)

        @pl.when(i == 3)
        def _():
            start(ex_a)

        for lane0, lanes in tiles:
            acc = dot(p1[pl.ds(row0, TILE), :], first_w[0:PACK, pl.ds(lane0, lanes)])
            for di in (1, 2):
                acc = acc + dot(
                    p1[pl.ds(row0 + REST * di, TILE), :], first_w[PACK * di : PACK * di + PACK, pl.ds(lane0, lanes)]
                )
            value = jnp.maximum(acc + bias_row(b_2a, lane0, lanes), 0.0)
            put3(x_a, row0 + REST, lane0, MIDDLE, value, REST)
        return carry

    lax.fori_loop(0, IN_CH, enc2a, 0)
    finish(copies_2b)

    def conv640(src, row0, base, lane0, lanes):
        acc = None
        for di in range(3):
            weights = jnp.concatenate(
                [
                    ring[base + MIDDLE * (t // 2) : base + MIDDLE * (t // 2) + MIDDLE, pl.ds(MIDDLE * (t % 2) + lane0, lanes)]
                    for t in range(3 * di, 3 * di + 3)
                ],
                axis=0,
            )
            part = dot(src[pl.ds(row0 + REST * di, TILE), :], weights)
            acc = part if acc is None else acc + part
        return acc

    def enc2b(i, carry):
        block = i + 1 - 2 * (i % 2)
        row0 = pl.multiple_of(block * TILE, TILE)

        @pl.when(i == 1)
        def _():
            finish(ex_a)
            halo(x_a, REST, MIDDLE, N16)

        @pl.when(i == 3)
        def _():
            start(ex_m1)
            start(ex_s)

        for lane0, lanes in tiles:
            value = jnp.maximum(conv640(x_a, row0, 0, lane0, lanes) + bias_row(b_2b, lane0, lanes), 0.0)
            put3(x_s, row0 + REST, lane0, MIDDLE, value, REST)
            put3(m_1, pl.multiple_of(block * REST + STRIP_ROWS, STRIP_ROWS), lane0, MIDDLE, pooled(value, REST, pool_buf), STRIP_ROWS)
        return carry

    lax.fori_loop(0, IN_CH, enc2b, 0)
    start(copies_mb[2:IN_CH])

    acc_ref[...] = jnp.zeros_like(acc_ref)
    finish(copies_ma)

    def mid_a(t, carry):
        di = (t + 1) % 2 + 2 * (t // 2) - t // 2

        @pl.when(t == 1)
        def _():
            finish(ex_m1)
            halo(m_1, STRIP_ROWS, MIDDLE, STRIPS)

        base = pl.multiple_of(N3200 + MIDDLE3 * t, LANES)
        lhs_row = pl.multiple_of(STRIP_ROWS * di, STRIP_ROWS)
        for lane0 in range(0, DEEP, TILE):
            acc_ref[:, pl.ds(lane0, TILE)] += dot(
                m_1[pl.ds(lhs_row, TILE), :], ring[pl.ds(base, MIDDLE3), pl.ds(lane0, TILE)]
            )
        return carry

    lax.fori_loop(0, 3, mid_a, 0)
    start(copies_mb[IN_CH:TAPS])
    for lane0 in range(0, DEEP, TILE):
        value = jnp.maximum(acc_ref[:, pl.ds(lane0, TILE)] + bias_row(b_ma, lane0, TILE), 0.0)
        put3(m_2, STRIP_ROWS, lane0, DEEP, value, STRIP_ROWS)
    start(ex_m2)
    acc_ref[...] = jnp.zeros_like(acc_ref)

    def mid_b(k, carry):
        t = k // 3
        di = (t + 1) % 2 + 2 * (t // 2) - t // 2

        for j in range(TAPS):
            @pl.when(k == j)
            def _(j=j):
                copies_mb[j].wait()

        @pl.when(k == 3)
        def _():
            start(copies_u2)
            finish(ex_m2)
            halo(m_2, STRIP_ROWS, DEEP, STRIPS)

        @pl.when(k == FIVE)
        def _():
            start(copies_d2a[0:IN_CH])

        @pl.when(k == STRIPS)
        def _():
            start(copies_d2a[IN_CH:TAPS])

        base = pl.multiple_of(mb_row(k), LANES)
        lhs_row = pl.multiple_of(STRIP_ROWS * di, STRIP_ROWS)
        lhs_lane = pl.multiple_of(DEEP * (k % 3), DEEP)
        for lane0 in range(0, DEEP, TILE):
            acc_ref[:, pl.ds(lane0, TILE)] += dot(
                m_2[pl.ds(lhs_row, TILE), pl.ds(lhs_lane, DEEP)], ring[pl.ds(base, DEEP), pl.ds(lane0, TILE)]
            )
        return carry

    lax.fori_loop(0, TAPS, mid_b, 0)
    for lane0 in range(0, DEEP, TILE):
        value = jnp.maximum(acc_ref[:, pl.ds(lane0, TILE)] + bias_row(b_mb, lane0, TILE), 0.0)
        m_o[:, pl.ds(lane0, TILE)] = value.astype(BF16)

    finish(copies_u2)
    for p in range(2):
        for q in range(2):
            for lane0, lanes in tiles:
                part = dot(m_o[...], ring[N8960 + DEEP * p : N10240 + DEEP * p, pl.ds(MIDDLE * q + lane0, lanes)])
                for lane in range(0, lanes, LANES):
                    wide[(lane0 + lane) // LANES, pl.ds(q, TILE, stride=2), :] = part[:, lane : lane + LANES]

        def place(i, carry):
            src = pl.multiple_of(REST * i, REST)
            dst = pl.multiple_of(REST * (1 + 2 * i + p), REST)
            for lane0 in range(0, MIDDLE, LANES):
                put3(x_u, dst, lane0, MIDDLE, wide[lane0 // LANES, pl.ds(src, REST), :], REST)
            return carry

        lax.fori_loop(0, STRIPS, place, 0)
    start(ex_u)
    start(copies_d2b)
    finish(ex_s)
    halo(x_s, REST, MIDDLE, N16)
    finish(copies_d2a)

    def dec2a(i, carry):
        block = i + 1 - 2 * (i % 2)
        row0 = pl.multiple_of(block * TILE, TILE)

        @pl.when(i == 1)
        def _():
            finish(ex_u)
            halo(x_u, REST, MIDDLE, N16)

        @pl.when(i == 3)
        def _():
            start(ex_b)

        for lane0, lanes in tiles:
            acc = None
            for tap in range(TAPS):
                rows = pl.ds(row0 + REST * (tap // 3), TILE)
                cols = pl.ds(MIDDLE * (tap % 3), MIDDLE)
                lhs = jnp.concatenate([x_u[rows, cols], x_s[rows, cols]], axis=1)
                base = DEEP * (tap // 2)
                part = dot(lhs, ring[base : base + DEEP, pl.ds(MIDDLE * (tap % 2) + lane0, lanes)])
                acc = part if acc is None else acc + part
            value = jnp.maximum(acc + bias_row(b_d2a, lane0, lanes), 0.0)
            put3(x_a, row0 + REST, lane0, MIDDLE, value, REST)
        return carry

    lax.fori_loop(0, IN_CH, dec2a, 0)
    finish(copies_d2b)

    def dec2b(i, carry):
        block = i + 1 - 2 * (i % 2)
        row0 = pl.multiple_of(block * TILE, TILE)

        @pl.when(i == 1)
        def _():
            finish(ex_b)
            halo(x_a, REST, MIDDLE, N16)

        @pl.when(i == 3)
        def _():
            start(ex_d)

        for lane0, lanes in tiles:
            value = jnp.maximum(conv640(x_a, row0, N6400, lane0, lanes) + bias_row(b_d2b, lane0, lanes), 0.0)
            d_2[pl.ds(row0 + REST, TILE), pl.ds(lane0, lanes)] = value.astype(BF16)
        return carry

    lax.fori_loop(0, IN_CH, dec2b, 0)
    finish(ex_d)
    halo(d_2, REST, MIDDLE, N16, plain=True)
    result = pltpu.make_async_copy(d_2, out, sem_out)
    result.start()
    result.wait()


def dec1_kernel(
    d_2, s1, w_u1, w_d1a, w_d1b, b_d1a, b_d1b, w_head, b_head, out,
    x_u, x_s, x_d, y_rest, st_u, st_a, st_b, wu_main, wu_rest, wa_main, wa_rest, wb_main, wb_rest, wide, result,
    sem, send_sem, recv_sem,
):
    strip = strip_index()
    row = lax.axis_index("row")
    col = lax.axis_index("col")
    copy_u = pltpu.make_async_copy(w_u1, st_u, sem.at[0])
    copy_a = pltpu.make_async_copy(w_d1a, st_a, sem.at[1])
    copy_s = pltpu.make_async_copy(s1, x_s, sem.at[2])
    copy_b = pltpu.make_async_copy(w_d1b, st_b, sem.at[3])
    for copy in (copy_u, copy_a, copy_s, copy_b):
        copy.start()
    barrier = enter_barrier()

    copy_u.wait()
    for tap in range(IN_CH):
        wu_main[MIDDLE * tap : MIDDLE * tap + MIDDLE, :] = st_u[BASE * tap : BASE * tap + TILE, :].T
    wu_rest[...] = jnp.concatenate([st_u[BASE * tap + TILE : BASE * tap + BASE, :] for tap in range(IN_CH)], axis=0).T

    def up1(i, carry):
        row0 = pl.multiple_of(i * BASE_PAD, LANES)
        lhs = d_2[pl.ds(row0, BASE_PAD), :]
        rest = dot(lhs, wu_rest[...])
        for p in range(2):
            part = rest[:, LANES * p : LANES * p + LANES]
            buf = wide.at[p]
            buf[2, pl.ds(0, BASE_PAD, stride=2), :] = low_lanes(part)
            buf[2, pl.ds(1, BASE_PAD, stride=2), :] = low_lanes(pltpu.roll(part, REST, axis=1))
            for q in range(2):
                tap = 2 * p + q
                main = dot(lhs, wu_main[MIDDLE * tap : MIDDLE * tap + MIDDLE, :])
                buf[0, pl.ds(q, BASE_PAD, stride=2), :] = main[:, 0:LANES]
                buf[1, pl.ds(q, BASE_PAD, stride=2), :] = main[:, LANES:TILE]
            for r in range(SIX):
                main = jnp.concatenate([buf[0, LANES * r : LANES * r + LANES, :], buf[1, LANES * r : LANES * r + LANES, :]], axis=1)
                put3_320(
                    x_u, pl.multiple_of((N12 * i + 2 * r + p) * LANES, LANES), main, buf[2, LANES * r : LANES * r + LANES, :], LANES
                )
        return carry

    lax.fori_loop(0, 3, up1, 0)

    copy_a.wait()
    pack_transposed(st_a, wa_main, wa_rest)
    copy_s.wait()

    def rest_a(i, carry):
        for j in range(SIX):
            rows = pl.ds(pl.multiple_of(i * N1536 + TILE * j, TILE), TILE)
            y_rest[rows, :] = dot(x_u[rows, :], wa_rest[0:PACK, :]) + dot(x_s[rows, :], wa_rest[PACK:N2048, :])
        return carry

    lax.fori_loop(0, 3, rest_a, 0)

    def conv_a(row0, first_row):
        acc = None
        for di in range(3):
            rows = pl.ds(row0 + LANES * di, TILE)
            for src, ref in enumerate((x_u, x_s)):
                base = N3072 * src + PACK * di
                part = dot(ref[rows, :], wa_main[base : base + PACK, :])
                acc = part if acc is None else acc + part
        main = valid_rows(jnp.maximum(acc + bias_row(b_d1a, 0, TILE), 0.0), first_row, LANES)
        tail = valid_rows(jnp.maximum(rest_sum(y_rest, row0, TILE) + bias_rest(b_d1a), 0.0), first_row, LANES)
        put3_320(x_d, row0, main, low_lanes(tail), LANES)

    def dec1a(i, carry):
        for j in range(IN_CH):
            conv_a(pl.multiple_of(i * PACK + TILE * j, TILE), STRIP_ROWS * strip - 1 + STRIPS * i + 2 * j)
        return carry

    lax.fori_loop(0, IN_CH, dec1a, 0)
    conv_a(N4096, STRIP_ROWS * strip + N31)

    copy_b.wait()
    pack_weights(st_b, wb_main, wb_rest)
    head_bias = jnp.zeros((IN_CH, LANES), F32)
    for channel in range(IN_CH):
        head_bias = jnp.where(lax.broadcasted_iota(jnp.int32, (IN_CH, LANES), 0) == channel, b_head[channel], head_bias)

    def dec1b(i, carry):
        base = pl.multiple_of(i * PACK, PACK)

        def rest(j):
            y_rest[TILE * j : TILE * j + TILE, :] = dot(x_d[pl.ds(base + TILE * j, TILE), :], wb_rest[...])

        rest(0)
        for j in range(IN_CH):
            rest(j + 1)
            acc = dot(x_d[pl.ds(base + TILE * j, TILE), :], wb_main[0:PACK, :])
            acc = acc + dot(x_d[pl.ds(base + TILE * j + LANES, TILE), :], wb_main[PACK:N2048, :])
            acc = acc + dot(x_d[pl.ds(base + TILE * j + TILE, TILE), :], wb_main[N2048:N3072, :])
            main = jnp.maximum(acc + bias_row(b_d1b, 0, TILE), 0.0).astype(BF16)
            tail = jnp.maximum(rest_sum(y_rest, TILE * j, TILE) + bias_rest(b_d1b), 0.0).astype(BF16)
            hidden = jnp.concatenate([main, tail[:, 0:REST]], axis=1)
            head = lax.dot_general(w_head[...], hidden, (((1,), (1,)), ((), ())), preferred_element_type=F32)
            for r in range(2):
                line = head[:, LANES * r : LANES * r + LANES] + head_bias
                result[0, STRIPS * i + 2 * j + r] = line[:, 0:REST]
                result[1, STRIPS * i + 2 * j + r] = line[:, REST:LANES]
        return carry

    lax.fori_loop(0, IN_CH, dec1b, 0)

    pl.semaphore_wait(barrier, STRIPS)
    pushes = []
    for side in range(2):
        tile_row = strip // 2
        pushes.append(
            Push(
                result.at[side],
                out.at[pl.ds(STRIP_ROWS * (strip % 2), STRIP_ROWS)],
                send_sem.at[side],
                recv_sem.at[strip % 2],
                (lax.axis_index("data"), side, tile_row),
                (tile_row == row) & (col == side),
            )
        )
    for push in pushes:
        push.start()
    for push in pushes:
        push.wait_send()
    for half in range(2):
        Push(
            result.at[0], out.at[pl.ds(STRIP_ROWS * half, STRIP_ROWS)], send_sem.at[0], recv_sem.at[half], strip_device(strip), strip < 0
        ).wait_recv()


def solution(mesh):
    tile_spec = P(("data", "row"), "col", None)

    def body(image_tile, *params):
        (w_enc1a, b_enc1a, w_enc1b, b_enc1b, w_enc2a, b_enc2a, w_enc2b, b_enc2b,
         w_mid_a, b_mid_a, w_mid_b, b_mid_b, w_up2, w_dec2a, b_dec2a, w_dec2b, b_dec2b,
         w_up1, w_dec1a, b_dec1a, w_dec1b, b_dec1b, w_head, b_head) = params
        def flat(weight):
            return weight.reshape(-1, weight.shape[-1])

        vmem = pl.BlockSpec(memory_space=pltpu.VMEM)
        hbm = pl.BlockSpec(memory_space=pl.ANY)
        dma = pltpu.SemaphoreType.DMA
        s1, p1 = pl.pallas_call(
            enc1_kernel,
            grid=(3,),
            out_shape=(jax.ShapeDtypeStruct((N4608, PACK), BF16), jax.ShapeDtypeStruct((N1152, PACK), BF16)),
            in_specs=[vmem, vmem, vmem, hbm, vmem],
            out_specs=(pl.BlockSpec((N1536, PACK), lambda i: (i, 0)), pl.BlockSpec((BASE_PAD, PACK), lambda i: (i, 0))),
            scratch_shapes=[
                pltpu.VMEM((2, N40, IN_CH, REST), BF16),
                pltpu.VMEM((N42, STRIP_ROWS, LANES), BF16),
                pltpu.VMEM((N96, BASE_PAD), BF16),
                pltpu.VMEM((N2880, BASE), BF16),
                pltpu.VMEM((N5120, PACK), BF16),
                pltpu.VMEM((N1792, TILE), F32),
                pltpu.VMEM((N3072, TILE), BF16),
                pltpu.VMEM((PACK, TILE), BF16),
                pltpu.VMEM((LANES, LANES), F32),
                dma, dma((IN_CH,)), dma((2, 2)),
            ],
            compiler_params=pltpu.CompilerParams(
                vmem_limit_bytes=VMEM_LIMIT, collective_id=1, has_side_effects=True, dimension_semantics=("arbitrary",)
            ),
            name="enc1",
        )(image_tile.transpose(0, 2, 1), w_enc1a, b_enc1a, flat(w_enc1b), b_enc1b)

        d2 = pl.pallas_call(
            mid_kernel,
            out_shape=jax.ShapeDtypeStruct((N1152, MIDDLE), BF16),
            in_specs=[vmem] + [hbm] * LAST_STRIP + [vmem] * SIX,
            out_specs=hbm,
            scratch_shapes=[
                pltpu.VMEM((N3072, MIDDLE), BF16),
                pltpu.VMEM((RING_ROWS, DEEP), BF16),
                pltpu.VMEM((N1152, MIDDLE3), BF16),
                pltpu.VMEM((N1152, MIDDLE3), BF16),
                pltpu.VMEM((N1152, MIDDLE3), BF16),
                pltpu.VMEM((BASE, MIDDLE3), BF16),
                pltpu.VMEM((BASE, N3840), BF16),
                pltpu.VMEM((TILE, DEEP), BF16),
                pltpu.VMEM((N1152, MIDDLE), BF16),
                pltpu.VMEM((TILE, DEEP), F32),
                pltpu.VMEM((FIVE, N512, LANES), F32),
                pltpu.VMEM((LANES, LANES), F32),
                dma((N18,)), dma((TAPS,)), dma((3,)), dma((TAPS,)), dma((IN_CH,)), dma((TAPS,)), dma((TAPS,)), dma,
                dma((LAST_STRIP, 2)), dma((LAST_STRIP, 2)),
            ],
            compiler_params=pltpu.CompilerParams(
                vmem_limit_bytes=VMEM_LIMIT, collective_id=0, has_side_effects=True
            ),
            name="mid",
        )(
            p1, flat(w_enc2a), flat(w_enc2b), flat(w_mid_a), flat(w_mid_b), flat(w_up2), flat(w_dec2a), flat(w_dec2b),
            b_enc2a, b_enc2b, b_mid_a, b_mid_b, b_dec2a, b_dec2b,
        )

        def turned(weight):
            return weight.transpose(0, 1, 3, 2).reshape(-1, weight.shape[2])

        y = pl.pallas_call(
            dec1_kernel,
            out_shape=jax.ShapeDtypeStruct((REST, IN_CH, REST), F32),
            in_specs=[vmem] + [hbm] * IN_CH + [vmem] * 3 + [pl.BlockSpec(memory_space=pltpu.SMEM)],
            out_specs=hbm,
            scratch_shapes=[
                pltpu.VMEM((N4608, PACK), BF16),
                pltpu.VMEM((N4608, PACK), BF16),
                pltpu.VMEM((N4352, PACK), BF16),
                pltpu.VMEM((N4608, TILE), F32),
                pltpu.VMEM((DEEP, MIDDLE), BF16),
                pltpu.VMEM((N2880, MIDDLE), BF16),
                pltpu.VMEM((N2880, BASE), BF16),
                pltpu.VMEM((N2560, TILE), BF16),
                pltpu.VMEM((MIDDLE, TILE), BF16),
                pltpu.VMEM((N6144, TILE), BF16),
                pltpu.VMEM((N2048, TILE), BF16),
                pltpu.VMEM((N3072, TILE), BF16),
                pltpu.VMEM((PACK, TILE), BF16),
                pltpu.VMEM((2, 3, REST_AT, LANES), F32),
                pltpu.VMEM((2, STRIP_ROWS, IN_CH, REST), F32),
                dma((IN_CH,)), dma((2,)), dma((2,)),
            ],
            compiler_params=pltpu.CompilerParams(vmem_limit_bytes=VMEM_LIMIT, collective_id=2, has_side_effects=True),
            name="dec1",
        )(d2, s1, turned(w_up1), turned(w_dec1a), flat(w_dec1b), b_dec1a, b_dec1b, w_head.T, b_head)
        return y.transpose(0, 2, 1)

    def program(image, *params):
        mapped = jax.shard_map(
            body, mesh=mesh, in_specs=(tile_spec,) + (P(),) * len(params), out_specs=tile_spec, check_vma=False
        )
        return mapped(image, *params)

    return program
```

time: 208 us -> 167 us (0.80)
  blocking collectives: 27.5 us -> 0 us
  local copies, waits for them, and re-layouts: 23.5 us -> 1.57 us
  Pallas kernels: 156 us -> 165 us
    all_gather x2 -> x0, blocking collectives: 27.5 us -> none  [the longest x1 15.1 us: body(): lax.all_gather(image_tile.transpose(2, 0, 1), ('col', 'row'), axis=0)]
    unnamed x44 -> x1, local copies, waits for them, and re-layouts: 13.3 us -> 1.57 us
    pallas_call x3, Pallas kernels: 156 us -> 165 us  [the longest x1 79.5 us: body(): pl.pallas_call(mid_kernel, out_shape=jax.ShapeDtypeStruct((N1152, MIDDLE)...]
    broadcast_in_dim x12 -> x0, local copies, waits for them, and re-layouts: 6.45 us -> none  [the longest x4 2.26 us: wide_bias(): return jnp.pad(bias, (0, 384 - bias.shape[0]))[None]]
where the time goes in v2:
time: 167 us; the launch traced here: 166 us
  Pallas kernels  165 us (99%)
    pallas_call x1, Pallas kernels, body(): pl.pallas_call(mid_kernel, out_shape=jax.ShapeDtypeStruct((N1152, MIDDLE)...  79.5 us
    pallas_call x1, Pallas kernels, body(): pl.pallas_call(dec1_kernel, out_shape=jax.ShapeDtypeStruct((REST, IN_CH,...  55.7 us
    pallas_call x1, Pallas kernels, body(): pl.pallas_call(enc1_kernel, grid=(3,), out_shape=(jax.ShapeDtypeStruct((N...  29.6 us

profile of v2, /device:TPU:0, one launch (start us, length us, event | category | flops | bytes accessed | tf_op | source)
XLA Modules:
  0.0 166.5 jit_solution(6250545395701293678)
XLA Ops:
  0.0 29.6 %enc1.1 = (bf16[4608,1024]{1,0:T(8,128)(2,1)}, bf16[1152,1024]{1,0:T(8,128)(2,1)}) custom-call(bf16[64,4,64]{2,1,0:T(4,128)(2,1)} %bitcast.30, bf16[3,3,4,320]{3,2,1,0:T(4,128)(2,1)} %w_a.1, f32[320]{0:T(512)} %b_a.1, bf16[2880,320]{1,0:T(8,128)(2,1)} %bitcast.26, f32[320]{0:T(512)} %b_b.1), custom_call_target="tpu_custom_call" | custom-call | tf_op jit(solution)/shard_map/enc1/pallas_call | solution.py:767
  29.6 79.5 %mid.1.d_2 = bf16[1152,640]{1,0:T(8,128)(2,1)} custom-call(bf16[1152,1024]{1,0:T(8,128)(2,1)} %get-tuple-element.7.p1, bf16[2880,640]{1,0:T(8,128)(2,1)} %bitcast.25, bf16[5760,640]{1,0:T(8,128)(2,1)} %bitcast.21, bf16[5760,1280]{1,0:T(8,128)(2,1)} %bitcast.19, bf16[11520,1280]{1,0:T(8,128)(2,1)} %bitcast.18, bf16[5120,640]{1,0:T(8,128)(2,1)} %bitcast.23, ...), custom_call_target="tpu_custom_call" | custom-call | tf_op jit(solution)/shard_map/mid/pallas_call | solution.py:791
  109.1 55.7 %dec1.1 = f32[64,4,64]{2,1,0:T(4,128)} custom-call(bf16[1152,640]{1,0:T(8,128)(2,1)} %mid.1.d_2, bf16[4608,1024]{1,0:T(8,128)(2,1)} %get-tuple-element.8.s1, bf16[1280,640]{1,0:T(8,128)(2,1)} %bitcast.28, bf16[2880,640]{1,0:T(8,128)(2,1)} %bitcast.24, bf16[2880,320]{1,0:T(8,128)(2,1)} %bitcast.27, f32[320]{0:T(512)} %b_d1a.1, f32[320]{0:T(512)} %b_d1b.1, ...), custom_call_target="tpu_custom_call" | custom-call | tf_op jit(solution)/shard_map/dec1/pallas_call | solution.py:824
  164.9 1.6 copy.27

commit v3 on v2

--- a/solution.py
+++ b/solution.py
@@ -299,14 +299,14 @@
     base = pl.multiple_of(step * N1536, N512)
 
     def rest(j):
-        y_rest[TILE * j : TILE * j + TILE, :] = dot(x_a[pl.ds(base + TILE * j, TILE), :], w_rest[...])
+        y_rest[TILE * j : TILE * j + TILE, :] = dot(x_a[pl.ds(base + TILE * j, TILE), 0:PACK], w_rest[...])
 
     rest(0)
     for j in range(SIX):
         rest(j + 1)
-        acc = dot(x_a[pl.ds(base + TILE * j, TILE), :], w_main[0:PACK, :])
-        acc = acc + dot(x_a[pl.ds(base + TILE * j + LANES, TILE), :], w_main[PACK:N2048, :])
-        acc = acc + dot(x_a[pl.ds(base + TILE * j + TILE, TILE), :], w_main[N2048:N3072, :])
+        acc = dot(x_a[pl.ds(base + TILE * j, TILE), 0:PACK], w_main[0:PACK, :])
+        acc = acc + dot(x_a[pl.ds(base + TILE * j + LANES, TILE), 0:PACK], w_main[PACK:N2048, :])
+        acc = acc + dot(x_a[pl.ds(base + TILE * j + TILE, TILE), 0:PACK], w_main[N2048:N3072, :])
         first_row = STRIP_ROWS * strip - 2 + N12 * step + 2 * j
         main = valid_rows(jnp.maximum(acc + bias_row(b_b, 0, TILE), 0.0), first_row, LANES)
         tail = jnp.maximum(rest_sum(y_rest, TILE * j, TILE) + bias_rest(b_b), 0.0)
@@ -431,10 +431,10 @@
             start(ex_a)
 
         for lane0, lanes in tiles:
-            acc = dot(p1[pl.ds(row0, TILE), :], first_w[0:PACK, pl.ds(lane0, lanes)])
+            acc = dot(p1[pl.ds(row0, TILE), 0:PACK], first_w[0:PACK, pl.ds(lane0, lanes)])
             for di in (1, 2):
                 acc = acc + dot(
-                    p1[pl.ds(row0 + REST * di, TILE), :], first_w[PACK * di : PACK * di + PACK, pl.ds(lane0, lanes)]
+                    p1[pl.ds(row0 + REST * di, TILE), 0:PACK], first_w[PACK * di : PACK * di + PACK, pl.ds(lane0, lanes)]
                 )
             value = jnp.maximum(acc + bias_row(b_2a, lane0, lanes), 0.0)
             put3(x_a, row0 + REST, lane0, MIDDLE, value, REST)
@@ -672,7 +672,9 @@
     def rest_a(i, carry):
         for j in range(SIX):
             rows = pl.ds(pl.multiple_of(i * N1536 + TILE * j, TILE), TILE)
-            y_rest[rows, :] = dot(x_u[rows, :], wa_rest[0:PACK, :]) + dot(x_s[rows, :], wa_rest[PACK:N2048, :])
+            y_rest[rows, :] = dot(x_u[rows, 0:PACK], wa_rest[0:PACK, :]) + dot(
+                x_s[rows, 0:PACK], wa_rest[PACK:N2048, :]
+            )
         return carry
 
     lax.fori_loop(0, 3, rest_a, 0)
@@ -683,7 +685,7 @@
             rows = pl.ds(row0 + LANES * di, TILE)
             for src, ref in enumerate((x_u, x_s)):
                 base = N3072 * src + PACK * di
-                part = dot(ref[rows, :], wa_main[base : base + PACK, :])
+                part = dot(ref[rows, 0:PACK], wa_main[base : base + PACK, :])
                 acc = part if acc is None else acc + part
         main = valid_rows(jnp.maximum(acc + bias_row(b_d1a, 0, TILE), 0.0), first_row, LANES)
         tail = valid_rows(jnp.maximum(rest_sum(y_rest, row0, TILE) + bias_rest(b_d1a), 0.0), first_row, LANES)
@@ -707,14 +709,14 @@
         base = pl.multiple_of(i * PACK, PACK)
 
         def rest(j):
-            y_rest[TILE * j : TILE * j + TILE, :] = dot(x_d[pl.ds(base + TILE * j, TILE), :], wb_rest[...])
+            y_rest[TILE * j : TILE * j + TILE, :] = dot(x_d[pl.ds(base + TILE * j, TILE), 0:PACK], wb_rest[...])
 
         rest(0)
         for j in range(IN_CH):
             rest(j + 1)
-            acc = dot(x_d[pl.ds(base + TILE * j, TILE), :], wb_main[0:PACK, :])
-            acc = acc + dot(x_d[pl.ds(base + TILE * j + LANES, TILE), :], wb_main[PACK:N2048, :])
-            acc = acc + dot(x_d[pl.ds(base + TILE * j + TILE, TILE), :], wb_main[N2048:N3072, :])
+            acc = dot(x_d[pl.ds(base + TILE * j, TILE), 0:PACK], wb_main[0:PACK, :])
+            acc = acc + dot(x_d[pl.ds(base + TILE * j + LANES, TILE), 0:PACK], wb_main[PACK:N2048, :])
+            acc = acc + dot(x_d[pl.ds(base + TILE * j + TILE, TILE), 0:PACK], wb_main[N2048:N3072, :])
             main = jnp.maximum(acc + bias_row(b_d1b, 0, TILE), 0.0).astype(BF16)
             tail = jnp.maximum(rest_sum(y_rest, TILE * j, TILE) + bias_rest(b_d1b), 0.0).astype(BF16)
             hidden = jnp.concatenate([main, tail[:, 0:REST]], axis=1)
@@ -767,15 +769,15 @@
         s1, p1 = pl.pallas_call(
             enc1_kernel,
             grid=(3,),
-            out_shape=(jax.ShapeDtypeStruct((N4608, PACK), BF16), jax.ShapeDtypeStruct((N1152, PACK), BF16)),
+            out_shape=(jax.ShapeDtypeStruct((N4608, N1152), BF16), jax.ShapeDtypeStruct((N1152, N1152), BF16)),
             in_specs=[vmem, vmem, vmem, hbm, vmem],
-            out_specs=(pl.BlockSpec((N1536, PACK), lambda i: (i, 0)), pl.BlockSpec((BASE_PAD, PACK), lambda i: (i, 0))),
+            out_specs=(pl.BlockSpec((N1536, N1152), lambda i: (i, 0)), pl.BlockSpec((BASE_PAD, N1152), lambda i: (i, 0))),
             scratch_shapes=[
                 pltpu.VMEM((2, N40, IN_CH, REST), BF16),
                 pltpu.VMEM((N42, STRIP_ROWS, LANES), BF16),
                 pltpu.VMEM((N96, BASE_PAD), BF16),
                 pltpu.VMEM((N2880, BASE), BF16),
-                pltpu.VMEM((N5120, PACK), BF16),
+                pltpu.VMEM((N5120, N1152), BF16),
                 pltpu.VMEM((N1792, TILE), F32),
                 pltpu.VMEM((N3072, TILE), BF16),
                 pltpu.VMEM((PACK, TILE), BF16),
@@ -827,9 +829,9 @@
             in_specs=[vmem] + [hbm] * IN_CH + [vmem] * 3 + [pl.BlockSpec(memory_space=pltpu.SMEM)],
             out_specs=hbm,
             scratch_shapes=[
-                pltpu.VMEM((N4608, PACK), BF16),
-                pltpu.VMEM((N4608, PACK), BF16),
-                pltpu.VMEM((N4352, PACK), BF16),
+                pltpu.VMEM((N4608, N1152), BF16),
+                pltpu.VMEM((N4608, N1152), BF16),
+                pltpu.VMEM((N4352, N1152), BF16),
                 pltpu.VMEM((N4608, TILE), F32),
                 pltpu.VMEM((DEEP, MIDDLE), BF16),
                 pltpu.VMEM((N2880, MIDDLE), BF16),

time: 167 us -> 164 us (0.982)
  Pallas kernels: 165 us -> 163 us
where the time goes in v3:
time: 164 us
  Pallas kernels  163 us (99%)
    pallas_call x1, Pallas kernels, body(): pl.pallas_call(mid_kernel, out_shape=jax.ShapeDtypeStruct((N1152, MIDDLE)...  79.2 us
    pallas_call x1, Pallas kernels, body(): pl.pallas_call(dec1_kernel, out_shape=jax.ShapeDtypeStruct((REST, IN_CH,...  55 us
    pallas_call x1, Pallas kernels, body(): pl.pallas_call(enc1_kernel, grid=(3,), out_shape=(jax.ShapeDtypeStruct((N...  28.4 us

profile of v3, /device:TPU:0, one launch (start us, length us, event | category | flops | bytes accessed | tf_op | source)
XLA Modules:
  0.0 164.3 jit_solution(14383953094812498984)
XLA Ops:
  0.0 28.4 %enc1.1 = (bf16[4608,1152]{1,0:T(8,128)(2,1)}, bf16[1152,1152]{1,0:T(8,128)(2,1)}) custom-call(bf16[64,4,64]{2,1,0:T(4,128)(2,1)} %bitcast.30, bf16[3,3,4,320]{3,2,1,0:T(4,128)(2,1)} %w_a.1, f32[320]{0:T(512)} %b_a.1, bf16[2880,320]{1,0:T(8,128)(2,1)} %bitcast.27, f32[320]{0:T(512)} %b_b.1), custom_call_target="tpu_custom_call" | custom-call | tf_op jit(solution)/shard_map/enc1/pallas_call | solution.py:769
  28.4 79.2 %mid.1.d_2 = bf16[1152,640]{1,0:T(8,128)(2,1)} custom-call(bf16[1152,1152]{1,0:T(8,128)(2,1)} %get-tuple-element.7.p1, bf16[2880,640]{1,0:T(8,128)(2,1)} %bitcast.25, bf16[5760,640]{1,0:T(8,128)(2,1)} %bitcast.21, bf16[5760,1280]{1,0:T(8,128)(2,1)} %bitcast.19, bf16[11520,1280]{1,0:T(8,128)(2,1)} %bitcast.18, bf16[5120,640]{1,0:T(8,128)(2,1)} %bitcast.23, ...), custom_call_target="tpu_custom_call" | custom-call | tf_op jit(solution)/shard_map/mid/pallas_call | solution.py:793
  107.6 55.0 %dec1.1 = f32[64,4,64]{2,1,0:T(4,128)} custom-call(bf16[1152,640]{1,0:T(8,128)(2,1)} %mid.1.d_2, bf16[4608,1152]{1,0:T(8,128)(2,1)} %get-tuple-element.8.s1, bf16[1280,640]{1,0:T(8,128)(2,1)} %bitcast.28, bf16[2880,640]{1,0:T(8,128)(2,1)} %bitcast.24, bf16[2880,320]{1,0:T(8,128)(2,1)} %bitcast.26, f32[320]{0:T(512)} %b_d1a.1, f32[320]{0:T(512)} %b_d1b.1, ...), custom_call_target="tpu_custom_call" | custom-call | tf_op jit(solution)/shard_map/dec1/pallas_call | solution.py:826
  162.7 1.6 copy.27

commit v4 on v3

--- a/solution.py
+++ b/solution.py
@@ -17,6 +17,7 @@
 N16 = 16
 N18 = 18
 N28 = 28
+N30 = 30
 N31 = 31
 STRIP_ROWS = 32
 N36 = 36
@@ -395,14 +396,18 @@
         )
         for k in range(TAPS)
     ]
-    copies_u2 = tap_copies(w_u2, DEEP, N8960, sem_u2)
+    copies_u2 = [
+        pltpu.make_async_copy(
+            w_u2.at[pl.ds(DEEP * tap, DEEP), :],
+            first_w.at[pl.ds(DEEP * tap, DEEP), :] if tap < 2 else ring.at[pl.ds(N8960, DEEP), pl.ds(MIDDLE * (tap - 2), MIDDLE)],
+            sem_u2.at[tap],
+        )
+        for tap in range(IN_CH)
+    ]
     copies_d2a = tap_copies(w_d2a, DEEP, 0, sem_d2a)
     copies_d2b = tap_copies(w_d2b, MIDDLE, N6400, sem_d2b)
 
     start(copies_2a)
-    start(copies_2b)
-    start(copies_ma)
-    start(copies_mb[0:2])
 
     barrier = pltpu.get_barrier_semaphore()
     for device in (prev_dev, next_dev):
@@ -412,6 +417,8 @@
     for di in range(3):
         first_w[PACK * di + PACK_USED : PACK * di + PACK, :] = jnp.zeros((REST, MIDDLE), BF16)
     finish(copies_2a)
+    start(copies_2b)
+    start(copies_ma)
 
     ex_a = exchange(x_a, REST, MIDDLE, MIDDLE, N16, 0)
     ex_s = exchange(x_s, REST, MIDDLE, MIDDLE, N16, 1)
@@ -442,6 +449,8 @@
 
     lax.fori_loop(0, IN_CH, enc2a, 0)
     finish(copies_2b)
+    start(copies_mb[0:2])
+    start(copies_u2[0:2])
 
     def conv640(src, row0, base, lane0, lanes):
         acc = None
@@ -488,8 +497,13 @@
 
         @pl.when(t == 1)
         def _():
+            start(copies_mb[IN_CH:SIX])
             finish(ex_m1)
             halo(m_1, STRIP_ROWS, MIDDLE, STRIPS)
+
+        @pl.when(t == 2)
+        def _():
+            start(copies_mb[SIX:LAST_STRIP])
 
         base = pl.multiple_of(N3200 + MIDDLE3 * t, LANES)
         lhs_row = pl.multiple_of(STRIP_ROWS * di, STRIP_ROWS)
@@ -500,7 +514,7 @@
         return carry
 
     lax.fori_loop(0, 3, mid_a, 0)
-    start(copies_mb[IN_CH:TAPS])
+    start(copies_mb[LAST_STRIP:TAPS])
     for lane0 in range(0, DEEP, TILE):
         value = jnp.maximum(acc_ref[:, pl.ds(lane0, TILE)] + bias_row(b_ma, lane0, TILE), 0.0)
         put3(m_2, STRIP_ROWS, lane0, DEEP, value, STRIP_ROWS)
@@ -518,7 +532,7 @@
 
         @pl.when(k == 3)
         def _():
-            start(copies_u2)
+            start(copies_u2[2:IN_CH])
             finish(ex_m2)
             halo(m_2, STRIP_ROWS, DEEP, STRIPS)
 
@@ -526,7 +540,7 @@
         def _():
             start(copies_d2a[0:IN_CH])
 
-        @pl.when(k == STRIPS)
+        @pl.when(k == LAST_STRIP)
         def _():
             start(copies_d2a[IN_CH:TAPS])
 
@@ -548,7 +562,11 @@
     for p in range(2):
         for q in range(2):
             for lane0, lanes in tiles:
-                part = dot(m_o[...], ring[N8960 + DEEP * p : N10240 + DEEP * p, pl.ds(MIDDLE * q + lane0, lanes)])
+                if p == 0:
+                    weights = first_w[DEEP * q : DEEP * q + DEEP, pl.ds(lane0, lanes)]
+                else:
+                    weights = ring[N8960:N10240, pl.ds(MIDDLE * q + lane0, lanes)]
+                part = dot(m_o[...], weights)
                 for lane in range(0, lanes, LANES):
                     wide[(lane0 + lane) // LANES, pl.ds(q, TILE, stride=2), :] = part[:, lane : lane + LANES]
 
@@ -623,7 +641,7 @@
 
 def dec1_kernel(
     d_2, s1, w_u1, w_d1a, w_d1b, b_d1a, b_d1b, w_head, b_head, out,
-    x_u, x_s, x_d, y_rest, st_u, st_a, st_b, wu_main, wu_rest, wa_main, wa_rest, wb_main, wb_rest, wide, result,
+    x_u, x_s, x_d, y_rest, st_u, st_a, st_b, wu_main, wu_rest, wa_main, wa_rest, wb_main, wb_rest, wide, result, pending,
     sem, send_sem, recv_sem,
 ):
     strip = strip_index()
@@ -705,6 +723,15 @@
     for channel in range(IN_CH):
         head_bias = jnp.where(lax.broadcasted_iota(jnp.int32, (IN_CH, LANES), 0) == channel, b_head[channel], head_bias)
 
+    pending[...] = jnp.zeros_like(pending)
+
+    def head(hidden, row0):
+        line = lax.dot_general(w_head[...], hidden, (((1,), (1,)), ((), ())), preferred_element_type=F32)
+        for r in range(2):
+            part = line[:, LANES * r : LANES * r + LANES] + head_bias
+            result[0, row0 + r] = part[:, 0:REST]
+            result[1, row0 + r] = part[:, REST:LANES]
+
     def dec1b(i, carry):
         base = pl.multiple_of(i * PACK, PACK)
 
@@ -712,22 +739,21 @@
             y_rest[TILE * j : TILE * j + TILE, :] = dot(x_d[pl.ds(base + TILE * j, TILE), 0:PACK], wb_rest[...])
 
         rest(0)
+        waiting = pending[...]
         for j in range(IN_CH):
             rest(j + 1)
             acc = dot(x_d[pl.ds(base + TILE * j, TILE), 0:PACK], wb_main[0:PACK, :])
             acc = acc + dot(x_d[pl.ds(base + TILE * j + LANES, TILE), 0:PACK], wb_main[PACK:N2048, :])
             acc = acc + dot(x_d[pl.ds(base + TILE * j + TILE, TILE), 0:PACK], wb_main[N2048:N3072, :])
+            head(waiting, jnp.maximum(STRIPS * i + 2 * j - 2, 0))
             main = jnp.maximum(acc + bias_row(b_d1b, 0, TILE), 0.0).astype(BF16)
             tail = jnp.maximum(rest_sum(y_rest, TILE * j, TILE) + bias_rest(b_d1b), 0.0).astype(BF16)
-            hidden = jnp.concatenate([main, tail[:, 0:REST]], axis=1)
-            head = lax.dot_general(w_head[...], hidden, (((1,), (1,)), ((), ())), preferred_element_type=F32)
-            for r in range(2):
-                line = head[:, LANES * r : LANES * r + LANES] + head_bias
-                result[0, STRIPS * i + 2 * j + r] = line[:, 0:REST]
-                result[1, STRIPS * i + 2 * j + r] = line[:, REST:LANES]
+            waiting = jnp.concatenate([main, tail[:, 0:REST]], axis=1)
+        pending[...] = waiting
         return carry
 
     lax.fori_loop(0, IN_CH, dec1b, 0)
+    head(pending[...], N30)
 
     pl.semaphore_wait(barrier, STRIPS)
     pushes = []
@@ -844,6 +870,7 @@
                 pltpu.VMEM((PACK, TILE), BF16),
                 pltpu.VMEM((2, 3, REST_AT, LANES), F32),
                 pltpu.VMEM((2, STRIP_ROWS, IN_CH, REST), F32),
+                pltpu.VMEM((TILE, BASE), BF16),
                 dma((IN_CH,)), dma((2,)), dma((2,)),
             ],
             compiler_params=pltpu.CompilerParams(vmem_limit_bytes=VMEM_LIMIT, collective_id=2, has_side_effects=True),

time: 164 us -> 147 us (0.90)
  Pallas kernels: 163 us -> 145 us
    pallas_call x1, Pallas kernels: 55 us -> 45.2 us  [body(): pl.pallas_call(dec1_kernel, out_shape=jax.ShapeDtypeStruct((REST, IN_CH,...]
    pallas_call x1, Pallas kernels: 79.2 us -> 71.9 us  [body(): pl.pallas_call(mid_kernel, out_shape=jax.ShapeDtypeStruct((N1152, MIDDLE)...]
where the time goes in v4:
time: 147 us
  Pallas kernels  145 us (99%)
  local copies, waits for them, and re-layouts  1.57 us (1%)
    pallas_call x1, Pallas kernels, body(): pl.pallas_call(mid_kernel, out_shape=jax.ShapeDtypeStruct((N1152, MIDDLE)...  71.9 us
    pallas_call x1, Pallas kernels, body(): pl.pallas_call(dec1_kernel, out_shape=jax.ShapeDtypeStruct((REST, IN_CH,...  45.2 us
    pallas_call x1, Pallas kernels, body(): pl.pallas_call(enc1_kernel, grid=(3,), out_shape=(jax.ShapeDtypeStruct((N...  28.4 us

profile of v4, /device:TPU:0, one launch (start us, length us, event | category | flops | bytes accessed | tf_op | source)
XLA Modules:
  0.0 147.1 jit_solution(12580014744049290610)
XLA Ops:
  0.0 28.4 %enc1.1 = (bf16[4608,1152]{1,0:T(8,128)(2,1)}, bf16[1152,1152]{1,0:T(8,128)(2,1)}) custom-call(bf16[64,4,64]{2,1,0:T(4,128)(2,1)} %bitcast.30, bf16[3,3,4,320]{3,2,1,0:T(4,128)(2,1)} %w_a.1, f32[320]{0:T(512)} %b_a.1, bf16[2880,320]{1,0:T(8,128)(2,1)} %bitcast.27, f32[320]{0:T(512)} %b_b.1), custom_call_target="tpu_custom_call" | custom-call | tf_op jit(solution)/shard_map/enc1/pallas_call | solution.py:795
  28.4 71.9 %mid.1.d_2 = bf16[1152,640]{1,0:T(8,128)(2,1)} custom-call(bf16[1152,1152]{1,0:T(8,128)(2,1)} %get-tuple-element.7.p1, bf16[2880,640]{1,0:T(8,128)(2,1)} %bitcast.25, bf16[5760,640]{1,0:T(8,128)(2,1)} %bitcast.21, bf16[5760,1280]{1,0:T(8,128)(2,1)} %bitcast.19, bf16[11520,1280]{1,0:T(8,128)(2,1)} %bitcast.18, bf16[5120,640]{1,0:T(8,128)(2,1)} %bitcast.23, ...), custom_call_target="tpu_custom_call" | custom-call | tf_op jit(solution)/shard_map/mid/pallas_call | solution.py:819
  100.3 45.2 %dec1.1 = f32[64,4,64]{2,1,0:T(4,128)} custom-call(bf16[1152,640]{1,0:T(8,128)(2,1)} %mid.1.d_2, bf16[4608,1152]{1,0:T(8,128)(2,1)} %get-tuple-element.8.s1, bf16[1280,640]{1,0:T(8,128)(2,1)} %bitcast.28, bf16[2880,640]{1,0:T(8,128)(2,1)} %bitcast.24, bf16[2880,320]{1,0:T(8,128)(2,1)} %bitcast.26, f32[320]{0:T(512)} %b_d1a.1, f32[320]{0:T(512)} %b_d1b.1, ...), custom_call_target="tpu_custom_call" | custom-call | tf_op jit(solution)/shard_map/dec1/pallas_call | solution.py:852
  145.5 1.6 %copy.27 = f32[64,64,4]{1,2,0:T(4,128)} copy(f32[64,64,4]{1,2,0:T(4,128)} %bitcast.29) | data formatting | bytes 131072

commit v5 on v4

--- a/solution.py
+++ b/solution.py
@@ -25,10 +25,14 @@
 N42 = 42
 N60 = 60
 REST = 64
+N80 = 80
 N96 = 96
 N127 = 127
 LANES = 128
+N192 = 192
+N224 = 224
 TILE = 256
+N288 = 288
 BASE = 320
 BASE_PAD = 384
 N512 = 512
@@ -96,13 +100,27 @@
         dst[pl.ds(row0, rows), pl.ds(step * channels + lane0, lanes)] = shifted(value, width, step).astype(BF16)
 
 
-def put3_320(dst, row0, main, rest, width):
+def put3_320(dst, row0, main, rest, width, stage=None):
     rows = main.shape[0]
+    pitch = width + N16
+    planes = [main[:, 0:LANES], main[:, LANES:TILE], rest]
+    for t, plane in enumerate(planes if stage is not None else []):
+        for r in range(rows // width):
+            stage[t, pitch * r + STRIPS : pitch * r + STRIPS + width, :] = plane[width * r : width * r + width]
+
+    def moved(t, step):
+        if step == 1 or stage is None:
+            return shifted(planes[t], width, step)
+        first = LAST_STRIP + step
+        parts = [stage[t, pitch * r + first : pitch * r + first + width, :] for r in range(rows // width)]
+        return jnp.concatenate(parts, axis=0) if len(parts) > 1 else parts[0]
+
     for step in range(3):
-        dst[pl.ds(row0, rows), pl.ds(step * TILE, TILE)] = shifted(main, width, step).astype(BF16)
-    first = shifted(rest, width, 0) + pltpu.roll(rest, REST, axis=1)
+        for t in range(2):
+            dst[pl.ds(row0, rows), pl.ds(step * TILE + LANES * t, LANES)] = moved(t, step).astype(BF16)
+    first = moved(2, 0) + pltpu.roll(rest, REST, axis=1)
     dst[pl.ds(row0, rows), pl.ds(REST_AT, LANES)] = first.astype(BF16)
-    dst[pl.ds(row0, rows), pl.ds(N896, LANES)] = shifted(rest, width, 2).astype(BF16)
+    dst[pl.ds(row0, rows), pl.ds(N896, LANES)] = moved(2, 2).astype(BF16)
 
 
 def low_lanes(value):
@@ -128,18 +146,16 @@
         ref[pl.ds(PACK * group + PACK_USED, REST), :] = jnp.zeros((REST, ref.shape[1]), BF16)
 
 
-def pack_transposed(staged, main_ref, rest_ref):
+def turn_main(staged, main_ref, di, dj):
+    turned = staged[pl.ds(pl.multiple_of(PACK_USED * di + BASE * dj, REST), TILE), :].T
+    for src in range(2):
+        base = N3072 * src + PACK * di
+        main_ref[pl.ds(pl.multiple_of(base + TILE * dj, REST), TILE), :] = turned[BASE * src : BASE * src + TILE]
+        main_ref[pl.ds(pl.multiple_of(base + REST_AT + REST * dj, REST), REST), :] = turned[BASE * src + TILE : BASE * src + BASE]
+
+
+def turn_rest(staged, main_ref, rest_ref):
     for dj in range(3):
-
-        def main_part(di, carry):
-            turned = staged[pl.ds(pl.multiple_of(PACK_USED * di + BASE * dj, REST), TILE), :].T
-            for src in range(2):
-                base = N3072 * src + PACK * di
-                main_ref[pl.ds(pl.multiple_of(base + TILE * dj, REST), TILE), :] = turned[BASE * src : BASE * src + TILE]
-                main_ref[pl.ds(pl.multiple_of(base + REST_AT + REST * dj, REST), REST), :] = turned[BASE * src + TILE : BASE * src + BASE]
-            return carry
-
-        lax.fori_loop(0, 3, main_part, 0)
         parts = [staged[pl.ds(PACK_USED * di + BASE * dj + TILE, REST), :] for di in range(3)] + [jnp.zeros((REST, MIDDLE), BF16)]
         turned = jnp.concatenate(parts, axis=0).T
         for src in range(2):
@@ -216,7 +232,7 @@
 
 def enc1_kernel(
     image, w_a, b_a, w_b, b_b, s1_out, p1_out,
-    halves, planes, w_stem, staged, x_a, y_rest, w_main, w_rest, pool_buf, w_sem, send_sem, recv_sem,
+    halves, planes, w_stem, staged, x_a, y_rest, w_main, w_rest, pool_buf, stage, stage_p, w_sem, send_sem, recv_sem,
 ):
     step = pl.program_id(0)
     strip = strip_index()
@@ -228,6 +244,8 @@
         copy_w = pltpu.make_async_copy(w_b, staged, w_sem)
         copy_w.start()
         barrier = enter_barrier()
+        stage[...] = jnp.zeros_like(stage)
+        stage_p[...] = jnp.zeros_like(stage_p)
 
         for di in range(3):
             taps = []
@@ -292,7 +310,9 @@
                 main = jnp.maximum(acc[:, 0:TILE] + bias_row(b_a, 0, TILE), 0.0)
                 tail = jnp.maximum(acc[:, TILE:BASE_PAD] + bias_rest(b_a), 0.0)
                 first_row = STRIP_ROWS * strip - 3 + r
-                put3_320(x_a, row0, valid_rows(main, first_row, LANES), valid_rows(tail, first_row, LANES), LANES)
+                put3_320(
+                    x_a, row0, valid_rows(main, first_row, LANES), valid_rows(tail, first_row, LANES), LANES, stage.at[j % 2]
+                )
             return carry
 
         lax.fori_loop(0, FIVE, stem, 0)
@@ -312,27 +332,29 @@
         main = valid_rows(jnp.maximum(acc + bias_row(b_b, 0, TILE), 0.0), first_row, LANES)
         tail = jnp.maximum(rest_sum(y_rest, TILE * j, TILE) + bias_rest(b_b), 0.0)
         tail = low_lanes(valid_rows(tail, first_row, LANES))
-        put3_320(s1_out, TILE * j, main, tail, LANES)
-        put3_320(p1_out, REST * j, pooled(main, LANES, pool_buf), pooled(tail, LANES, pool_buf), REST)
+        s1_out[TILE * j : TILE * j + TILE, 0:TILE] = main.astype(BF16)
+        s1_out[TILE * j : TILE * j + TILE, TILE:BASE_PAD] = tail.astype(BF16)
+        put3_320(p1_out, REST * j, pooled(main, LANES, pool_buf.at[j % 2]), pooled(tail, LANES, pool_buf.at[j % 2]), REST, stage_p.at[j % 2])
 
 
 def mid_kernel(
-    p1, w_2a, w_2b, w_ma, w_mb, w_u2, w_d2a, w_d2b, b_2a, b_2b, b_ma, b_mb, b_d2a, b_d2b, out,
-    first_w, ring, x_a, x_s, x_u, m_1, m_2, m_o, d_2, acc_ref, wide, pool_buf,
-    sem_2a, sem_2b, sem_ma, sem_mb, sem_u2, sem_d2a, sem_d2b, sem_out, send_sem, recv_sem,
+    p1_hbm, w_2a, w_2b, w_ma, w_mb, w_u2, w_d2a, w_d2b, b_2a, b_2b, b_ma, b_mb, b_d2a, b_d2b, out,
+    p1, first_w, ring, x_a, x_s, x_u, m_1, m_2, m_o, d_2, acc_ref, wide, pool_buf,
+    sem_2a, sem_2b, sem_ma, sem_mb, sem_u2, sem_d2a, sem_d2b, sem_p1, sem_out, send_sem, recv_sem,
 ):
     strip = strip_index()
     prev_dev = strip_device((strip + LAST_STRIP) % STRIPS)
     next_dev = strip_device((strip + 1) % STRIPS)
 
-    def exchange(buf, width, lane0, lanes, rows, index):
+    def exchange(buf, width, lane0, lanes, rows, index, target=None):
+        target = buf if target is None else target
         lane = pl.ds(lane0, lanes)
         copies = []
         for side, src_row, dst_row, device in ((0, 1, rows + 1, prev_dev), (1, rows, 0, next_dev)):
             copies.append(
                 pltpu.make_async_remote_copy(
                     src_ref=buf.at[pl.ds(src_row * width, width), lane],
-                    dst_ref=buf.at[pl.ds(dst_row * width, width), lane],
+                    dst_ref=target.at[pl.ds(dst_row * width, width), lane],
                     send_sem=send_sem.at[index, side],
                     recv_sem=recv_sem.at[index, side],
                     device_id=device,
@@ -349,15 +371,10 @@
         for copy in copies:
             copy.wait()
 
-    def halo(buf, width, channels, rows, plain=False):
+    def halo(buf, width, channels, rows):
         for row, inside in ((0, strip > 0), (rows + 1, strip < LAST_STRIP)):
-            lanes = pl.ds(0 if plain else channels, channels)
-            value = buf[pl.ds(row * width, width), lanes].astype(F32)
-            value = jnp.where(inside, value, 0.0)
-            if plain:
-                buf[pl.ds(row * width, width), lanes] = value.astype(BF16)
-            else:
-                put3(buf, row * width, 0, channels, value, width)
+            value = buf[pl.ds(row * width, width), pl.ds(channels, channels)].astype(F32)
+            put3(buf, row * width, 0, channels, jnp.where(inside, value, 0.0), width)
 
     copies_2a = []
     for tap in range(TAPS):
@@ -407,6 +424,8 @@
     copies_d2a = tap_copies(w_d2a, DEEP, 0, sem_d2a)
     copies_d2b = tap_copies(w_d2b, MIDDLE, N6400, sem_d2b)
 
+    copy_p1 = pltpu.make_async_copy(p1_hbm, p1, sem_p1)
+    copy_p1.start()
     start(copies_2a)
 
     barrier = pltpu.get_barrier_semaphore()
@@ -416,6 +435,7 @@
 
     for di in range(3):
         first_w[PACK * di + PACK_USED : PACK * di + PACK, :] = jnp.zeros((REST, MIDDLE), BF16)
+    copy_p1.wait()
     finish(copies_2a)
     start(copies_2b)
     start(copies_ma)
@@ -426,28 +446,28 @@
     ex_m2 = exchange(m_2, STRIP_ROWS, DEEP, DEEP, STRIPS, 3)
     ex_u = exchange(x_u, REST, MIDDLE, MIDDLE, N16, IN_CH)
     ex_b = exchange(x_a, REST, MIDDLE, MIDDLE, N16, FIVE)
-    ex_d = exchange(d_2, REST, 0, MIDDLE, N16, SIX)
+    ex_d = exchange(d_2, REST, 0, MIDDLE, N16, SIX, out)
     tiles = ((0, TILE), (TILE, TILE), (N512, LANES))
 
     def enc2a(i, carry):
-        block = i + 1 - 2 * (i % 2)
-        row0 = pl.multiple_of(block * TILE, TILE)
-
-        @pl.when(i == 3)
+        @pl.when(i == 1)
         def _():
             start(ex_a)
 
-        for lane0, lanes in tiles:
-            acc = dot(p1[pl.ds(row0, TILE), 0:PACK], first_w[0:PACK, pl.ds(lane0, lanes)])
-            for di in (1, 2):
-                acc = acc + dot(
-                    p1[pl.ds(row0 + REST * di, TILE), 0:PACK], first_w[PACK * di : PACK * di + PACK, pl.ds(lane0, lanes)]
-                )
-            value = jnp.maximum(acc + bias_row(b_2a, lane0, lanes), 0.0)
-            put3(x_a, row0 + REST, lane0, MIDDLE, value, REST)
+        for block in (i, 3 - i):
+            row0 = pl.multiple_of(block * TILE, TILE)
+            for lane0, lanes in tiles:
+                acc = dot(p1[pl.ds(row0, TILE), 0:PACK], first_w[0:PACK, pl.ds(lane0, lanes)])
+                for di in (1, 2):
+                    acc = acc + dot(
+                        p1[pl.ds(row0 + REST * di, TILE), 0:PACK],
+                        first_w[PACK * di : PACK * di + PACK, pl.ds(lane0, lanes)],
+                    )
+                value = jnp.maximum(acc + bias_row(b_2a, lane0, lanes), 0.0)
+                put3(x_a, row0 + REST, lane0, MIDDLE, value, REST)
         return carry
 
-    lax.fori_loop(0, IN_CH, enc2a, 0)
+    lax.fori_loop(0, 2, enc2a, 0)
     finish(copies_2b)
     start(copies_mb[0:2])
     start(copies_u2[0:2])
@@ -515,10 +535,16 @@
 
     lax.fori_loop(0, 3, mid_a, 0)
     start(copies_mb[LAST_STRIP:TAPS])
-    for lane0 in range(0, DEEP, TILE):
-        value = jnp.maximum(acc_ref[:, pl.ds(lane0, TILE)] + bias_row(b_ma, lane0, TILE), 0.0)
-        put3(m_2, STRIP_ROWS, lane0, DEEP, value, STRIP_ROWS)
+
+    def mid_a_rows(first, rows):
+        for lane0 in range(0, DEEP, TILE):
+            value = jnp.maximum(acc_ref[pl.ds(first, rows), pl.ds(lane0, TILE)] + bias_row(b_ma, lane0, TILE), 0.0)
+            put3(m_2, STRIP_ROWS + first, lane0, DEEP, value, STRIP_ROWS)
+
+    mid_a_rows(0, STRIP_ROWS)
+    mid_a_rows(N224, STRIP_ROWS)
     start(ex_m2)
+    mid_a_rows(STRIP_ROWS, N192)
     acc_ref[...] = jnp.zeros_like(acc_ref)
 
     def mid_b(k, carry):
@@ -632,16 +658,15 @@
         return carry
 
     lax.fori_loop(0, IN_CH, dec2b, 0)
+    result = pltpu.make_async_copy(d_2.at[pl.ds(REST, PACK), :], out.at[pl.ds(REST, PACK), :], sem_out)
+    result.start()
     finish(ex_d)
-    halo(d_2, REST, MIDDLE, N16, plain=True)
-    result = pltpu.make_async_copy(d_2, out, sem_out)
-    result.start()
     result.wait()
 
 
 def dec1_kernel(
     d_2, s1, w_u1, w_d1a, w_d1b, b_d1a, b_d1b, w_head, b_head, out,
-    x_u, x_s, x_d, y_rest, st_u, st_a, st_b, wu_main, wu_rest, wa_main, wa_rest, wb_main, wb_rest, wide, result, pending,
+    x_u, x_s, x_d, y_rest, st_u, st_a, st_b, wu_main, wu_rest, wa_main, wa_rest, wb_main, wb_rest, wide, result, pending, stage, skip, low,
     sem, send_sem, recv_sem,
 ):
     strip = strip_index()
@@ -649,20 +674,26 @@
     col = lax.axis_index("col")
     copy_u = pltpu.make_async_copy(w_u1, st_u, sem.at[0])
     copy_a = pltpu.make_async_copy(w_d1a, st_a, sem.at[1])
-    copy_s = pltpu.make_async_copy(s1, x_s, sem.at[2])
+    copy_s = pltpu.make_async_copy(s1, skip, sem.at[2])
     copy_b = pltpu.make_async_copy(w_d1b, st_b, sem.at[3])
-    for copy in (copy_u, copy_a, copy_s, copy_b):
-        copy.start()
+    copy_d = pltpu.make_async_copy(d_2, low, sem.at[IN_CH])
+    copy_u.start()
+    copy_d.start()
     barrier = enter_barrier()
 
+    stage[...] = jnp.zeros_like(stage)
     copy_u.wait()
+    copy_a.start()
+    copy_s.start()
+    copy_b.start()
     for tap in range(IN_CH):
         wu_main[MIDDLE * tap : MIDDLE * tap + MIDDLE, :] = st_u[BASE * tap : BASE * tap + TILE, :].T
     wu_rest[...] = jnp.concatenate([st_u[BASE * tap + TILE : BASE * tap + BASE, :] for tap in range(IN_CH)], axis=0).T
+    copy_d.wait()
 
     def up1(i, carry):
         row0 = pl.multiple_of(i * BASE_PAD, LANES)
-        lhs = d_2[pl.ds(row0, BASE_PAD), :]
+        lhs = low[pl.ds(row0, BASE_PAD), :]
         rest = dot(lhs, wu_rest[...])
         for p in range(2):
             part = rest[:, LANES * p : LANES * p + LANES]
@@ -683,21 +714,42 @@
 
     lax.fori_loop(0, 3, up1, 0)
 
+    @pl.when(strip == 0)
+    def _():
+        x_u[0:TILE, :] = jnp.zeros((TILE, N1152), BF16)
+
+    @pl.when(strip == LAST_STRIP)
+    def _():
+        x_u[N4352:N4608, :] = jnp.zeros((TILE, N1152), BF16)
+
     copy_a.wait()
-    pack_transposed(st_a, wa_main, wa_rest)
+    turn_rest(st_a, wa_main, wa_rest)
     copy_s.wait()
 
     def rest_a(i, carry):
+        base = pl.multiple_of(i * N1536, N512)
+
+        def spread(j):
+            rows = pl.ds(base + TILE * j, TILE)
+            put3_320(
+                x_s, base + TILE * j, skip[rows, 0:TILE].astype(F32), skip[rows, TILE:BASE_PAD].astype(F32), LANES, stage.at[j % 2]
+            )
+
+        spread(0)
         for j in range(SIX):
-            rows = pl.ds(pl.multiple_of(i * N1536 + TILE * j, TILE), TILE)
+            rows = pl.ds(base + TILE * j, TILE)
             y_rest[rows, :] = dot(x_u[rows, 0:PACK], wa_rest[0:PACK, :]) + dot(
                 x_s[rows, 0:PACK], wa_rest[PACK:N2048, :]
             )
+            if j < FIVE:
+                spread(j + 1)
+            if j < 3:
+                turn_main(st_a, wa_main, i, j)
         return carry
 
     lax.fori_loop(0, 3, rest_a, 0)
 
-    def conv_a(row0, first_row):
+    def conv_a(row0, first_row, slot):
         acc = None
         for di in range(3):
             rows = pl.ds(row0 + LANES * di, TILE)
@@ -707,15 +759,15 @@
                 acc = part if acc is None else acc + part
         main = valid_rows(jnp.maximum(acc + bias_row(b_d1a, 0, TILE), 0.0), first_row, LANES)
         tail = valid_rows(jnp.maximum(rest_sum(y_rest, row0, TILE) + bias_rest(b_d1a), 0.0), first_row, LANES)
-        put3_320(x_d, row0, main, low_lanes(tail), LANES)
+        put3_320(x_d, row0, main, low_lanes(tail), LANES, stage.at[slot])
 
     def dec1a(i, carry):
         for j in range(IN_CH):
-            conv_a(pl.multiple_of(i * PACK + TILE * j, TILE), STRIP_ROWS * strip - 1 + STRIPS * i + 2 * j)
+            conv_a(pl.multiple_of(i * PACK + TILE * j, TILE), STRIP_ROWS * strip - 1 + STRIPS * i + 2 * j, j % 2)
         return carry
 
     lax.fori_loop(0, IN_CH, dec1a, 0)
-    conv_a(N4096, STRIP_ROWS * strip + N31)
+    conv_a(N4096, STRIP_ROWS * strip + N31, 0)
 
     copy_b.wait()
     pack_weights(st_b, wb_main, wb_rest)
@@ -795,9 +847,9 @@
         s1, p1 = pl.pallas_call(
             enc1_kernel,
             grid=(3,),
-            out_shape=(jax.ShapeDtypeStruct((N4608, N1152), BF16), jax.ShapeDtypeStruct((N1152, N1152), BF16)),
+            out_shape=(jax.ShapeDtypeStruct((N4608, BASE_PAD), BF16), jax.ShapeDtypeStruct((N1152, N1152), BF16)),
             in_specs=[vmem, vmem, vmem, hbm, vmem],
-            out_specs=(pl.BlockSpec((N1536, N1152), lambda i: (i, 0)), pl.BlockSpec((BASE_PAD, N1152), lambda i: (i, 0))),
+            out_specs=(pl.BlockSpec((N1536, BASE_PAD), lambda i: (i, 0)), pl.BlockSpec((BASE_PAD, N1152), lambda i: (i, 0))),
             scratch_shapes=[
                 pltpu.VMEM((2, N40, IN_CH, REST), BF16),
                 pltpu.VMEM((N42, STRIP_ROWS, LANES), BF16),
@@ -807,7 +859,9 @@
                 pltpu.VMEM((N1792, TILE), F32),
                 pltpu.VMEM((N3072, TILE), BF16),
                 pltpu.VMEM((PACK, TILE), BF16),
-                pltpu.VMEM((LANES, LANES), F32),
+                pltpu.VMEM((2, LANES, LANES), F32),
+                pltpu.VMEM((2, 3, N288, LANES), F32),
+                pltpu.VMEM((2, 3, N80, LANES), F32),
                 dma, dma((IN_CH,)), dma((2, 2)),
             ],
             compiler_params=pltpu.CompilerParams(
@@ -819,9 +873,10 @@
         d2 = pl.pallas_call(
             mid_kernel,
             out_shape=jax.ShapeDtypeStruct((N1152, MIDDLE), BF16),
-            in_specs=[vmem] + [hbm] * LAST_STRIP + [vmem] * SIX,
+            in_specs=[hbm] * STRIPS + [vmem] * SIX,
             out_specs=hbm,
             scratch_shapes=[
+                pltpu.VMEM((N1152, N1152), BF16),
                 pltpu.VMEM((N3072, MIDDLE), BF16),
                 pltpu.VMEM((RING_ROWS, DEEP), BF16),
                 pltpu.VMEM((N1152, MIDDLE3), BF16),
@@ -834,7 +889,7 @@
                 pltpu.VMEM((TILE, DEEP), F32),
                 pltpu.VMEM((FIVE, N512, LANES), F32),
                 pltpu.VMEM((LANES, LANES), F32),
-                dma((N18,)), dma((TAPS,)), dma((3,)), dma((TAPS,)), dma((IN_CH,)), dma((TAPS,)), dma((TAPS,)), dma,
+                dma((N18,)), dma((TAPS,)), dma((3,)), dma((TAPS,)), dma((IN_CH,)), dma((TAPS,)), dma((TAPS,)), dma, dma,
                 dma((LAST_STRIP, 2)), dma((LAST_STRIP, 2)),
             ],
             compiler_params=pltpu.CompilerParams(
@@ -852,7 +907,7 @@
         y = pl.pallas_call(
             dec1_kernel,
             out_shape=jax.ShapeDtypeStruct((REST, IN_CH, REST), F32),
-            in_specs=[vmem] + [hbm] * IN_CH + [vmem] * 3 + [pl.BlockSpec(memory_space=pltpu.SMEM)],
+            in_specs=[hbm] * FIVE + [vmem] * 3 + [pl.BlockSpec(memory_space=pltpu.SMEM)],
             out_specs=hbm,
             scratch_shapes=[
                 pltpu.VMEM((N4608, N1152), BF16),
@@ -871,7 +926,10 @@
                 pltpu.VMEM((2, 3, REST_AT, LANES), F32),
                 pltpu.VMEM((2, STRIP_ROWS, IN_CH, REST), F32),
                 pltpu.VMEM((TILE, BASE), BF16),
-                dma((IN_CH,)), dma((2,)), dma((2,)),
+                pltpu.VMEM((2, 3, N288, LANES), F32),
+                pltpu.VMEM((N4608, BASE_PAD), BF16),
+                pltpu.VMEM((N1152, MIDDLE), BF16),
+                dma((FIVE,)), dma((2,)), dma((2,)),
             ],
             compiler_params=pltpu.CompilerParams(vmem_limit_bytes=VMEM_LIMIT, collective_id=2, has_side_effects=True),
             name="dec1",

time: 147 us -> 144 us (0.980)
  Pallas kernels: 145 us -> 141 us
    pallas_call x1, Pallas kernels: 28.4 us -> 26.4 us  [body(): pl.pallas_call(enc1_kernel, grid=(3,), out_shape=(jax.ShapeDtypeStruct((N...]
    pallas_call x1, Pallas kernels: 71.9 us -> 70.4 us  [body(): pl.pallas_call(mid_kernel, out_shape=jax.ShapeDtypeStruct((N1152, MIDDLE)...]
where the time goes in v5:
time: 144 us; the launch traced here: 143 us
  Pallas kernels  141 us (98%)
  local copies, waits for them, and re-layouts  1.57 us (1%)
    pallas_call x1, Pallas kernels, body(): pl.pallas_call(mid_kernel, out_shape=jax.ShapeDtypeStruct((N1152, MIDDLE)...  70.4 us
    pallas_call x1, Pallas kernels, body(): pl.pallas_call(dec1_kernel, out_shape=jax.ShapeDtypeStruct((REST, IN_CH,...  44.8 us
    pallas_call x1, Pallas kernels, body(): pl.pallas_call(enc1_kernel, grid=(3,), out_shape=(jax.ShapeDtypeStruct((N...  26.4 us

profile of v5, /device:TPU:0, one launch (start us, length us, event | category | flops | bytes accessed | tf_op | source)
XLA Modules:
  0.0 143.1 jit_solution(11147127987729289078)
XLA Ops:
  0.0 26.4 %enc1.1 = (bf16[4608,384]{1,0:T(8,128)(2,1)}, bf16[1152,1152]{1,0:T(8,128)(2,1)}) custom-call(bf16[64,4,64]{2,1,0:T(4,128)(2,1)} %bitcast.30, bf16[3,3,4,320]{3,2,1,0:T(4,128)(2,1)} %w_a.1, f32[320]{0:T(512)} %b_a.1, bf16[2880,320]{1,0:T(8,128)(2,1)} %bitcast.26, f32[320]{0:T(512)} %b_b.1), custom_call_target="tpu_custom_call" | custom-call | tf_op jit(solution)/shard_map/enc1/pallas_call | solution.py:847
  26.4 70.4 %mid.1.d_2 = bf16[1152,640]{1,0:T(8,128)(2,1)} custom-call(bf16[1152,1152]{1,0:T(8,128)(2,1)} %get-tuple-element.7.p1_hbm, bf16[2880,640]{1,0:T(8,128)(2,1)} %bitcast.24, bf16[5760,640]{1,0:T(8,128)(2,1)} %bitcast.21, bf16[5760,1280]{1,0:T(8,128)(2,1)} %bitcast.19, bf16[11520,1280]{1,0:T(8,128)(2,1)} %bitcast.18, bf16[5120,640]{1,0:T(8,128)(2,1)} %bitcast.23, ...), custom_call_target="tpu_custom_call" | custom-call | tf_op jit(solution)/shard_map/mid/pallas_call | solution.py:873
  96.7 44.8 %dec1.1 = f32[64,4,64]{2,1,0:T(4,128)} custom-call(bf16[1152,640]{1,0:T(8,128)(2,1)} %mid.1.d_2, bf16[4608,384]{1,0:T(8,128)(2,1)} %get-tuple-element.8.s1, bf16[1280,640]{1,0:T(8,128)(2,1)} %bitcast.28, bf16[2880,640]{1,0:T(8,128)(2,1)} %bitcast.25, bf16[2880,320]{1,0:T(8,128)(2,1)} %bitcast.27, f32[320]{0:T(512)} %b_d1a.1, f32[320]{0:T(512)} %b_d1b.1, ...), custom_call_target="tpu_custom_call" | custom-call | tf_op jit(solution)/shard_map/dec1/pallas_call | solution.py:907
  141.5 1.6 %copy.27 = f32[64,64,4]{1,2,0:T(4,128)} copy(f32[64,64,4]{1,2,0:T(4,128)} %bitcast.29) | data formatting | bytes 131072

commit v6 on v5

--- a/solution.py
+++ b/solution.py
@@ -7,16 +7,20 @@
 from jax.experimental.pallas import tpu as pltpu
 from jax.sharding import PartitionSpec as P
 
+KERNEL = 3
 IN_CH = 4
 FIVE = 5
 SIX = 6
 LAST_STRIP = 7
 STRIPS = 8
 TAPS = 9
+N10 = 10
 N12 = 12
 N16 = 16
 N18 = 18
+N22 = 22
 N28 = 28
+N29 = 29
 N30 = 30
 N31 = 31
 STRIP_ROWS = 32
@@ -77,7 +81,7 @@
 def strip_device(position):
     col = position // IN_CH
     rest = position % IN_CH
-    return (lax.axis_index("data"), col, rest + col * (3 - 2 * rest))
+    return (lax.axis_index("data"), col, rest + col * (KERNEL - 2 * rest))
 
 
 def dot(a, b):
@@ -96,7 +100,7 @@
 
 def put3(dst, row0, lane0, channels, value, width):
     rows, lanes = value.shape
-    for step in range(3):
+    for step in range(KERNEL):
         dst[pl.ds(row0, rows), pl.ds(step * channels + lane0, lanes)] = shifted(value, width, step).astype(BF16)
 
 
@@ -109,16 +113,16 @@
             stage[t, pitch * r + STRIPS : pitch * r + STRIPS + width, :] = plane[width * r : width * r + width]
 
     def moved(t, step):
-        if step == 1 or stage is None:
+        if stage is None:
             return shifted(planes[t], width, step)
         first = LAST_STRIP + step
         parts = [stage[t, pitch * r + first : pitch * r + first + width, :] for r in range(rows // width)]
         return jnp.concatenate(parts, axis=0) if len(parts) > 1 else parts[0]
 
-    for step in range(3):
+    for step in range(KERNEL):
         for t in range(2):
             dst[pl.ds(row0, rows), pl.ds(step * TILE + LANES * t, LANES)] = moved(t, step).astype(BF16)
-    first = moved(2, 0) + pltpu.roll(rest, REST, axis=1)
+    first = moved(2, 0) + pltpu.roll(moved(2, 1), REST, axis=1)
     dst[pl.ds(row0, rows), pl.ds(REST_AT, LANES)] = first.astype(BF16)
     dst[pl.ds(row0, rows), pl.ds(N896, LANES)] = moved(2, 2).astype(BF16)
 
@@ -128,16 +132,16 @@
 
 
 def pack_weights(staged, main_ref, rest_ref):
-    for dj in range(3):
+    for dj in range(KERNEL):
         for start, size, row in ((0, TILE, TILE * dj), (TILE, REST, REST_AT + REST * dj)):
             parts = []
-            for di in range(3):
-                base = (3 * di + dj) * BASE + start
+            for di in range(KERNEL):
+                base = (KERNEL * di + dj) * BASE + start
                 main_ref[pl.ds(PACK * di + row, size), :] = staged[pl.ds(base, size), 0:TILE]
                 parts.append(staged[pl.ds(base, size), TILE:BASE])
             parts.append(jnp.zeros((size, REST), BF16))
             rest_ref[pl.ds(row, size), :] = jnp.concatenate(parts, axis=1)
-    clear_pad(main_ref, 3)
+    clear_pad(main_ref, KERNEL)
     clear_pad(rest_ref, 1)
 
 
@@ -155,8 +159,8 @@
 
 
 def turn_rest(staged, main_ref, rest_ref):
-    for dj in range(3):
-        parts = [staged[pl.ds(PACK_USED * di + BASE * dj + TILE, REST), :] for di in range(3)] + [jnp.zeros((REST, MIDDLE), BF16)]
+    for dj in range(KERNEL):
+        parts = [staged[pl.ds(PACK_USED * di + BASE * dj + TILE, REST), :] for di in range(KERNEL)] + [jnp.zeros((REST, MIDDLE), BF16)]
         turned = jnp.concatenate(parts, axis=0).T
         for src in range(2):
             rest_ref[pl.ds(PACK * src + TILE * dj, TILE), :] = turned[BASE * src : BASE * src + TILE]
@@ -247,9 +251,9 @@
         stage[...] = jnp.zeros_like(stage)
         stage_p[...] = jnp.zeros_like(stage_p)
 
-        for di in range(3):
+        for di in range(KERNEL):
             taps = []
-            for dj in range(3):
+            for dj in range(KERNEL):
                 tap = jnp.concatenate([w_a[di, dj].astype(F32), jnp.zeros((IN_CH, BASE), F32)], axis=0)
                 taps.append(jnp.concatenate([tap, jnp.zeros((STRIPS, REST), F32)], axis=1))
             taps.append(jnp.zeros((STRIPS, BASE_PAD), F32))
@@ -300,19 +304,15 @@
         lax.fori_loop(0, FIVE, expand, 0)
 
         def stem(i, carry):
-            for j in range(IN_CH):
-                r = STRIPS * i + 2 * j
-                row0 = pl.multiple_of(r * LANES, TILE)
-                patch = jnp.concatenate(
-                    [jnp.concatenate([planes[r + k + di] for di in range(3)], axis=0) for k in range(2)], axis=1
-                )
+            for j in range(STRIPS):
+                r = STRIPS * i + j
+                patch = jnp.concatenate([planes[r + di] for di in range(KERNEL)], axis=0)
                 acc = lax.dot_general(patch, w_stem[...], (((0,), (0,)), ((), ())), preferred_element_type=F32)
-                main = jnp.maximum(acc[:, 0:TILE] + bias_row(b_a, 0, TILE), 0.0)
-                tail = jnp.maximum(acc[:, TILE:BASE_PAD] + bias_rest(b_a), 0.0)
-                first_row = STRIP_ROWS * strip - 3 + r
-                put3_320(
-                    x_a, row0, valid_rows(main, first_row, LANES), valid_rows(tail, first_row, LANES), LANES, stage.at[j % 2]
-                )
+                image_row = STRIP_ROWS * strip - KERNEL + r
+                inside = (image_row >= 0) & (image_row < TILE)
+                main = jnp.where(inside, jnp.maximum(acc[:, 0:TILE] + bias_row(b_a, 0, TILE), 0.0), 0.0)
+                tail = jnp.where(inside, jnp.maximum(acc[:, TILE:BASE_PAD] + bias_rest(b_a), 0.0), 0.0)
+                put3_320(x_a, pl.multiple_of(r * LANES, LANES), main, tail, LANES, stage.at[j % 2])
             return carry
 
         lax.fori_loop(0, FIVE, stem, 0)
@@ -378,7 +378,7 @@
 
     copies_2a = []
     for tap in range(TAPS):
-        di, dj = tap // 3, tap % 3
+        di, dj = tap // KERNEL, tap % KERNEL
         for part, (start_row, size, row) in enumerate(((0, TILE, TILE * dj), (TILE, REST, REST_AT + REST * dj))):
             copies_2a.append(
                 pltpu.make_async_copy(
@@ -409,7 +409,7 @@
 
     copies_mb = [
         pltpu.make_async_copy(
-            w_mb.at[pl.ds(DEEP * (3 * (1, 0, 2)[k // 3] + k % 3), DEEP), :], ring.at[pl.ds(mb_row(k), DEEP), :], sem_mb.at[k]
+            w_mb.at[pl.ds(DEEP * (KERNEL * (1, 0, 2)[k // KERNEL] + k % KERNEL), DEEP), :], ring.at[pl.ds(mb_row(k), DEEP), :], sem_mb.at[k]
         )
         for k in range(TAPS)
     ]
@@ -433,7 +433,7 @@
         pl.semaphore_signal(barrier, inc=1, device_id=device, device_id_type=MESH)
     pl.semaphore_wait(barrier, 2)
 
-    for di in range(3):
+    for di in range(KERNEL):
         first_w[PACK * di + PACK_USED : PACK * di + PACK, :] = jnp.zeros((REST, MIDDLE), BF16)
     copy_p1.wait()
     finish(copies_2a)
@@ -443,7 +443,7 @@
     ex_a = exchange(x_a, REST, MIDDLE, MIDDLE, N16, 0)
     ex_s = exchange(x_s, REST, MIDDLE, MIDDLE, N16, 1)
     ex_m1 = exchange(m_1, STRIP_ROWS, MIDDLE, MIDDLE, STRIPS, 2)
-    ex_m2 = exchange(m_2, STRIP_ROWS, DEEP, DEEP, STRIPS, 3)
+    ex_m2 = exchange(m_2, STRIP_ROWS, DEEP, DEEP, STRIPS, KERNEL)
     ex_u = exchange(x_u, REST, MIDDLE, MIDDLE, N16, IN_CH)
     ex_b = exchange(x_a, REST, MIDDLE, MIDDLE, N16, FIVE)
     ex_d = exchange(d_2, REST, 0, MIDDLE, N16, SIX, out)
@@ -454,7 +454,7 @@
         def _():
             start(ex_a)
 
-        for block in (i, 3 - i):
+        for block in (i, KERNEL - i):
             row0 = pl.multiple_of(block * TILE, TILE)
             for lane0, lanes in tiles:
                 acc = dot(p1[pl.ds(row0, TILE), 0:PACK], first_w[0:PACK, pl.ds(lane0, lanes)])
@@ -474,11 +474,11 @@
 
     def conv640(src, row0, base, lane0, lanes):
         acc = None
-        for di in range(3):
+        for di in range(KERNEL):
             weights = jnp.concatenate(
                 [
                     ring[base + MIDDLE * (t // 2) : base + MIDDLE * (t // 2) + MIDDLE, pl.ds(MIDDLE * (t % 2) + lane0, lanes)]
-                    for t in range(3 * di, 3 * di + 3)
+                    for t in range(KERNEL * di, KERNEL * di + KERNEL)
                 ],
                 axis=0,
             )
@@ -495,7 +495,7 @@
             finish(ex_a)
             halo(x_a, REST, MIDDLE, N16)
 
-        @pl.when(i == 3)
+        @pl.when(i == KERNEL)
         def _():
             start(ex_m1)
             start(ex_s)
@@ -533,7 +533,7 @@
             )
         return carry
 
-    lax.fori_loop(0, 3, mid_a, 0)
+    lax.fori_loop(0, KERNEL, mid_a, 0)
     start(copies_mb[LAST_STRIP:TAPS])
 
     def mid_a_rows(first, rows):
@@ -547,39 +547,39 @@
     mid_a_rows(STRIP_ROWS, N192)
     acc_ref[...] = jnp.zeros_like(acc_ref)
 
-    def mid_b(k, carry):
-        t = k // 3
+    def mid_b(t, carry):
         di = (t + 1) % 2 + 2 * (t // 2) - t // 2
 
-        for j in range(TAPS):
-            @pl.when(k == j)
+        for j in range(KERNEL):
+            @pl.when(t == j)
             def _(j=j):
-                copies_mb[j].wait()
-
-        @pl.when(k == 3)
+                finish(copies_mb[KERNEL * j : KERNEL * j + KERNEL])
+
+        @pl.when(t == 1)
         def _():
             start(copies_u2[2:IN_CH])
+            start(copies_d2a[0:2])
             finish(ex_m2)
             halo(m_2, STRIP_ROWS, DEEP, STRIPS)
 
-        @pl.when(k == FIVE)
-        def _():
-            start(copies_d2a[0:IN_CH])
-
-        @pl.when(k == LAST_STRIP)
-        def _():
-            start(copies_d2a[IN_CH:TAPS])
-
-        base = pl.multiple_of(mb_row(k), LANES)
+        @pl.when(t == 2)
+        def _():
+            start(copies_d2a[2:STRIPS])
+
         lhs_row = pl.multiple_of(STRIP_ROWS * di, STRIP_ROWS)
-        lhs_lane = pl.multiple_of(DEEP * (k % 3), DEEP)
         for lane0 in range(0, DEEP, TILE):
-            acc_ref[:, pl.ds(lane0, TILE)] += dot(
-                m_2[pl.ds(lhs_row, TILE), pl.ds(lhs_lane, DEEP)], ring[pl.ds(base, DEEP), pl.ds(lane0, TILE)]
-            )
+            acc = None
+            for dj in range(KERNEL):
+                base = pl.multiple_of(mb_row(KERNEL * t + dj), LANES)
+                part = dot(
+                    m_2[pl.ds(lhs_row, TILE), DEEP * dj : DEEP * dj + DEEP], ring[pl.ds(base, DEEP), pl.ds(lane0, TILE)]
+                )
+                acc = part if acc is None else acc + part
+            acc_ref[:, pl.ds(lane0, TILE)] += acc
         return carry
 
-    lax.fori_loop(0, TAPS, mid_b, 0)
+    lax.fori_loop(0, KERNEL, mid_b, 0)
+    start(copies_d2a[STRIPS:TAPS])
     for lane0 in range(0, DEEP, TILE):
         value = jnp.maximum(acc_ref[:, pl.ds(lane0, TILE)] + bias_row(b_mb, lane0, TILE), 0.0)
         m_o[:, pl.ds(lane0, TILE)] = value.astype(BF16)
@@ -619,15 +619,15 @@
             finish(ex_u)
             halo(x_u, REST, MIDDLE, N16)
 
-        @pl.when(i == 3)
+        @pl.when(i == KERNEL)
         def _():
             start(ex_b)
 
         for lane0, lanes in tiles:
             acc = None
             for tap in range(TAPS):
-                rows = pl.ds(row0 + REST * (tap // 3), TILE)
-                cols = pl.ds(MIDDLE * (tap % 3), MIDDLE)
+                rows = pl.ds(row0 + REST * (tap // KERNEL), TILE)
+                cols = pl.ds(MIDDLE * (tap % KERNEL), MIDDLE)
                 lhs = jnp.concatenate([x_u[rows, cols], x_s[rows, cols]], axis=1)
                 base = DEEP * (tap // 2)
                 part = dot(lhs, ring[base : base + DEEP, pl.ds(MIDDLE * (tap % 2) + lane0, lanes)])
@@ -648,7 +648,7 @@
             finish(ex_b)
             halo(x_a, REST, MIDDLE, N16)
 
-        @pl.when(i == 3)
+        @pl.when(i == KERNEL)
         def _():
             start(ex_d)
 
@@ -666,7 +666,7 @@
 
 def dec1_kernel(
     d_2, s1, w_u1, w_d1a, w_d1b, b_d1a, b_d1b, w_head, b_head, out,
-    x_u, x_s, x_d, y_rest, st_u, st_a, st_b, wu_main, wu_rest, wa_main, wa_rest, wb_main, wb_rest, wide, result, pending, stage, skip, low,
+    x_u, x_s, x_d, y_rest, st_u, st_a, st_b, wu_main, wu_rest, wa_main, wa_rest, wb_main, wb_rest, wide, result, pending, stage, skip, low, late,
     sem, send_sem, recv_sem,
 ):
     strip = strip_index()
@@ -675,7 +675,7 @@
     copy_u = pltpu.make_async_copy(w_u1, st_u, sem.at[0])
     copy_a = pltpu.make_async_copy(w_d1a, st_a, sem.at[1])
     copy_s = pltpu.make_async_copy(s1, skip, sem.at[2])
-    copy_b = pltpu.make_async_copy(w_d1b, st_b, sem.at[3])
+    copy_b = pltpu.make_async_copy(w_d1b, st_b, sem.at[KERNEL])
     copy_d = pltpu.make_async_copy(d_2, low, sem.at[IN_CH])
     copy_u.start()
     copy_d.start()
@@ -712,7 +712,7 @@
                 )
         return carry
 
-    lax.fori_loop(0, 3, up1, 0)
+    lax.fori_loop(0, KERNEL, up1, 0)
 
     @pl.when(strip == 0)
     def _():
@@ -743,31 +743,43 @@
             )
             if j < FIVE:
                 spread(j + 1)
-            if j < 3:
+            if j < KERNEL:
                 turn_main(st_a, wa_main, i, j)
         return carry
 
-    lax.fori_loop(0, 3, rest_a, 0)
-
-    def conv_a(row0, first_row, slot):
+    lax.fori_loop(0, KERNEL, rest_a, 0)
+
+    def conv_a(row0):
         acc = None
-        for di in range(3):
+        for di in range(KERNEL):
             rows = pl.ds(row0 + LANES * di, TILE)
             for src, ref in enumerate((x_u, x_s)):
                 base = N3072 * src + PACK * di
                 part = dot(ref[rows, 0:PACK], wa_main[base : base + PACK, :])
                 acc = part if acc is None else acc + part
+        return acc
+
+    def put_a(acc, row0, first_row, slot):
         main = valid_rows(jnp.maximum(acc + bias_row(b_d1a, 0, TILE), 0.0), first_row, LANES)
         tail = valid_rows(jnp.maximum(rest_sum(y_rest, row0, TILE) + bias_rest(b_d1a), 0.0), first_row, LANES)
         put3_320(x_d, row0, main, low_lanes(tail), LANES, stage.at[slot])
 
+    late[...] = jnp.zeros_like(late)
+
     def dec1a(i, carry):
+        base = pl.multiple_of(i * PACK, PACK)
+        put_a(late[...], pl.multiple_of(jnp.maximum(base - TILE, 0), TILE), STRIP_ROWS * strip - KERNEL + STRIPS * i, 1)
         for j in range(IN_CH):
-            conv_a(pl.multiple_of(i * PACK + TILE * j, TILE), STRIP_ROWS * strip - 1 + STRIPS * i + 2 * j, j % 2)
+            acc = conv_a(base + TILE * j)
+            if j == KERNEL:
+                late[...] = acc
+            else:
+                put_a(acc, base + TILE * j, STRIP_ROWS * strip - 1 + STRIPS * i + 2 * j, j % 2)
         return carry
 
     lax.fori_loop(0, IN_CH, dec1a, 0)
-    conv_a(N4096, STRIP_ROWS * strip + N31, 0)
+    put_a(late[...], N3840, STRIP_ROWS * strip + N29, 1)
+    put_a(conv_a(N4096), N4096, STRIP_ROWS * strip + N31, 0)
 
     copy_b.wait()
     pack_weights(st_b, wb_main, wb_rest)
@@ -804,31 +816,37 @@
         pending[...] = waiting
         return carry
 
-    lax.fori_loop(0, IN_CH, dec1b, 0)
+    pushes = []
+    for part, first, rows in ((0, 0, N22), (1, N22, N10)):
+        for side in range(2):
+            pushes.append(
+                Push(
+                    result.at[side, pl.ds(first, rows)],
+                    out.at[pl.ds(STRIP_ROWS * (strip % 2) + first, rows)],
+                    send_sem.at[part, side],
+                    recv_sem.at[part, strip % 2],
+                    (lax.axis_index("data"), side, strip // 2),
+                    (strip // 2 == row) & (col == side),
+                )
+            )
+
+    lax.fori_loop(0, KERNEL, dec1b, 0)
+    pl.semaphore_wait(barrier, STRIPS)
+    for push in pushes[0:2]:
+        push.start()
+    lax.fori_loop(KERNEL, IN_CH, dec1b, 0)
     head(pending[...], N30)
 
-    pl.semaphore_wait(barrier, STRIPS)
-    pushes = []
-    for side in range(2):
-        tile_row = strip // 2
-        pushes.append(
-            Push(
-                result.at[side],
-                out.at[pl.ds(STRIP_ROWS * (strip % 2), STRIP_ROWS)],
-                send_sem.at[side],
-                recv_sem.at[strip % 2],
-                (lax.axis_index("data"), side, tile_row),
-                (tile_row == row) & (col == side),
-            )
-        )
-    for push in pushes:
+    for push in pushes[2:IN_CH]:
         push.start()
     for push in pushes:
         push.wait_send()
-    for half in range(2):
-        Push(
-            result.at[0], out.at[pl.ds(STRIP_ROWS * half, STRIP_ROWS)], send_sem.at[0], recv_sem.at[half], strip_device(strip), strip < 0
-        ).wait_recv()
+    for part, first, rows in ((0, 0, N22), (1, N22, N10)):
+        for half in range(2):
+            Push(
+                result.at[0, pl.ds(first, rows)], out.at[pl.ds(STRIP_ROWS * half + first, rows)],
+                send_sem.at[part, 0], recv_sem.at[part, half], strip_device(strip), strip < 0,
+            ).wait_recv()
 
 
 def solution(mesh):
@@ -846,7 +864,7 @@
         dma = pltpu.SemaphoreType.DMA
         s1, p1 = pl.pallas_call(
             enc1_kernel,
-            grid=(3,),
+            grid=(KERNEL,),
             out_shape=(jax.ShapeDtypeStruct((N4608, BASE_PAD), BF16), jax.ShapeDtypeStruct((N1152, N1152), BF16)),
             in_specs=[vmem, vmem, vmem, hbm, vmem],
             out_specs=(pl.BlockSpec((N1536, BASE_PAD), lambda i: (i, 0)), pl.BlockSpec((BASE_PAD, N1152), lambda i: (i, 0))),
@@ -860,8 +878,8 @@
                 pltpu.VMEM((N3072, TILE), BF16),
                 pltpu.VMEM((PACK, TILE), BF16),
                 pltpu.VMEM((2, LANES, LANES), F32),
-                pltpu.VMEM((2, 3, N288, LANES), F32),
-                pltpu.VMEM((2, 3, N80, LANES), F32),
+                pltpu.VMEM((2, KERNEL, N288, LANES), F32),
+                pltpu.VMEM((2, KERNEL, N80, LANES), F32),
                 dma, dma((IN_CH,)), dma((2, 2)),
             ],
             compiler_params=pltpu.CompilerParams(
@@ -889,7 +907,7 @@
                 pltpu.VMEM((TILE, DEEP), F32),
                 pltpu.VMEM((FIVE, N512, LANES), F32),
                 pltpu.VMEM((LANES, LANES), F32),
-                dma((N18,)), dma((TAPS,)), dma((3,)), dma((TAPS,)), dma((IN_CH,)), dma((TAPS,)), dma((TAPS,)), dma, dma,
+                dma((N18,)), dma((TAPS,)), dma((KERNEL,)), dma((TAPS,)), dma((IN_CH,)), dma((TAPS,)), dma((TAPS,)), dma, dma,
                 dma((LAST_STRIP, 2)), dma((LAST_STRIP, 2)),
             ],
             compiler_params=pltpu.CompilerParams(
@@ -902,12 +920,12 @@
         )
 
         def turned(weight):
-            return weight.transpose(0, 1, 3, 2).reshape(-1, weight.shape[2])
+            return weight.transpose(0, 1, KERNEL, 2).reshape(-1, weight.shape[2])
 
         y = pl.pallas_call(
             dec1_kernel,
             out_shape=jax.ShapeDtypeStruct((REST, IN_CH, REST), F32),
-            in_specs=[hbm] * FIVE + [vmem] * 3 + [pl.BlockSpec(memory_space=pltpu.SMEM)],
+            in_specs=[hbm] * FIVE + [vmem] * KERNEL + [pl.BlockSpec(memory_space=pltpu.SMEM)],
             out_specs=hbm,
             scratch_shapes=[
                 pltpu.VMEM((N4608, N1152), BF16),
@@ -923,13 +941,14 @@
                 pltpu.VMEM((N2048, TILE), BF16),
                 pltpu.VMEM((N3072, TILE), BF16),
                 pltpu.VMEM((PACK, TILE), BF16),
-                pltpu.VMEM((2, 3, REST_AT, LANES), F32),
+                pltpu.VMEM((2, KERNEL, REST_AT, LANES), F32),
                 pltpu.VMEM((2, STRIP_ROWS, IN_CH, REST), F32),
                 pltpu.VMEM((TILE, BASE), BF16),
-                pltpu.VMEM((2, 3, N288, LANES), F32),
+                pltpu.VMEM((2, KERNEL, N288, LANES), F32),
                 pltpu.VMEM((N4608, BASE_PAD), BF16),
                 pltpu.VMEM((N1152, MIDDLE), BF16),
-                dma((FIVE,)), dma((2,)), dma((2,)),
+                pltpu.VMEM((TILE, TILE), F32),
+                dma((FIVE,)), dma((2, 2)), dma((2, 2)),
             ],
             compiler_params=pltpu.CompilerParams(vmem_limit_bytes=VMEM_LIMIT, collective_id=2, has_side_effects=True),
             name="dec1",

time: 144 us -> 142 us (0.986)
  no operation moved by 1% of the time
where the time goes in v6:
time: 142 us
  Pallas kernels  140 us (99%)
  local copies, waits for them, and re-layouts  1.57 us (1%)
    pallas_call x1, Pallas kernels, body(): pl.pallas_call(mid_kernel, out_shape=jax.ShapeDtypeStruct((N1152, MIDDLE)...  69.2 us
    pallas_call x1, Pallas kernels, body(): pl.pallas_call(dec1_kernel, out_shape=jax.ShapeDtypeStruct((REST, IN_CH,...  44.8 us
    pallas_call x1, Pallas kernels, body(): pl.pallas_call(enc1_kernel, grid=(KERNEL,), out_shape=(jax.ShapeDtypeStru...  26.2 us

profile of v6, /device:TPU:0, one launch (start us, length us, event | category | flops | bytes accessed | tf_op | source)
XLA Modules:
  0.0 141.7 jit_solution(13593915966997963843)
XLA Ops:
  0.0 26.2 %enc1.1 = (bf16[4608,384]{1,0:T(8,128)(2,1)}, bf16[1152,1152]{1,0:T(8,128)(2,1)}) custom-call(bf16[64,4,64]{2,1,0:T(4,128)(2,1)} %bitcast.30, bf16[3,3,4,320]{3,2,1,0:T(4,128)(2,1)} %w_a.1, f32[320]{0:T(512)} %b_a.1, bf16[2880,320]{1,0:T(8,128)(2,1)} %bitcast.26, f32[320]{0:T(512)} %b_b.1), custom_call_target="tpu_custom_call" | custom-call | tf_op jit(solution)/shard_map/enc1/pallas_call | solution.py:865
  26.2 69.2 %mid.1.d_2 = bf16[1152,640]{1,0:T(8,128)(2,1)} custom-call(bf16[1152,1152]{1,0:T(8,128)(2,1)} %get-tuple-element.7.p1_hbm, bf16[2880,640]{1,0:T(8,128)(2,1)} %bitcast.24, bf16[5760,640]{1,0:T(8,128)(2,1)} %bitcast.21, bf16[5760,1280]{1,0:T(8,128)(2,1)} %bitcast.19, bf16[11520,1280]{1,0:T(8,128)(2,1)} %bitcast.18, bf16[5120,640]{1,0:T(8,128)(2,1)} %bitcast.23, ...), custom_call_target="tpu_custom_call" | custom-call | tf_op jit(solution)/shard_map/mid/pallas_call | solution.py:891
  95.4 44.8 %dec1.1 = f32[64,4,64]{2,1,0:T(4,128)} custom-call(bf16[1152,640]{1,0:T(8,128)(2,1)} %mid.1.d_2, bf16[4608,384]{1,0:T(8,128)(2,1)} %get-tuple-element.8.s1, bf16[1280,640]{1,0:T(8,128)(2,1)} %bitcast.28, bf16[2880,640]{1,0:T(8,128)(2,1)} %bitcast.25, bf16[2880,320]{1,0:T(8,128)(2,1)} %bitcast.27, f32[320]{0:T(512)} %b_d1a.1, f32[320]{0:T(512)} %b_d1b.1, ...), custom_call_target="tpu_custom_call" | custom-call | tf_op jit(solution)/shard_map/dec1/pallas_call | solution.py:925
  140.2 1.6 %copy.27 = f32[64,64,4]{1,2,0:T(4,128)} copy(f32[64,64,4]{1,2,0:T(4,128)} %bitcast.29) | data formatting | bytes 131072

commit v7 on v6

--- a/solution.py
+++ b/solution.py
@@ -16,6 +16,7 @@
 TAPS = 9
 N10 = 10
 N12 = 12
+N14 = 14
 N16 = 16
 N18 = 18
 N22 = 22
@@ -42,10 +43,10 @@
 N512 = 512
 MIDDLE = 640
 REST_AT = 768
-N896 = 896
 PACK_USED = 960
 PACK = 1024
 N1152 = 1152
+N1168 = 1168
 DEEP = 1280
 N1536 = 1536
 N1792 = 1792
@@ -58,8 +59,10 @@
 N3840 = 3840
 N4096 = 4096
 N4352 = 4352
+N4368 = 4368
 N4608 = 4608
-N5120 = 5120
+N4624 = 4624
+N5136 = 5136
 N6144 = 6144
 N6400 = 6400
 N8960 = 8960
@@ -121,10 +124,14 @@
 
     for step in range(KERNEL):
         for t in range(2):
-            dst[pl.ds(row0, rows), pl.ds(step * TILE + LANES * t, LANES)] = moved(t, step).astype(BF16)
+            dst[2 * step + t, pl.ds(row0, rows), :] = moved(t, step).astype(BF16)
     first = moved(2, 0) + pltpu.roll(moved(2, 1), REST, axis=1)
-    dst[pl.ds(row0, rows), pl.ds(REST_AT, LANES)] = first.astype(BF16)
-    dst[pl.ds(row0, rows), pl.ds(N896, LANES)] = moved(2, 2).astype(BF16)
+    dst[SIX, pl.ds(row0, rows), :] = first.astype(BF16)
+    dst[LAST_STRIP, pl.ds(row0, rows), :] = moved(2, 2).astype(BF16)
+
+
+def packed_rows(ref, row0, rows):
+    return jnp.concatenate([ref[t, pl.ds(row0, rows), :] for t in range(STRIPS)], axis=1)
 
 
 def low_lanes(value):
@@ -184,6 +191,13 @@
     return barrier
 
 
+def fetch(sources, targets, sems):
+    copies = [pltpu.make_async_copy(src, dst, sems.at[i]) for i, (src, dst) in enumerate(zip(sources, targets))]
+    for copy in copies:
+        copy.start()
+    return copies
+
+
 class Push:
     def __init__(self, src, dst, send_sem, recv_sem, device, here):
         self.here = here
@@ -235,8 +249,8 @@
 
 
 def enc1_kernel(
-    image, w_a, b_a, w_b, b_b, s1_out, p1_out,
-    halves, planes, w_stem, staged, x_a, y_rest, w_main, w_rest, pool_buf, stage, stage_p, w_sem, send_sem, recv_sem,
+    image_hbm, w_a_hbm, b_a_hbm, w_b, b_b_hbm, s1_out, p1_out,
+    image, w_a, b_a, b_b, halves, planes, w_stem, staged, x_a, y_rest, w_main, w_rest, pool_buf, stage, stage_p, w_sem, small_sem, send_sem, recv_sem,
 ):
     step = pl.program_id(0)
     strip = strip_index()
@@ -245,12 +259,15 @@
     def _():
         row = lax.axis_index("row")
         col = lax.axis_index("col")
+        barrier = enter_barrier()
+        small = fetch((image_hbm, w_a_hbm, b_a_hbm, b_b_hbm), (image, w_a, b_a, b_b), small_sem)
         copy_w = pltpu.make_async_copy(w_b, staged, w_sem)
         copy_w.start()
-        barrier = enter_barrier()
         stage[...] = jnp.zeros_like(stage)
         stage_p[...] = jnp.zeros_like(stage_p)
 
+        for copy in small:
+            copy.wait()
         for di in range(KERNEL):
             taps = []
             for dj in range(KERNEL):
@@ -320,14 +337,14 @@
     base = pl.multiple_of(step * N1536, N512)
 
     def rest(j):
-        y_rest[TILE * j : TILE * j + TILE, :] = dot(x_a[pl.ds(base + TILE * j, TILE), 0:PACK], w_rest[...])
+        y_rest[TILE * j : TILE * j + TILE, :] = dot(packed_rows(x_a, base + TILE * j, TILE), w_rest[...])
 
     rest(0)
     for j in range(SIX):
         rest(j + 1)
-        acc = dot(x_a[pl.ds(base + TILE * j, TILE), 0:PACK], w_main[0:PACK, :])
-        acc = acc + dot(x_a[pl.ds(base + TILE * j + LANES, TILE), 0:PACK], w_main[PACK:N2048, :])
-        acc = acc + dot(x_a[pl.ds(base + TILE * j + TILE, TILE), 0:PACK], w_main[N2048:N3072, :])
+        acc = dot(packed_rows(x_a, base + TILE * j, TILE), w_main[0:PACK, :])
+        acc = acc + dot(packed_rows(x_a, base + TILE * j + LANES, TILE), w_main[PACK:N2048, :])
+        acc = acc + dot(packed_rows(x_a, base + TILE * j + TILE, TILE), w_main[N2048:N3072, :])
         first_row = STRIP_ROWS * strip - 2 + N12 * step + 2 * j
         main = valid_rows(jnp.maximum(acc + bias_row(b_b, 0, TILE), 0.0), first_row, LANES)
         tail = jnp.maximum(rest_sum(y_rest, TILE * j, TILE) + bias_rest(b_b), 0.0)
@@ -338,9 +355,10 @@
 
 
 def mid_kernel(
-    p1_hbm, w_2a, w_2b, w_ma, w_mb, w_u2, w_d2a, w_d2b, b_2a, b_2b, b_ma, b_mb, b_d2a, b_d2b, out,
+    p1_hbm, w_2a, w_2b, w_ma, w_mb, w_u2, w_d2a, w_d2b, b_2a_h, b_2b_h, b_ma_h, b_mb_h, b_d2a_h, b_d2b_h, out,
+    b_2a, b_2b, b_ma, b_mb, b_d2a, b_d2b,
     p1, first_w, ring, x_a, x_s, x_u, m_1, m_2, m_o, d_2, acc_ref, wide, pool_buf,
-    sem_2a, sem_2b, sem_ma, sem_mb, sem_u2, sem_d2a, sem_d2b, sem_p1, sem_out, send_sem, recv_sem,
+    sem_2a, sem_2b, sem_ma, sem_mb, sem_u2, sem_d2a, sem_d2b, sem_p1, sem_out, small_sem, send_sem, recv_sem,
 ):
     strip = strip_index()
     prev_dev = strip_device((strip + LAST_STRIP) % STRIPS)
@@ -424,18 +442,21 @@
     copies_d2a = tap_copies(w_d2a, DEEP, 0, sem_d2a)
     copies_d2b = tap_copies(w_d2b, MIDDLE, N6400, sem_d2b)
 
-    copy_p1 = pltpu.make_async_copy(p1_hbm, p1, sem_p1)
-    copy_p1.start()
-    start(copies_2a)
-
+    copy_p1 = pltpu.make_async_copy(p1_hbm, p1.at[:, pl.ds(0, N1152), :], sem_p1)
     barrier = pltpu.get_barrier_semaphore()
     for device in (prev_dev, next_dev):
         pl.semaphore_signal(barrier, inc=1, device_id=device, device_id_type=MESH)
+    copy_p1.start()
+    start(copies_2a)
+    small = fetch(
+        (b_2a_h, b_2b_h, b_ma_h, b_mb_h, b_d2a_h, b_d2b_h), (b_2a, b_2b, b_ma, b_mb, b_d2a, b_d2b), small_sem
+    )
     pl.semaphore_wait(barrier, 2)
 
     for di in range(KERNEL):
         first_w[PACK * di + PACK_USED : PACK * di + PACK, :] = jnp.zeros((REST, MIDDLE), BF16)
     copy_p1.wait()
+    finish(small)
     finish(copies_2a)
     start(copies_2b)
     start(copies_ma)
@@ -457,10 +478,10 @@
         for block in (i, KERNEL - i):
             row0 = pl.multiple_of(block * TILE, TILE)
             for lane0, lanes in tiles:
-                acc = dot(p1[pl.ds(row0, TILE), 0:PACK], first_w[0:PACK, pl.ds(lane0, lanes)])
+                acc = dot(packed_rows(p1, row0, TILE), first_w[0:PACK, pl.ds(lane0, lanes)])
                 for di in (1, 2):
                     acc = acc + dot(
-                        p1[pl.ds(row0 + REST * di, TILE), 0:PACK],
+                        packed_rows(p1, row0 + REST * di, TILE),
                         first_w[PACK * di : PACK * di + PACK, pl.ds(lane0, lanes)],
                     )
                 value = jnp.maximum(acc + bias_row(b_2a, lane0, lanes), 0.0)
@@ -665,9 +686,9 @@
 
 
 def dec1_kernel(
-    d_2, s1, w_u1, w_d1a, w_d1b, b_d1a, b_d1b, w_head, b_head, out,
-    x_u, x_s, x_d, y_rest, st_u, st_a, st_b, wu_main, wu_rest, wa_main, wa_rest, wb_main, wb_rest, wide, result, pending, stage, skip, low, late,
-    sem, send_sem, recv_sem,
+    d_2, s1, w_u1, w_d1a, w_d1b, b_d1a_h, b_d1b_h, w_head_h, b_head_h, out,
+    b_d1a, b_d1b, w_head, b_head, x_u, x_s, x_d, y_rest, st_u, st_a, st_b, wu_main, wu_rest, wa_main, wa_rest, wb_main, wb_rest, wide, result, pending, stage, skip, low, late,
+    sem, small_sem, send_sem, recv_sem,
 ):
     strip = strip_index()
     row = lax.axis_index("row")
@@ -677,9 +698,10 @@
     copy_s = pltpu.make_async_copy(s1, skip, sem.at[2])
     copy_b = pltpu.make_async_copy(w_d1b, st_b, sem.at[KERNEL])
     copy_d = pltpu.make_async_copy(d_2, low, sem.at[IN_CH])
+    barrier = enter_barrier()
     copy_u.start()
     copy_d.start()
-    barrier = enter_barrier()
+    small = fetch((b_d1a_h, b_d1b_h, w_head_h, b_head_h), (b_d1a, b_d1b, w_head, b_head), small_sem)
 
     stage[...] = jnp.zeros_like(stage)
     copy_u.wait()
@@ -690,6 +712,8 @@
         wu_main[MIDDLE * tap : MIDDLE * tap + MIDDLE, :] = st_u[BASE * tap : BASE * tap + TILE, :].T
     wu_rest[...] = jnp.concatenate([st_u[BASE * tap + TILE : BASE * tap + BASE, :] for tap in range(IN_CH)], axis=0).T
     copy_d.wait()
+    for copy in small:
+        copy.wait()
 
     def up1(i, carry):
         row0 = pl.multiple_of(i * BASE_PAD, LANES)
@@ -716,11 +740,11 @@
 
     @pl.when(strip == 0)
     def _():
-        x_u[0:TILE, :] = jnp.zeros((TILE, N1152), BF16)
+        x_u[:, 0:TILE, :] = jnp.zeros((STRIPS, TILE, LANES), BF16)
 
     @pl.when(strip == LAST_STRIP)
     def _():
-        x_u[N4352:N4608, :] = jnp.zeros((TILE, N1152), BF16)
+        x_u[:, N4352:N4608, :] = jnp.zeros((STRIPS, TILE, LANES), BF16)
 
     copy_a.wait()
     turn_rest(st_a, wa_main, wa_rest)
@@ -738,8 +762,8 @@
         spread(0)
         for j in range(SIX):
             rows = pl.ds(base + TILE * j, TILE)
-            y_rest[rows, :] = dot(x_u[rows, 0:PACK], wa_rest[0:PACK, :]) + dot(
-                x_s[rows, 0:PACK], wa_rest[PACK:N2048, :]
+            y_rest[rows, :] = dot(packed_rows(x_u, base + TILE * j, TILE), wa_rest[0:PACK, :]) + dot(
+                packed_rows(x_s, base + TILE * j, TILE), wa_rest[PACK:N2048, :]
             )
             if j < FIVE:
                 spread(j + 1)
@@ -752,10 +776,9 @@
     def conv_a(row0):
         acc = None
         for di in range(KERNEL):
-            rows = pl.ds(row0 + LANES * di, TILE)
             for src, ref in enumerate((x_u, x_s)):
                 base = N3072 * src + PACK * di
-                part = dot(ref[rows, 0:PACK], wa_main[base : base + PACK, :])
+                part = dot(packed_rows(ref, row0 + LANES * di, TILE), wa_main[base : base + PACK, :])
                 acc = part if acc is None else acc + part
         return acc
 
@@ -800,15 +823,15 @@
         base = pl.multiple_of(i * PACK, PACK)
 
         def rest(j):
-            y_rest[TILE * j : TILE * j + TILE, :] = dot(x_d[pl.ds(base + TILE * j, TILE), 0:PACK], wb_rest[...])
+            y_rest[TILE * j : TILE * j + TILE, :] = dot(packed_rows(x_d, base + TILE * j, TILE), wb_rest[...])
 
         rest(0)
         waiting = pending[...]
         for j in range(IN_CH):
             rest(j + 1)
-            acc = dot(x_d[pl.ds(base + TILE * j, TILE), 0:PACK], wb_main[0:PACK, :])
-            acc = acc + dot(x_d[pl.ds(base + TILE * j + LANES, TILE), 0:PACK], wb_main[PACK:N2048, :])
-            acc = acc + dot(x_d[pl.ds(base + TILE * j + TILE, TILE), 0:PACK], wb_main[N2048:N3072, :])
+            acc = dot(packed_rows(x_d, base + TILE * j, TILE), wb_main[0:PACK, :])
+            acc = acc + dot(packed_rows(x_d, base + TILE * j + LANES, TILE), wb_main[PACK:N2048, :])
+            acc = acc + dot(packed_rows(x_d, base + TILE * j + TILE, TILE), wb_main[N2048:N3072, :])
             head(waiting, jnp.maximum(STRIPS * i + 2 * j - 2, 0))
             main = jnp.maximum(acc + bias_row(b_d1b, 0, TILE), 0.0).astype(BF16)
             tail = jnp.maximum(rest_sum(y_rest, TILE * j, TILE) + bias_rest(b_d1b), 0.0).astype(BF16)
@@ -859,28 +882,31 @@
         def flat(weight):
             return weight.reshape(-1, weight.shape[-1])
 
-        vmem = pl.BlockSpec(memory_space=pltpu.VMEM)
         hbm = pl.BlockSpec(memory_space=pl.ANY)
         dma = pltpu.SemaphoreType.DMA
         s1, p1 = pl.pallas_call(
             enc1_kernel,
             grid=(KERNEL,),
-            out_shape=(jax.ShapeDtypeStruct((N4608, BASE_PAD), BF16), jax.ShapeDtypeStruct((N1152, N1152), BF16)),
-            in_specs=[vmem, vmem, vmem, hbm, vmem],
-            out_specs=(pl.BlockSpec((N1536, BASE_PAD), lambda i: (i, 0)), pl.BlockSpec((BASE_PAD, N1152), lambda i: (i, 0))),
+            out_shape=(jax.ShapeDtypeStruct((N4608, BASE_PAD), BF16), jax.ShapeDtypeStruct((STRIPS, N1152, LANES), BF16)),
+            in_specs=[hbm] * FIVE,
+            out_specs=(pl.BlockSpec((N1536, BASE_PAD), lambda i: (i, 0)), pl.BlockSpec((STRIPS, BASE_PAD, LANES), lambda i: (0, i, 0))),
             scratch_shapes=[
+                pltpu.VMEM((REST, IN_CH, REST), BF16),
+                pltpu.VMEM((KERNEL, KERNEL, IN_CH, BASE), BF16),
+                pltpu.VMEM((BASE,), F32),
+                pltpu.VMEM((BASE,), F32),
                 pltpu.VMEM((2, N40, IN_CH, REST), BF16),
                 pltpu.VMEM((N42, STRIP_ROWS, LANES), BF16),
                 pltpu.VMEM((N96, BASE_PAD), BF16),
                 pltpu.VMEM((N2880, BASE), BF16),
-                pltpu.VMEM((N5120, N1152), BF16),
+                pltpu.VMEM((STRIPS, N5136, LANES), BF16),
                 pltpu.VMEM((N1792, TILE), F32),
                 pltpu.VMEM((N3072, TILE), BF16),
                 pltpu.VMEM((PACK, TILE), BF16),
                 pltpu.VMEM((2, LANES, LANES), F32),
                 pltpu.VMEM((2, KERNEL, N288, LANES), F32),
                 pltpu.VMEM((2, KERNEL, N80, LANES), F32),
-                dma, dma((IN_CH,)), dma((2, 2)),
+                dma, dma((IN_CH,)), dma((IN_CH,)), dma((2, 2)),
             ],
             compiler_params=pltpu.CompilerParams(
                 vmem_limit_bytes=VMEM_LIMIT, collective_id=1, has_side_effects=True, dimension_semantics=("arbitrary",)
@@ -891,10 +917,11 @@
         d2 = pl.pallas_call(
             mid_kernel,
             out_shape=jax.ShapeDtypeStruct((N1152, MIDDLE), BF16),
-            in_specs=[hbm] * STRIPS + [vmem] * SIX,
+            in_specs=[hbm] * N14,
             out_specs=hbm,
             scratch_shapes=[
-                pltpu.VMEM((N1152, N1152), BF16),
+                *[pltpu.VMEM((size,), F32) for size in (MIDDLE, MIDDLE, DEEP, DEEP, MIDDLE, MIDDLE)],
+                pltpu.VMEM((STRIPS, N1168, LANES), BF16),
                 pltpu.VMEM((N3072, MIDDLE), BF16),
                 pltpu.VMEM((RING_ROWS, DEEP), BF16),
                 pltpu.VMEM((N1152, MIDDLE3), BF16),
@@ -907,7 +934,7 @@
                 pltpu.VMEM((TILE, DEEP), F32),
                 pltpu.VMEM((FIVE, N512, LANES), F32),
                 pltpu.VMEM((LANES, LANES), F32),
-                dma((N18,)), dma((TAPS,)), dma((KERNEL,)), dma((TAPS,)), dma((IN_CH,)), dma((TAPS,)), dma((TAPS,)), dma, dma,
+                dma((N18,)), dma((TAPS,)), dma((KERNEL,)), dma((TAPS,)), dma((IN_CH,)), dma((TAPS,)), dma((TAPS,)), dma, dma, dma((SIX,)),
                 dma((LAST_STRIP, 2)), dma((LAST_STRIP, 2)),
             ],
             compiler_params=pltpu.CompilerParams(
@@ -925,12 +952,16 @@
         y = pl.pallas_call(
             dec1_kernel,
             out_shape=jax.ShapeDtypeStruct((REST, IN_CH, REST), F32),
-            in_specs=[hbm] * FIVE + [vmem] * KERNEL + [pl.BlockSpec(memory_space=pltpu.SMEM)],
+            in_specs=[hbm] * TAPS,
             out_specs=hbm,
             scratch_shapes=[
-                pltpu.VMEM((N4608, N1152), BF16),
-                pltpu.VMEM((N4608, N1152), BF16),
-                pltpu.VMEM((N4352, N1152), BF16),
+                pltpu.VMEM((BASE,), F32),
+                pltpu.VMEM((BASE,), F32),
+                pltpu.VMEM((IN_CH, BASE), BF16),
+                pltpu.SMEM((IN_CH,), F32),
+                pltpu.VMEM((STRIPS, N4624, LANES), BF16),
+                pltpu.VMEM((STRIPS, N4624, LANES), BF16),
+                pltpu.VMEM((STRIPS, N4368, LANES), BF16),
                 pltpu.VMEM((N4608, TILE), F32),
                 pltpu.VMEM((DEEP, MIDDLE), BF16),
                 pltpu.VMEM((N2880, MIDDLE), BF16),
@@ -948,7 +979,7 @@
                 pltpu.VMEM((N4608, BASE_PAD), BF16),
                 pltpu.VMEM((N1152, MIDDLE), BF16),
                 pltpu.VMEM((TILE, TILE), F32),
-                dma((FIVE,)), dma((2, 2)), dma((2, 2)),
+                dma((FIVE,)), dma((IN_CH,)), dma((2, 2)), dma((2, 2)),
             ],
             compiler_params=pltpu.CompilerParams(vmem_limit_bytes=VMEM_LIMIT, collective_id=2, has_side_effects=True),
             name="dec1",

time: 142 us -> 139 us (0.979)
  Pallas kernels: 140 us -> 137 us
    pallas_call x1, Pallas kernels: 26.2 us -> 24.3 us  [body(): pl.pallas_call(enc1_kernel, grid=(KERNEL,), out_shape=(jax.ShapeDtypeStru...]
where the time goes in v7:
time: 139 us
  Pallas kernels  137 us (99%)
  local copies, waits for them, and re-layouts  1.57 us (1%)
    pallas_call x1, Pallas kernels, body(): pl.pallas_call(mid_kernel, out_shape=jax.ShapeDtypeStruct((N1152, MIDDLE)...  69.5 us
    pallas_call x1, Pallas kernels, body(): pl.pallas_call(dec1_kernel, out_shape=jax.ShapeDtypeStruct((REST, IN_CH,...  43.6 us
    pallas_call x1, Pallas kernels, body(): pl.pallas_call(enc1_kernel, grid=(KERNEL,), out_shape=(jax.ShapeDtypeStru...  24.3 us

profile of v7, /device:TPU:0, one launch (start us, length us, event | category | flops | bytes accessed | tf_op | source)
XLA Modules:
  0.0 138.9 jit_solution(18202155310237792145)
XLA Ops:
  0.0 24.3 %enc1.1 = (bf16[4608,384]{1,0:T(8,128)(2,1)}, bf16[8,1152,128]{2,1,0:T(8,128)(2,1)}) custom-call(bf16[64,4,64]{2,1,0:T(4,128)(2,1)} %bitcast.30, bf16[3,3,4,320]{3,2,1,0:T(4,128)(2,1)} %w_a_hbm.1, f32[320]{0:T(512)} %b_a_hbm.1, bf16[2880,320]{1,0:T(8,128)(2,1)} %bitcast.26, f32[320]{0:T(512)} %b_b_hbm.1), custom_call_target="tpu_custom_call" | custom-call | tf_op jit(solution)/shard_map/enc1/pallas_call | solution.py:887
  24.3 69.5 %mid.1.d_2 = bf16[1152,640]{1,0:T(8,128)(2,1)} custom-call(bf16[8,1152,128]{2,1,0:T(8,128)(2,1)} %get-tuple-element.7.p1_hbm, bf16[2880,640]{1,0:T(8,128)(2,1)} %bitcast.24, bf16[5760,640]{1,0:T(8,128)(2,1)} %bitcast.21, bf16[5760,1280]{1,0:T(8,128)(2,1)} %bitcast.19, bf16[11520,1280]{1,0:T(8,128)(2,1)} %bitcast.18, bf16[5120,640]{1,0:T(8,128)(2,1)} %bitcast.23, ...), custom_call_target="tpu_custom_call" | custom-call | tf_op jit(solution)/shard_map/mid/pallas_call | solution.py:917
  93.8 43.6 %dec1.1 = f32[64,4,64]{2,1,0:T(4,128)} custom-call(bf16[1152,640]{1,0:T(8,128)(2,1)} %mid.1.d_2, bf16[4608,384]{1,0:T(8,128)(2,1)} %get-tuple-element.8.s1, bf16[1280,640]{1,0:T(8,128)(2,1)} %bitcast.28, bf16[2880,640]{1,0:T(8,128)(2,1)} %bitcast.25, bf16[2880,320]{1,0:T(8,128)(2,1)} %bitcast.27, f32[320]{0:T(512)} %b_d1a_h.1, f32[320]{0:T(512)} %b_d1b_h.1, ...), custom_call_target="tpu_custom_call" | custom-call | tf_op jit(solution)/shard_map/dec1/pallas_call | solution.py:952
  137.4 1.6 %copy.27 = f32[64,64,4]{1,2,0:T(4,128)} copy(f32[64,64,4]{1,2,0:T(4,128)} %bitcast.29) | data formatting | bytes 131072

commit v8 on v7

--- a/solution.py
+++ b/solution.py
@@ -15,8 +15,8 @@
 STRIPS = 8
 TAPS = 9
 N10 = 10
+N11 = 11
 N12 = 12
-N14 = 14
 N16 = 16
 N18 = 18
 N22 = 22
@@ -165,15 +165,12 @@
         main_ref[pl.ds(pl.multiple_of(base + REST_AT + REST * dj, REST), REST), :] = turned[BASE * src + TILE : BASE * src + BASE]
 
 
-def turn_rest(staged, main_ref, rest_ref):
-    for dj in range(KERNEL):
-        parts = [staged[pl.ds(PACK_USED * di + BASE * dj + TILE, REST), :] for di in range(KERNEL)] + [jnp.zeros((REST, MIDDLE), BF16)]
-        turned = jnp.concatenate(parts, axis=0).T
-        for src in range(2):
-            rest_ref[pl.ds(PACK * src + TILE * dj, TILE), :] = turned[BASE * src : BASE * src + TILE]
-            rest_ref[pl.ds(PACK * src + REST_AT + REST * dj, REST), :] = turned[BASE * src + TILE : BASE * src + BASE]
-    clear_pad(main_ref, SIX)
-    clear_pad(rest_ref, 2)
+def turn_rest(staged, rest_ref, dj):
+    parts = [staged[pl.ds(pl.multiple_of(PACK_USED * di + BASE * dj + TILE, REST), REST), :] for di in range(KERNEL)]
+    turned = jnp.concatenate(parts + [jnp.zeros((REST, MIDDLE), BF16)], axis=0).T
+    for src in range(2):
+        rest_ref[pl.ds(pl.multiple_of(PACK * src + TILE * dj, REST), TILE), :] = turned[BASE * src : BASE * src + TILE]
+        rest_ref[pl.ds(pl.multiple_of(PACK * src + REST_AT + REST * dj, REST), REST), :] = turned[BASE * src + TILE : BASE * src + BASE]
 
 
 def bias_row(ref, start, size):
@@ -355,10 +352,11 @@
 
 
 def mid_kernel(
-    p1_hbm, w_2a, w_2b, w_ma, w_mb, w_u2, w_d2a, w_d2b, b_2a_h, b_2b_h, b_ma_h, b_mb_h, b_d2a_h, b_d2b_h, out,
-    b_2a, b_2b, b_ma, b_mb, b_d2a, b_d2b,
+    p1_hbm, w_2a, w_2b, w_ma, w_mb, w_u2, w_d2a, w_d2b, w_u1, w_d1a, b_2a_h, b_2b_h, b_ma_h, b_mb_h, b_d2a_h, b_d2b_h,
+    out, um_out, ur_out, am_out, ar_out,
+    b_2a, b_2b, b_ma, b_mb, b_d2a, b_d2b, wu_main, wu_rest, wa_main, wa_rest,
     p1, first_w, ring, x_a, x_s, x_u, m_1, m_2, m_o, d_2, acc_ref, wide, pool_buf,
-    sem_2a, sem_2b, sem_ma, sem_mb, sem_u2, sem_d2a, sem_d2b, sem_p1, sem_out, small_sem, send_sem, recv_sem,
+    sem_2a, sem_2b, sem_ma, sem_mb, sem_u2, sem_d2a, sem_d2b, sem_p1, sem_out, turn_sem, small_sem, send_sem, recv_sem,
 ):
     strip = strip_index()
     prev_dev = strip_device((strip + LAST_STRIP) % STRIPS)
@@ -439,6 +437,11 @@
         )
         for tap in range(IN_CH)
     ]
+    st_u = ring.at[pl.ds(N10240, DEEP), pl.ds(0, MIDDLE)]
+    copies_turn = [
+        pltpu.make_async_copy(w_u1, st_u, turn_sem.at[0]),
+        pltpu.make_async_copy(w_d1a, first_w.at[pl.ds(0, N2880), :], turn_sem.at[1]),
+    ]
     copies_d2a = tap_copies(w_d2a, DEEP, 0, sem_d2a)
     copies_d2b = tap_copies(w_d2b, MIDDLE, N6400, sem_d2b)
 
@@ -494,18 +497,15 @@
     start(copies_u2[0:2])
 
     def conv640(src, row0, base, lane0, lanes):
-        acc = None
-        for di in range(KERNEL):
-            weights = jnp.concatenate(
-                [
-                    ring[base + MIDDLE * (t // 2) : base + MIDDLE * (t // 2) + MIDDLE, pl.ds(MIDDLE * (t % 2) + lane0, lanes)]
-                    for t in range(KERNEL * di, KERNEL * di + KERNEL)
-                ],
-                axis=0,
-            )
-            part = dot(src[pl.ds(row0 + REST * di, TILE), :], weights)
-            acc = part if acc is None else acc + part
-        return acc
+        weights = jnp.concatenate(
+            [
+                ring[base + MIDDLE * (t // 2) : base + MIDDLE * (t // 2) + MIDDLE, pl.ds(MIDDLE * (t % 2) + lane0, lanes)]
+                for t in range(TAPS)
+            ],
+            axis=0,
+        )
+        rows = jnp.concatenate([src[pl.ds(row0 + REST * di, TILE), :] for di in range(KERNEL)], axis=1)
+        return dot(rows, weights)
 
     def enc2b(i, carry):
         block = i + 1 - 2 * (i % 2)
@@ -617,6 +617,9 @@
                 for lane in range(0, lanes, LANES):
                     wide[(lane0 + lane) // LANES, pl.ds(q, TILE, stride=2), :] = part[:, lane : lane + LANES]
 
+        if p == 0:
+            start(copies_turn)
+
         def place(i, carry):
             src = pl.multiple_of(REST * i, REST)
             dst = pl.multiple_of(REST * (1 + 2 * i + p), REST)
@@ -630,6 +633,9 @@
     finish(ex_s)
     halo(x_s, REST, MIDDLE, N16)
     finish(copies_d2a)
+    finish(copies_turn)
+    clear_pad(wa_main, SIX)
+    clear_pad(wa_rest, 2)
 
     def dec2a(i, carry):
         block = i + 1 - 2 * (i % 2)
@@ -655,9 +661,21 @@
                 acc = part if acc is None else acc + part
             value = jnp.maximum(acc + bias_row(b_d2a, lane0, lanes), 0.0)
             put3(x_a, row0 + REST, lane0, MIDDLE, value, REST)
+
+        part = jnp.minimum(i, 2)
+        for dj in range(KERNEL):
+            turn_main(first_w, wa_main, part, dj)
+        turn_rest(first_w, wa_rest, part)
+        wu_main[pl.ds(pl.multiple_of(MIDDLE * i, REST), MIDDLE), :] = st_u[pl.ds(pl.multiple_of(BASE * i, REST), TILE), :].T
+        wu_rest[...] = jnp.concatenate([st_u[BASE * tap + TILE : BASE * tap + BASE, :] for tap in range(IN_CH)], axis=0).T
         return carry
 
     lax.fori_loop(0, IN_CH, dec2a, 0)
+    turned = [
+        pltpu.make_async_copy(src, dst, turn_sem.at[2 + index])
+        for index, (src, dst) in enumerate(((wu_main, um_out), (wu_rest, ur_out), (wa_main, am_out), (wa_rest, ar_out)))
+    ]
+    start(turned)
     finish(copies_d2b)
 
     def dec2b(i, carry):
@@ -681,36 +699,39 @@
     lax.fori_loop(0, IN_CH, dec2b, 0)
     result = pltpu.make_async_copy(d_2.at[pl.ds(REST, PACK), :], out.at[pl.ds(REST, PACK), :], sem_out)
     result.start()
+    finish(turned)
     finish(ex_d)
     result.wait()
 
 
 def dec1_kernel(
-    d_2, s1, w_u1, w_d1a, w_d1b, b_d1a_h, b_d1b_h, w_head_h, b_head_h, out,
-    b_d1a, b_d1b, w_head, b_head, x_u, x_s, x_d, y_rest, st_u, st_a, st_b, wu_main, wu_rest, wa_main, wa_rest, wb_main, wb_rest, wide, result, pending, stage, skip, low, late,
+    d_2, s1, um_h, ur_h, am_h, ar_h, w_d1b, b_d1a_h, b_d1b_h, w_head_h, b_head_h, out,
+    b_d1a, b_d1b, w_head, b_head, x_u, x_s, x_d, y_rest, st_b, wu_main, wu_rest, wa_main, wa_rest, wb_main, wb_rest, wide, result, pending, stage, skip, low, late,
     sem, small_sem, send_sem, recv_sem,
 ):
     strip = strip_index()
     row = lax.axis_index("row")
     col = lax.axis_index("col")
-    copy_u = pltpu.make_async_copy(w_u1, st_u, sem.at[0])
-    copy_a = pltpu.make_async_copy(w_d1a, st_a, sem.at[1])
+    copy_um = pltpu.make_async_copy(um_h, wu_main, sem.at[0])
+    copy_ur = pltpu.make_async_copy(ur_h, wu_rest, sem.at[1])
+    copy_am = pltpu.make_async_copy(am_h, wa_main, sem.at[FIVE])
+    copy_ar = pltpu.make_async_copy(ar_h, wa_rest, sem.at[SIX])
     copy_s = pltpu.make_async_copy(s1, skip, sem.at[2])
     copy_b = pltpu.make_async_copy(w_d1b, st_b, sem.at[KERNEL])
     copy_d = pltpu.make_async_copy(d_2, low, sem.at[IN_CH])
     barrier = enter_barrier()
-    copy_u.start()
+    copy_um.start()
+    copy_ur.start()
     copy_d.start()
     small = fetch((b_d1a_h, b_d1b_h, w_head_h, b_head_h), (b_d1a, b_d1b, w_head, b_head), small_sem)
 
     stage[...] = jnp.zeros_like(stage)
-    copy_u.wait()
-    copy_a.start()
+    copy_um.wait()
+    copy_ur.wait()
     copy_s.start()
+    copy_ar.start()
+    copy_am.start()
     copy_b.start()
-    for tap in range(IN_CH):
-        wu_main[MIDDLE * tap : MIDDLE * tap + MIDDLE, :] = st_u[BASE * tap : BASE * tap + TILE, :].T
-    wu_rest[...] = jnp.concatenate([st_u[BASE * tap + TILE : BASE * tap + BASE, :] for tap in range(IN_CH)], axis=0).T
     copy_d.wait()
     for copy in small:
         copy.wait()
@@ -746,9 +767,8 @@
     def _():
         x_u[:, N4352:N4608, :] = jnp.zeros((STRIPS, TILE, LANES), BF16)
 
-    copy_a.wait()
-    turn_rest(st_a, wa_main, wa_rest)
     copy_s.wait()
+    copy_ar.wait()
 
     def rest_a(i, carry):
         base = pl.multiple_of(i * N1536, N512)
@@ -767,11 +787,10 @@
             )
             if j < FIVE:
                 spread(j + 1)
-            if j < KERNEL:
-                turn_main(st_a, wa_main, i, j)
         return carry
 
     lax.fori_loop(0, KERNEL, rest_a, 0)
+    copy_am.wait()
 
     def conv_a(row0):
         acc = None
@@ -914,13 +933,19 @@
             name="enc1",
         )(image_tile.transpose(0, 2, 1), w_enc1a, b_enc1a, flat(w_enc1b), b_enc1b)
 
-        d2 = pl.pallas_call(
+        turned_shapes = ((N2560, TILE), (MIDDLE, TILE), (N6144, TILE), (N2048, TILE))
+
+        def turned(weight):
+            return weight.transpose(0, 1, KERNEL, 2).reshape(-1, weight.shape[2])
+
+        d2, *level_one = pl.pallas_call(
             mid_kernel,
-            out_shape=jax.ShapeDtypeStruct((N1152, MIDDLE), BF16),
-            in_specs=[hbm] * N14,
-            out_specs=hbm,
+            out_shape=[jax.ShapeDtypeStruct(shape, BF16) for shape in ((N1152, MIDDLE),) + turned_shapes],
+            in_specs=[hbm] * N16,
+            out_specs=[hbm] * FIVE,
             scratch_shapes=[
                 *[pltpu.VMEM((size,), F32) for size in (MIDDLE, MIDDLE, DEEP, DEEP, MIDDLE, MIDDLE)],
+                *[pltpu.VMEM(shape, BF16) for shape in turned_shapes],
                 pltpu.VMEM((STRIPS, N1168, LANES), BF16),
                 pltpu.VMEM((N3072, MIDDLE), BF16),
                 pltpu.VMEM((RING_ROWS, DEEP), BF16),
@@ -934,7 +959,7 @@
                 pltpu.VMEM((TILE, DEEP), F32),
                 pltpu.VMEM((FIVE, N512, LANES), F32),
                 pltpu.VMEM((LANES, LANES), F32),
-                dma((N18,)), dma((TAPS,)), dma((KERNEL,)), dma((TAPS,)), dma((IN_CH,)), dma((TAPS,)), dma((TAPS,)), dma, dma, dma((SIX,)),
+                dma((N18,)), dma((TAPS,)), dma((KERNEL,)), dma((TAPS,)), dma((IN_CH,)), dma((TAPS,)), dma((TAPS,)), dma, dma, dma((SIX,)), dma((SIX,)),
                 dma((LAST_STRIP, 2)), dma((LAST_STRIP, 2)),
             ],
             compiler_params=pltpu.CompilerParams(
@@ -943,16 +968,14 @@
             name="mid",
         )(
             p1, flat(w_enc2a), flat(w_enc2b), flat(w_mid_a), flat(w_mid_b), flat(w_up2), flat(w_dec2a), flat(w_dec2b),
+            turned(w_up1), turned(w_dec1a),
             b_enc2a, b_enc2b, b_mid_a, b_mid_b, b_dec2a, b_dec2b,
         )
-
-        def turned(weight):
-            return weight.transpose(0, 1, KERNEL, 2).reshape(-1, weight.shape[2])
 
         y = pl.pallas_call(
             dec1_kernel,
             out_shape=jax.ShapeDtypeStruct((REST, IN_CH, REST), F32),
-            in_specs=[hbm] * TAPS,
+            in_specs=[hbm] * N11,
             out_specs=hbm,
             scratch_shapes=[
                 pltpu.VMEM((BASE,), F32),
@@ -963,8 +986,6 @@
                 pltpu.VMEM((STRIPS, N4624, LANES), BF16),
                 pltpu.VMEM((STRIPS, N4368, LANES), BF16),
                 pltpu.VMEM((N4608, TILE), F32),
-                pltpu.VMEM((DEEP, MIDDLE), BF16),
-                pltpu.VMEM((N2880, MIDDLE), BF16),
                 pltpu.VMEM((N2880, BASE), BF16),
                 pltpu.VMEM((N2560, TILE), BF16),
                 pltpu.VMEM((MIDDLE, TILE), BF16),
@@ -979,11 +1000,11 @@
                 pltpu.VMEM((N4608, BASE_PAD), BF16),
                 pltpu.VMEM((N1152, MIDDLE), BF16),
                 pltpu.VMEM((TILE, TILE), F32),
-                dma((FIVE,)), dma((IN_CH,)), dma((2, 2)), dma((2, 2)),
+                dma((LAST_STRIP,)), dma((IN_CH,)), dma((2, 2)), dma((2, 2)),
             ],
             compiler_params=pltpu.CompilerParams(vmem_limit_bytes=VMEM_LIMIT, collective_id=2, has_side_effects=True),
             name="dec1",
-        )(d2, s1, turned(w_up1), turned(w_dec1a), flat(w_dec1b), b_dec1a, b_dec1b, w_head.T, b_head)
+        )(d2, s1, *level_one, flat(w_dec1b), b_dec1a, b_dec1b, w_head.T, b_head)
         return y.transpose(0, 2, 1)
 
     def program(image, *params):

time: 139 us -> 139 us (level)
  no operation moved by 1% of the time
where the time goes in v8:
time: 139 us; the launch traced here: 138 us
  Pallas kernels  137 us (99%)
  local copies, waits for them, and re-layouts  1.57 us (1%)
    pallas_call x1, Pallas kernels, body(): pl.pallas_call(mid_kernel, out_shape=[jax.ShapeDtypeStruct(shape, BF16) f...  69.3 us
    pallas_call x1, Pallas kernels, body(): pl.pallas_call(dec1_kernel, out_shape=jax.ShapeDtypeStruct((REST, IN_CH,...  43.4 us
    pallas_call x1, Pallas kernels, body(): pl.pallas_call(enc1_kernel, grid=(KERNEL,), out_shape=(jax.ShapeDtypeStru...  24.3 us

profile of v8, /device:TPU:0, one launch (start us, length us, event | category | flops | bytes accessed | tf_op | source)
XLA Modules:
  0.0 138.5 jit_solution(13921616008576564580)
XLA Ops:
  0.0 24.3 %enc1.1 = (bf16[4608,384]{1,0:T(8,128)(2,1)}, bf16[8,1152,128]{2,1,0:T(8,128)(2,1)}) custom-call(bf16[64,4,64]{2,1,0:T(4,128)(2,1)} %bitcast.30, bf16[3,3,4,320]{3,2,1,0:T(4,128)(2,1)} %w_a_hbm.1, f32[320]{0:T(512)} %b_a_hbm.1, bf16[2880,320]{1,0:T(8,128)(2,1)} %bitcast.26, f32[320]{0:T(512)} %b_b_hbm.1), custom_call_target="tpu_custom_call" | custom-call | tf_op jit(solution)/shard_map/enc1/pallas_call | solution.py:906
  24.3 69.3 %mid.1 = (bf16[1152,640]{1,0:T(8,128)(2,1)}, bf16[2560,256]{1,0:T(8,128)(2,1)}, bf16[640,256]{1,0:T(8,128)(2,1)}, bf16[6144,256]{1,0:T(8,128)(2,1)}, bf16[2048,256]{1,0:T(8,128)(2,1)}) custom-call(bf16[8,1152,128]{2,1,0:T(8,128)(2,1)} %get-tuple-element.12.p1_hbm, bf16[2880,640]{1,0:T(8,128)(2,1)} %bitcast.24, bf16[5760,640]{1,0:T(8,128)(2,1)} %bitcast.21, ...), custom_call_target="tpu_custom_call" | custom-call | tf_op jit(solution)/shard_map/mid/pallas_call | solution.py:941
  93.6 43.4 %dec1.1 = f32[64,4,64]{2,1,0:T(4,128)} custom-call(bf16[1152,640]{1,0:T(8,128)(2,1)} %get-tuple-element.13.d_2, bf16[4608,384]{1,0:T(8,128)(2,1)} %get-tuple-element.14.s1, bf16[2560,256]{1,0:T(8,128)(2,1)} %get-tuple-element.15.um_h, bf16[640,256]{1,0:T(8,128)(2,1)} %get-tuple-element.16.ur_h, bf16[6144,256]{1,0:T(8,128)(2,1)} %get-tuple-element.17.am_h, ...), custom_call_target="tpu_custom_call" | custom-call | tf_op jit(solution)/shard_map/dec1/pallas_call | solution.py:975
  136.9 1.6 %copy.27 = f32[64,64,4]{1,2,0:T(4,128)} copy(f32[64,64,4]{1,2,0:T(4,128)} %bitcast.29) | data formatting | bytes 131072

commit v9 on v8

--- a/solution.py
+++ b/solution.py
@@ -18,6 +18,7 @@
 N11 = 11
 N12 = 12
 N16 = 16
+N17 = 17
 N18 = 18
 N22 = 22
 N28 = 28
@@ -28,6 +29,7 @@
 N36 = 36
 N40 = 40
 N42 = 42
+N50 = 50
 N60 = 60
 REST = 64
 N80 = 80
@@ -58,7 +60,6 @@
 N3200 = 3200
 N3840 = 3840
 N4096 = 4096
-N4352 = 4352
 N4368 = 4368
 N4608 = 4608
 N4624 = 4624
@@ -272,6 +273,7 @@
                 taps.append(jnp.concatenate([tap, jnp.zeros((STRIPS, REST), F32)], axis=1))
             taps.append(jnp.zeros((STRIPS, BASE_PAD), F32))
             w_stem[STRIP_ROWS * di : STRIP_ROWS * di + STRIP_ROWS, :] = jnp.concatenate(taps, axis=0).astype(BF16)
+
         planes[N40:N42, :, :] = jnp.zeros((2, STRIP_ROWS, LANES), BF16)
 
         pl.semaphore_wait(barrier, STRIPS)
@@ -736,13 +738,12 @@
     for copy in small:
         copy.wait()
 
-    def up1(i, carry):
-        row0 = pl.multiple_of(i * BASE_PAD, LANES)
-        lhs = low[pl.ds(row0, BASE_PAD), :]
+    def up1(i):
+        lhs = low[BASE_PAD * i : BASE_PAD * i + BASE_PAD, :]
         rest = dot(lhs, wu_rest[...])
         for p in range(2):
             part = rest[:, LANES * p : LANES * p + LANES]
-            buf = wide.at[p]
+            buf = wide.at[2 * i + p]
             buf[2, pl.ds(0, BASE_PAD, stride=2), :] = low_lanes(part)
             buf[2, pl.ds(1, BASE_PAD, stride=2), :] = low_lanes(pltpu.roll(part, REST, axis=1))
             for q in range(2):
@@ -752,44 +753,33 @@
                 buf[1, pl.ds(q, BASE_PAD, stride=2), :] = main[:, LANES:TILE]
             for r in range(SIX):
                 main = jnp.concatenate([buf[0, LANES * r : LANES * r + LANES, :], buf[1, LANES * r : LANES * r + LANES, :]], axis=1)
-                put3_320(
-                    x_u, pl.multiple_of((N12 * i + 2 * r + p) * LANES, LANES), main, buf[2, LANES * r : LANES * r + LANES, :], LANES
-                )
-        return carry
-
-    lax.fori_loop(0, KERNEL, up1, 0)
-
-    @pl.when(strip == 0)
-    def _():
-        x_u[:, 0:TILE, :] = jnp.zeros((STRIPS, TILE, LANES), BF16)
-
-    @pl.when(strip == LAST_STRIP)
-    def _():
-        x_u[:, N4352:N4608, :] = jnp.zeros((STRIPS, TILE, LANES), BF16)
-
+                tail = buf[2, LANES * r : LANES * r + LANES, :]
+                if (i, r) == (0, 0):
+                    main, tail = jnp.where(strip > 0, main, 0.0), jnp.where(strip > 0, tail, 0.0)
+                if (i, r) == (2, FIVE):
+                    main, tail = jnp.where(strip < LAST_STRIP, main, 0.0), jnp.where(strip < LAST_STRIP, tail, 0.0)
+                put3_320(x_u, (N12 * i + 2 * r + p) * LANES, main, tail, LANES)
+
+    def spread(j):
+        rows = pl.ds(TILE * j, TILE)
+        put3_320(x_s, TILE * j, skip[rows, 0:TILE].astype(F32), skip[rows, TILE:BASE_PAD].astype(F32), LANES, stage.at[j % 2])
+
+    def rest_a(i):
+        for j in range(SIX * i, SIX * i + SIX):
+            y_rest[TILE * j : TILE * j + TILE, :] = dot(packed_rows(x_u, TILE * j, TILE), wa_rest[0:PACK, :]) + dot(
+                packed_rows(x_s, TILE * j, TILE), wa_rest[PACK:N2048, :]
+            )
+            if j < N17:
+                spread(j + 1)
+
+    up1(0)
+    up1(1)
     copy_s.wait()
     copy_ar.wait()
-
-    def rest_a(i, carry):
-        base = pl.multiple_of(i * N1536, N512)
-
-        def spread(j):
-            rows = pl.ds(base + TILE * j, TILE)
-            put3_320(
-                x_s, base + TILE * j, skip[rows, 0:TILE].astype(F32), skip[rows, TILE:BASE_PAD].astype(F32), LANES, stage.at[j % 2]
-            )
-
-        spread(0)
-        for j in range(SIX):
-            rows = pl.ds(base + TILE * j, TILE)
-            y_rest[rows, :] = dot(packed_rows(x_u, base + TILE * j, TILE), wa_rest[0:PACK, :]) + dot(
-                packed_rows(x_s, base + TILE * j, TILE), wa_rest[PACK:N2048, :]
-            )
-            if j < FIVE:
-                spread(j + 1)
-        return carry
-
-    lax.fori_loop(0, KERNEL, rest_a, 0)
+    spread(0)
+    up1(2)
+    for i in range(KERNEL):
+        rest_a(i)
     copy_am.wait()
 
     def conv_a(row0):
@@ -819,12 +809,12 @@
                 put_a(acc, base + TILE * j, STRIP_ROWS * strip - 1 + STRIPS * i + 2 * j, j % 2)
         return carry
 
+    copy_b.wait()
     lax.fori_loop(0, IN_CH, dec1a, 0)
+    pack_weights(st_b, wb_main, wb_rest)
     put_a(late[...], N3840, STRIP_ROWS * strip + N29, 1)
     put_a(conv_a(N4096), N4096, STRIP_ROWS * strip + N31, 0)
 
-    copy_b.wait()
-    pack_weights(st_b, wb_main, wb_rest)
     head_bias = jnp.zeros((IN_CH, LANES), F32)
     for channel in range(IN_CH):
         head_bias = jnp.where(lax.broadcasted_iota(jnp.int32, (IN_CH, LANES), 0) == channel, b_head[channel], head_bias)
@@ -838,8 +828,28 @@
             result[0, row0 + r] = part[:, 0:REST]
             result[1, row0 + r] = part[:, REST:LANES]
 
+    pushes = []
+    for part, first, rows in ((0, 0, N22), (1, N22, N10)):
+        for side in range(2):
+            pushes.append(
+                Push(
+                    result.at[side, pl.ds(first, rows)],
+                    out.at[pl.ds(STRIP_ROWS * (strip % 2) + first, rows)],
+                    send_sem.at[part, side],
+                    recv_sem.at[part, strip % 2],
+                    (lax.axis_index("data"), side, strip // 2),
+                    (strip // 2 == row) & (col == side),
+                )
+            )
+
     def dec1b(i, carry):
         base = pl.multiple_of(i * PACK, PACK)
+
+        @pl.when(i == KERNEL)
+        def _():
+            pl.semaphore_wait(barrier, STRIPS)
+            for push in pushes[0:2]:
+                push.start()
 
         def rest(j):
             y_rest[TILE * j : TILE * j + TILE, :] = dot(packed_rows(x_d, base + TILE * j, TILE), wb_rest[...])
@@ -858,25 +868,7 @@
         pending[...] = waiting
         return carry
 
-    pushes = []
-    for part, first, rows in ((0, 0, N22), (1, N22, N10)):
-        for side in range(2):
-            pushes.append(
-                Push(
-                    result.at[side, pl.ds(first, rows)],
-                    out.at[pl.ds(STRIP_ROWS * (strip % 2) + first, rows)],
-                    send_sem.at[part, side],
-                    recv_sem.at[part, strip % 2],
-                    (lax.axis_index("data"), side, strip // 2),
-                    (strip // 2 == row) & (col == side),
-                )
-            )
-
-    lax.fori_loop(0, KERNEL, dec1b, 0)
-    pl.semaphore_wait(barrier, STRIPS)
-    for push in pushes[0:2]:
-        push.start()
-    lax.fori_loop(KERNEL, IN_CH, dec1b, 0)
+    lax.fori_loop(0, IN_CH, dec1b, 0)
     head(pending[...], N30)
 
     for push in pushes[2:IN_CH]:
@@ -915,7 +907,7 @@
                 pltpu.VMEM((BASE,), F32),
                 pltpu.VMEM((BASE,), F32),
                 pltpu.VMEM((2, N40, IN_CH, REST), BF16),
-                pltpu.VMEM((N42, STRIP_ROWS, LANES), BF16),
+                pltpu.VMEM((N50, STRIP_ROWS, LANES), BF16),
                 pltpu.VMEM((N96, BASE_PAD), BF16),
                 pltpu.VMEM((N2880, BASE), BF16),
                 pltpu.VMEM((STRIPS, N5136, LANES), BF16),
@@ -993,7 +985,7 @@
                 pltpu.VMEM((N2048, TILE), BF16),
                 pltpu.VMEM((N3072, TILE), BF16),
                 pltpu.VMEM((PACK, TILE), BF16),
-                pltpu.VMEM((2, KERNEL, REST_AT, LANES), F32),
+                pltpu.VMEM((SIX, KERNEL, REST_AT, LANES), F32),
                 pltpu.VMEM((2, STRIP_ROWS, IN_CH, REST), F32),
                 pltpu.VMEM((TILE, BASE), BF16),
                 pltpu.VMEM((2, KERNEL, N288, LANES), F32),

time: 139 us -> 136 us (0.978)
  Pallas kernels: 137 us -> 134 us
    pallas_call x1, Pallas kernels: 43.4 us -> 40.6 us  [body(): pl.pallas_call(dec1_kernel, out_shape=jax.ShapeDtypeStruct((REST, IN_CH,...]
where the time goes in v9:
time: 136 us
  Pallas kernels  134 us (99%)
  local copies, waits for them, and re-layouts  1.57 us (1%)
    pallas_call x1, Pallas kernels, body(): pl.pallas_call(mid_kernel, out_shape=[jax.ShapeDtypeStruct(shape, BF16) f...  69.5 us
    pallas_call x1, Pallas kernels, body(): pl.pallas_call(dec1_kernel, out_shape=jax.ShapeDtypeStruct((REST, IN_CH,...  40.6 us
    pallas_call x1, Pallas kernels, body(): pl.pallas_call(enc1_kernel, grid=(KERNEL,), out_shape=(jax.ShapeDtypeStru...  24.3 us

profile of v9, /device:TPU:0, one launch (start us, length us, event | category | flops | bytes accessed | tf_op | source)
XLA Modules:
  0.0 136.0 jit_solution(14812373769927865957)
XLA Ops:
  0.0 24.3 %enc1.1 = (bf16[4608,384]{1,0:T(8,128)(2,1)}, bf16[8,1152,128]{2,1,0:T(8,128)(2,1)}) custom-call(bf16[64,4,64]{2,1,0:T(4,128)(2,1)} %bitcast.30, bf16[3,3,4,320]{3,2,1,0:T(4,128)(2,1)} %w_a_hbm.1, f32[320]{0:T(512)} %b_a_hbm.1, bf16[2880,320]{1,0:T(8,128)(2,1)} %bitcast.26, f32[320]{0:T(512)} %b_b_hbm.1), custom_call_target="tpu_custom_call" | custom-call | tf_op jit(solution)/shard_map/enc1/pallas_call | solution.py:898
  24.3 69.5 %mid.1 = (bf16[1152,640]{1,0:T(8,128)(2,1)}, bf16[2560,256]{1,0:T(8,128)(2,1)}, bf16[640,256]{1,0:T(8,128)(2,1)}, bf16[6144,256]{1,0:T(8,128)(2,1)}, bf16[2048,256]{1,0:T(8,128)(2,1)}) custom-call(bf16[8,1152,128]{2,1,0:T(8,128)(2,1)} %get-tuple-element.12.p1_hbm, bf16[2880,640]{1,0:T(8,128)(2,1)} %bitcast.24, bf16[5760,640]{1,0:T(8,128)(2,1)} %bitcast.21, ...), custom_call_target="tpu_custom_call" | custom-call | tf_op jit(solution)/shard_map/mid/pallas_call | solution.py:933
  93.8 40.6 %dec1.1 = f32[64,4,64]{2,1,0:T(4,128)} custom-call(bf16[1152,640]{1,0:T(8,128)(2,1)} %get-tuple-element.13.d_2, bf16[4608,384]{1,0:T(8,128)(2,1)} %get-tuple-element.14.s1, bf16[2560,256]{1,0:T(8,128)(2,1)} %get-tuple-element.15.um_h, bf16[640,256]{1,0:T(8,128)(2,1)} %get-tuple-element.16.ur_h, bf16[6144,256]{1,0:T(8,128)(2,1)} %get-tuple-element.17.am_h, ...), custom_call_target="tpu_custom_call" | custom-call | tf_op jit(solution)/shard_map/dec1/pallas_call | solution.py:967
  134.4 1.6 %copy.27 = f32[64,64,4]{1,2,0:T(4,128)} copy(f32[64,64,4]{1,2,0:T(4,128)} %bitcast.29) | data formatting | bytes 131072

commit v10 on v9

--- a/solution.py
+++ b/solution.py
@@ -20,6 +20,7 @@
 N16 = 16
 N17 = 17
 N18 = 18
+N20 = 20
 N22 = 22
 N28 = 28
 N29 = 29
@@ -305,8 +306,8 @@
                 ).wait_recv()
 
         def expand(i, carry):
-            for j in range(STRIPS):
-                r = STRIPS * i + j
+            for j in range(N20):
+                r = N20 * i + j
                 both = jnp.concatenate([halves[0, r].astype(F32), halves[1, r].astype(F32)], axis=1)
                 image_row = STRIP_ROWS * strip - IN_CH + r
                 both = jnp.where((image_row >= 0) & (image_row < TILE), both, 0.0)
@@ -317,7 +318,7 @@
                 planes[r] = jnp.concatenate([before, both, after, jnp.zeros((STRIPS, LANES), F32)], axis=0).astype(BF16)
             return carry
 
-        lax.fori_loop(0, FIVE, expand, 0)
+        lax.fori_loop(0, 2, expand, 0)
 
         def stem(i, carry):
             for j in range(STRIPS):

time: 136 us -> 136 us (level)
  no operation moved by 1% of the time
where the time goes in v10:
time: 136 us
  Pallas kernels  134 us (99%)
  local copies, waits for them, and re-layouts  1.57 us (1%)
    pallas_call x1, Pallas kernels, body(): pl.pallas_call(mid_kernel, out_shape=[jax.ShapeDtypeStruct(shape, BF16) f...  69.5 us
    pallas_call x1, Pallas kernels, body(): pl.pallas_call(dec1_kernel, out_shape=jax.ShapeDtypeStruct((REST, IN_CH,...  40.6 us
    pallas_call x1, Pallas kernels, body(): pl.pallas_call(enc1_kernel, grid=(KERNEL,), out_shape=(jax.ShapeDtypeStru...  23.9 us

profile of v10, /device:TPU:0, one launch (start us, length us, event | category | flops | bytes accessed | tf_op | source)
XLA Modules:
  0.0 135.6 jit_solution(11678286192589764026)
XLA Ops:
  0.0 23.9 %enc1.1 = (bf16[4608,384]{1,0:T(8,128)(2,1)}, bf16[8,1152,128]{2,1,0:T(8,128)(2,1)}) custom-call(bf16[64,4,64]{2,1,0:T(4,128)(2,1)} %bitcast.30, bf16[3,3,4,320]{3,2,1,0:T(4,128)(2,1)} %w_a_hbm.1, f32[320]{0:T(512)} %b_a_hbm.1, bf16[2880,320]{1,0:T(8,128)(2,1)} %bitcast.26, f32[320]{0:T(512)} %b_b_hbm.1), custom_call_target="tpu_custom_call" | custom-call | tf_op jit(solution)/shard_map/enc1/pallas_call | solution.py:899
  23.9 69.5 %mid.1 = (bf16[1152,640]{1,0:T(8,128)(2,1)}, bf16[2560,256]{1,0:T(8,128)(2,1)}, bf16[640,256]{1,0:T(8,128)(2,1)}, bf16[6144,256]{1,0:T(8,128)(2,1)}, bf16[2048,256]{1,0:T(8,128)(2,1)}) custom-call(bf16[8,1152,128]{2,1,0:T(8,128)(2,1)} %get-tuple-element.12.p1_hbm, bf16[2880,640]{1,0:T(8,128)(2,1)} %bitcast.24, bf16[5760,640]{1,0:T(8,128)(2,1)} %bitcast.21, ...), custom_call_target="tpu_custom_call" | custom-call | tf_op jit(solution)/shard_map/mid/pallas_call | solution.py:934
  93.4 40.6 %dec1.1 = f32[64,4,64]{2,1,0:T(4,128)} custom-call(bf16[1152,640]{1,0:T(8,128)(2,1)} %get-tuple-element.13.d_2, bf16[4608,384]{1,0:T(8,128)(2,1)} %get-tuple-element.14.s1, bf16[2560,256]{1,0:T(8,128)(2,1)} %get-tuple-element.15.um_h, bf16[640,256]{1,0:T(8,128)(2,1)} %get-tuple-element.16.ur_h, bf16[6144,256]{1,0:T(8,128)(2,1)} %get-tuple-element.17.am_h, ...), custom_call_target="tpu_custom_call" | custom-call | tf_op jit(solution)/shard_map/dec1/pallas_call | solution.py:968
  134.0 1.6 %copy.27 = f32[64,64,4]{1,2,0:T(4,128)} copy(f32[64,64,4]{1,2,0:T(4,128)} %bitcast.29) | data formatting | bytes 131072

commit v11 on v10

--- a/solution.py
+++ b/solution.py
@@ -733,8 +733,6 @@
     copy_ur.wait()
     copy_s.start()
     copy_ar.start()
-    copy_am.start()
-    copy_b.start()
     copy_d.wait()
     for copy in small:
         copy.wait()
@@ -777,6 +775,8 @@
     up1(1)
     copy_s.wait()
     copy_ar.wait()
+    copy_am.start()
+    copy_b.start()
     spread(0)
     up1(2)
     for i in range(KERNEL):

time: 136 us -> 136 us (level)
  no operation moved by 1% of the time
where the time goes in v11:
time: 136 us
  Pallas kernels  134 us (99%)
  local copies, waits for them, and re-layouts  1.57 us (1%)
    pallas_call x1, Pallas kernels, body(): pl.pallas_call(mid_kernel, out_shape=[jax.ShapeDtypeStruct(shape, BF16) f...  69.5 us
    pallas_call x1, Pallas kernels, body(): pl.pallas_call(dec1_kernel, out_shape=jax.ShapeDtypeStruct((REST, IN_CH,...  40.6 us
    pallas_call x1, Pallas kernels, body(): pl.pallas_call(enc1_kernel, grid=(KERNEL,), out_shape=(jax.ShapeDtypeStru...  23.9 us

profile of v11, /device:TPU:0, one launch (start us, length us, event | category | flops | bytes accessed | tf_op | source)
XLA Modules:
  0.0 135.6 jit_solution(239536642502678075)
XLA Ops:
  0.0 23.9 %enc1.1 = (bf16[4608,384]{1,0:T(8,128)(2,1)}, bf16[8,1152,128]{2,1,0:T(8,128)(2,1)}) custom-call(bf16[64,4,64]{2,1,0:T(4,128)(2,1)} %bitcast.30, bf16[3,3,4,320]{3,2,1,0:T(4,128)(2,1)} %w_a_hbm.1, f32[320]{0:T(512)} %b_a_hbm.1, bf16[2880,320]{1,0:T(8,128)(2,1)} %bitcast.26, f32[320]{0:T(512)} %b_b_hbm.1), custom_call_target="tpu_custom_call" | custom-call | tf_op jit(solution)/shard_map/enc1/pallas_call | solution.py:899
  23.9 69.5 %mid.1 = (bf16[1152,640]{1,0:T(8,128)(2,1)}, bf16[2560,256]{1,0:T(8,128)(2,1)}, bf16[640,256]{1,0:T(8,128)(2,1)}, bf16[6144,256]{1,0:T(8,128)(2,1)}, bf16[2048,256]{1,0:T(8,128)(2,1)}) custom-call(bf16[8,1152,128]{2,1,0:T(8,128)(2,1)} %get-tuple-element.12.p1_hbm, bf16[2880,640]{1,0:T(8,128)(2,1)} %bitcast.24, bf16[5760,640]{1,0:T(8,128)(2,1)} %bitcast.21, ...), custom_call_target="tpu_custom_call" | custom-call | tf_op jit(solution)/shard_map/mid/pallas_call | solution.py:934
  93.4 40.6 %dec1.1 = f32[64,4,64]{2,1,0:T(4,128)} custom-call(bf16[1152,640]{1,0:T(8,128)(2,1)} %get-tuple-element.13.d_2, bf16[4608,384]{1,0:T(8,128)(2,1)} %get-tuple-element.14.s1, bf16[2560,256]{1,0:T(8,128)(2,1)} %get-tuple-element.15.um_h, bf16[640,256]{1,0:T(8,128)(2,1)} %get-tuple-element.16.ur_h, bf16[6144,256]{1,0:T(8,128)(2,1)} %get-tuple-element.17.am_h, ...), custom_call_target="tpu_custom_call" | custom-call | tf_op jit(solution)/shard_map/dec1/pallas_call | solution.py:968
  134.0 1.6 %copy.27 = f32[64,64,4]{1,2,0:T(4,128)} copy(f32[64,64,4]{1,2,0:T(4,128)} %bitcast.29) | data formatting | bytes 131072
